TPU v7x, 256 devices: a 8x8x2 block of a 8x8x16 slice. The times are simulated.
256 devices in a mesh: region: 2 (over z), member: 16 (over y, core), space: 8 (over x).
Axes of the slice: x: 8, y: 8, z: 2, core: 2. Of those that a mesh axis runs over, the one named last changes fastest.
The devices are a block of a 8x8x16 slice.
Arguments:
- prior_trials: bfloat16 [80, 12288, 256], P('member', ('region', 'space')), parts along dimension 1, may hold values from -6 to 6
- prior_at_sensors: bfloat16 [80, 12288], P('member', ('region', 'space')), parts along dimension 1, may hold values from -6 to 6
- sensor_readings: bfloat16 [12288], P(('region', 'space')), parts along dimension 0, may hold values from -8 to 8
- sensor_noise_spread: bfloat16 [12288], P(('region', 'space')), parts along dimension 0, may hold values from 1 to 10
- nearby_readings: int32 [12288, 128], P(('region', 'space')), parts along dimension 0, may hold values from 0 to 1407, as said below
- subarea_cutoff_level: int32 [12288], P(('region', 'space')), parts along dimension 0, may hold values from 0 to 3
Outputs:
- analysis: bfloat16 [80, 12288, 256], P('member', ('region', 'space')), parts along dimension 1
There are 2 independent parts, one for each index of `region`. A program takes and returns all parts, laid end to end along the dimension named above; each array names one. Nothing has to cross between parts.
Inputs may be any that keep to these rules, and one draw needn't show every extreme that they name: `nearby_readings`: row c lists 128 distinct observations whose region-wide index o lies within (subarea_cutoff_level[c] + 2) * 64 of c and inside the region.
All inputs are finite; a program needn't handle non-finite values. Where the computation divides by a largest or mean magnitude, that divisor is 1e-20 or more.
Results may differ from a plain program's by a relative error of at most 0.0053.
Values may be sent and summed in bfloat16 or wider, within the bound.
No kernel may reach another device: no remote copies, remote signals or barrier semaphores. Data moves between devices by JAX's collectives and lax.ppermute only.
A program may use at most 64 MiB of HBM per device.

v0:
```python
import jax
import jax.numpy as jnp
from jax import lax
from jax.experimental import pallas as pl
from jax.experimental.pallas import tpu as pltpu
from jax.sharding import Mesh
from jax.sharding import PartitionSpec as P

NS_STEPS = 4
MEMBER = ("member_0", "member_1")
LANES = 128
SUB = 8


def spread_copies(value, axis):
    copies = jnp.broadcast_to(value, (lax.axis_size(axis), *value.shape))
    return lax.all_to_all(copies, axis, split_axis=0, concat_axis=0, tiled=True)


def with_halo(value, axis, width):
    count, length = lax.axis_size(axis), value.shape[1]
    up = [(i, i + 1) for i in range(count - 1)]
    down = [(j, i) for i, j in up]
    before = lax.ppermute(value[:, length - width :], axis, up)
    after = lax.ppermute(value[:, :width], axis, down)
    return jnp.concatenate([before, value, after], axis=1)


def lookup(table_rows, low, high):
    tiles = 6
    found = jnp.take_along_axis(table_rows(0), low, axis=1, mode="promise_in_bounds")
    for t in range(1, tiles):
        value = jnp.take_along_axis(table_rows(t), low, axis=1, mode="promise_in_bounds")
        found = jnp.where(high == t, value, found)
    return found


def make_table_kernel(members, halo):
    def kernel(first_ref, window_ref, lists_ref, tiers_ref, anom_ref, innov_ref, weight_ref, sums_ref, table, flat):
        tiles = window_ref.shape[0]
        for t in range(tiles):
            raw = window_ref[t].astype(jnp.float32)
            observ = raw[:members]
            mean = jnp.sum(observ, axis=0, keepdims=True) * (1.0 / members)
            anomaly = observ - mean
            innov = raw[members : members + 1] - mean
            noise = raw[members + 1 : members + 2]
            table[t, :members] = anomaly
            table[t, members : members + 1] = innov
            table[t, members + 1 : members + 2] = noise
            energy = jnp.sum(anomaly * anomaly, axis=0, keepdims=True)
            flat[t, 0:SUB] = jnp.broadcast_to(innov * innov / noise, (SUB, LANES))
            flat[t, SUB : 2 * SUB] = jnp.broadcast_to(energy / noise, (SUB, LANES))

        columns = lists_ref.shape[0]

        def decay_of(index, start, tiers):
            column = start + lax.broadcasted_iota(jnp.int32, (SUB, LANES), 0)
            radius = (tiers.astype(jnp.float32) + 2.0) * (0.5 * LANES)
            distance = jnp.abs(index - halo - column).astype(jnp.float32) / radius
            return jnp.exp(-2.0 * distance * distance)

        def block_sum(i, carry):
            fit, spread = carry
            start = pl.multiple_of(i * SUB, SUB)
            index = lists_ref[pl.ds(start, SUB), :]
            first_tile = start // LANES
            local = index - first_tile * LANES
            low, high = local & (LANES - 1), local >> 7
            decay = decay_of(index, start, tiers_ref[pl.ds(start, SUB), :])
            fits = lookup(lambda t: flat[first_tile + t, 0:SUB], low, high)
            spreads = lookup(lambda t: flat[first_tile + t, SUB : 2 * SUB], low, high)
            return fit + decay * fits, spread + decay * spreads

        zero = jnp.zeros((SUB, LANES), jnp.float32)
        fit, spread = lax.fori_loop(0, columns // SUB, block_sum, (zero, zero))
        sums_ref[0:1, :] = jnp.broadcast_to(jnp.sum(fit), (1, LANES))
        sums_ref[1:2, :] = jnp.broadcast_to(jnp.sum(spread), (1, LANES))

        first = first_ref[0]
        own = innov_ref.shape[0]
        groups = members // SUB

        def own_block(b, unused):
            start = pl.multiple_of(first + b * SUB, SUB)
            indices = lists_ref[pl.ds(start, SUB), :]
            decay = decay_of(indices, start, tiers_ref[pl.ds(start, SUB), :])
            innovs, noises = [], []
            for s in range(SUB):
                column = start + s
                first_tile = column // LANES
                local = jnp.broadcast_to(indices[s : s + 1], (SUB, LANES)) - first_tile * LANES
                low, high = local & (LANES - 1), local >> 7
                for g in range(groups):
                    anom_ref[b * SUB + s, g * SUB : (g + 1) * SUB] = lookup(
                        lambda t: table[first_tile + t, g * SUB : (g + 1) * SUB], low, high
                    )
                tail = lookup(lambda t: table[first_tile + t, members : members + SUB], low, high)
                innovs.append(tail[0:1])
                noises.append(tail[1:2])
            rows = pl.ds(pl.multiple_of(b * SUB, SUB), SUB)
            innov_ref[rows, :] = jnp.concatenate(innovs, axis=0)
            weight_ref[rows, :] = decay / jnp.concatenate(noises, axis=0)
            return unused

        lax.fori_loop(0, own // SUB, own_block, 0)

    return kernel


def select_domains(window, first, lists, tiers, members, own, halo):
    obs = lists.shape[1]
    tiles = window.shape[0]
    f32 = jnp.float32
    return pl.pallas_call(
        make_table_kernel(members, halo),
        in_specs=[
            pl.BlockSpec(memory_space=pltpu.SMEM),
            pl.BlockSpec(memory_space=pltpu.VMEM),
            pl.BlockSpec(memory_space=pltpu.VMEM),
            pl.BlockSpec(memory_space=pltpu.VMEM),
        ],
        out_specs=[pl.BlockSpec(memory_space=pltpu.VMEM)] * 4,
        out_shape=[
            jax.ShapeDtypeStruct((own, members, obs), f32),
            jax.ShapeDtypeStruct((own, obs), f32),
            jax.ShapeDtypeStruct((own, obs), f32),
            jax.ShapeDtypeStruct((2, LANES), f32),
        ],
        scratch_shapes=[
            pltpu.VMEM((tiles, members + SUB, LANES), f32),
            pltpu.VMEM((tiles, 2 * SUB, LANES), f32),
        ],
        name="select_domains",
    )(first, window, lists, tiers)


def transform(anomaly, innovation, weight, inflation, sweeps):
    exact = lax.Precision.HIGH
    trial_lines = anomaly.shape[1]
    weighted = anomaly * weight[:, None]
    gram = jnp.einsum("nak,nbk->nab", weighted, anomaly, precision=exact)
    identity = jnp.eye(trial_lines, dtype=jnp.float32)[None]
    matrix = gram + (trial_lines - 1.0) / inflation * identity
    row_bound = jnp.max(jnp.sum(jnp.abs(matrix), axis=2), axis=1)[:, None, None]
    root_iter = matrix / row_bound
    inverse = jnp.broadcast_to(identity, matrix.shape)
    for repeat in range(sweeps):
        if repeat == 0:
            factor = 1.5 * identity - 0.5 * root_iter
        else:
            factor = 1.5 * identity - 0.5 * jnp.einsum("nab,nbc->nac", inverse, root_iter, precision=exact)
        if repeat < sweeps - 1:
            root_iter = jnp.einsum("nab,nbc->nac", root_iter, factor, precision=exact)
        inverse = factor if repeat == 0 else jnp.einsum("nab,nbc->nac", factor, inverse, precision=exact)
    inv_root = inverse / jnp.sqrt(row_bound)
    target = jnp.sum(weighted * innovation[:, None], axis=2)
    half_gain = jnp.einsum("nab,nb->na", inv_root, target, precision=exact)
    mean_gain = jnp.einsum("nab,nb->na", inv_root, half_gain, precision=exact)
    weights_full = jnp.sqrt(trial_lines - 1.0) * inv_root + mean_gain[:, :, None]
    centred = weights_full - jnp.mean(weights_full, axis=1, keepdims=True) + 1.0 / trial_lines
    return centred.astype(jnp.bfloat16)


def per_device(
    prior_trials,
    prior_at_sensors,
    sensor_readings,
    sensor_noise_spread,
    nearby_readings,
    subarea_cutoff_level,
):
    held, patch_cells, quantities = prior_trials.shape
    obs_count = nearby_readings.shape[1]
    halo_cells = 5 * obs_count // 2
    groups = lax.axis_size(MEMBER)
    members = held * groups
    domains = patch_cells // groups

    gathered = spread_copies(prior_at_sensors, MEMBER).reshape(members, patch_cells)
    outgoing = prior_trials.reshape(held, groups, domains, quantities).transpose(1, 0, 2, 3)
    outgoing, gathered = lax.optimization_barrier((outgoing, gathered))
    incoming = lax.all_to_all(outgoing, MEMBER, split_axis=0, concat_axis=0, tiled=True)
    incoming = incoming.reshape(members, domains, quantities)

    obs_rows = jnp.stack([sensor_readings, sensor_noise_spread], axis=0)
    window = with_halo(jnp.concatenate([gathered, obs_rows], axis=0), "space", halo_cells)
    tiles = patch_cells // LANES + 6
    window = jnp.pad(window, ((0, SUB - 2), (0, tiles * LANES - window.shape[1])))
    window = window.reshape(members + SUB, tiles, LANES).transpose(1, 0, 2)

    first = (lax.axis_index(MEMBER) * domains).astype(jnp.int32).reshape(1)
    anomaly, innovation, weight, sums = select_domains(
        window, first, nearby_readings, subarea_cutoff_level[:, None], members, domains, halo_cells
    )
    total = jnp.sum(spread_copies(sums, "space").reshape(-1, 2, LANES)[:, :, 0], axis=0)
    inflation = total[0] / (total[1] / (members - 1.0))
    trans_w = transform(anomaly, innovation, weight, inflation, NS_STEPS)

    updated = jnp.einsum(
        "inc,nij->jnc", incoming, trans_w, preferred_element_type=jnp.float32
    ).astype(jnp.bfloat16)
    returned = lax.all_to_all(
        updated.reshape(groups, held, domains, quantities), MEMBER, split_axis=0, concat_axis=0, tiled=True
    )
    return returned.transpose(1, 0, 2, 3).reshape(held, patch_cells, quantities)


def solution(mesh):
    finer = Mesh(
        mesh.devices.reshape(mesh.shape["region"], 8, 2, mesh.shape["space"]),
        ("region", "member_0", "member_1", "space"),
    )
    return jax.shard_map(
        per_device,
        mesh=finer,
        in_specs=(
            P(MEMBER, ("region", "space"), None),
            P(MEMBER, ("region", "space")),
            P(("region", "space")),
            P(("region", "space")),
            P(("region", "space"), None),
            P(("region", "space")),
        ),
        out_specs=P(MEMBER, ("region", "space"), None),
        check_vma=False,
    )
```

profile of v0, /device:TPU:513, one launch (start us, length us, event | category | flops | bytes accessed | tf_op | source)
XLA Modules:
  0.0 184.0 jit_solution(6318290104155774771)
XLA Ops:
  1.4 23.7 %all-to-all-start = ((bf16[16,5,768]{2,1,0:T(8,128)(2,1)}), bf16[16,5,768]{2,1,0:T(8,128)(2,1)S(1)}, u32[]{:S(2)}, u32[]{:S(2)}) async-start(bf16[16,5,768]{2,1,0:T(8,128)(2,1)} %broadcast_in_dim.6), calls=%async_computation | async-start | bytes 393216 | tf_op jit(solution)/shard_map/all_to_all | solution.py:17
  26.5 9.3 %all-to-all-done = bf16[16,5,768]{2,1,0:T(8,128)(2,1)S(1)} async-done(((bf16[16,5,768]{2,1,0:T(8,128)(2,1)}), bf16[16,5,768]{2,1,0:T(8,128)(2,1)S(1)}, u32[]{:S(2)}, u32[]{:S(2)}) %all-to-all-start) | async-done | bytes 122912 | tf_op jit(solution)/shard_map/all_to_all | solution.py:17
  37.3 4.0 %collective-permute-start = (bf16[82,320]{1,0:T(8,128)(2,1)S(1)}, bf16[82,320]{1,0:T(8,128)(2,1)S(1)}, u32[]{:S(2)}, u32[]{:S(2)}) collective-permute-start(bf16[82,320]{1,0:T(8,128)(2,1)S(1)} %get-tuple-element.18), channel_id=1, source_target_pairs={{0,1},{1,2},{2,3},{3,4},{4,5},{5,6},{6,7},{8,9},{9,10},{10,11},{11... | collective-permute-start | bytes 157448 | tf_op jit(solution)/shard_map/ppermute | solution.py:24
  41.3 1.6 broadcast_in_dim.18.tiers_ref
  43.0 2.9 %copy.108 = bf16[16,5,48,256]{3,2,1,0:T(8,128)(2,1)} copy(bf16[16,5,48,256]{3,2,0,1:T(8,128)(2,1)} %bitcast.47) | data formatting | bytes 3932160 | tf_op jit(solution)/shard_map/optimization_barrier | solution.py:182
  46.9 16.0 %select_domains.1 = (f32[48,80,128]{2,1,0:T(8,128)}, f32[48,128]{1,0:T(8,128)}, f32[48,128]{1,0:T(8,128)}, f32[2,128]{1,0:T(2,128)}) custom-call(s32[1]{0:T(128)} %bitcast.first_ref, bf16[12,88,128]{2,1,0:T(8,128)(2,1)} %bitcast_bitcast_fusion.window_ref, s32[768,128]{1,0:T(8,128)} %lists_ref.1, s32[768,1]{1,0:T(8,128)} %broadcast_in_dim.18.tiers_ref), custom_call_target="tpu_custom_call" | custom-call | tf_op jit(solution)/shard_map/select_domains/pallas_call | solution.py:115
  64.2 3.5 %all-to-all-start.1 = ((f32[8,2,128]{2,1,0:T(2,128)}), f32[8,2,128]{2,1,0:T(2,128)S(1)}, u32[]{:S(2)}, u32[]{:S(2)}) async-start(f32[8,2,128]{2,1,0:T(2,128)} %broadcast_in_dim.8), calls=%async_computation.1 | async-start | bytes 16384 | tf_op jit(solution)/shard_map/all_to_all | solution.py:17
  67.7 2.5 %fusion.2 = f32[48,80]{1,0:T(8,128)S(1)} fusion(f32[48,80,128]{2,1,0:T(8,128)} %get-tuple-element.12, f32[48,128]{1,0:T(8,128)} %get-tuple-element.15, f32[48,128]{1,0:T(8,128)} %get-tuple-element.13), kind=kLoop, calls=%fused_computation.3 | loop fusion | flops 1470720 | bytes 2030592 | tf_op jit(solution)/shard_map/reduce_sum | solution.py:157
  70.2 3.9 %all-to-all-done.1 = f32[8,2,128]{2,1,0:T(2,128)S(1)} async-done(((f32[8,2,128]{2,1,0:T(2,128)}), f32[8,2,128]{2,1,0:T(2,128)S(1)}, u32[]{:S(2)}, u32[]{:S(2)}) %all-to-all-start.1) | async-done | bytes 8224 | tf_op jit(solution)/shard_map/all_to_all | solution.py:17
  74.1 5.4 %all-to-all-start.2 = ((bf16[16,5,48,256]{3,2,1,0:T(8,128)(2,1)}), bf16[16,5,48,256]{3,2,1,0:T(8,128)(2,1)}, u32[]{:S(2)}, u32[]{:S(2)}) async-start(bf16[16,5,48,256]{3,2,1,0:T(8,128)(2,1)} %copy.108), calls=%async_computation.2 | async-start | bytes 3932160 | tf_op jit(solution)/shard_map/all_to_all | solution.py:183
  81.5 3.0 %abs_reduce_fusion = (f32[48,80]{1,0:T(8,128)S(1)}, f32[48,80,80]{1,2,0:T(8,128)}) fusion(f32[80,80]{0,1:T(8,128)S(1)} %fusion.36, f32[48,80,128]{2,1,0:T(8,128)S(1)} %copy-done, f32[48,128]{1,0:T(8,128)S(1)} %copy-done.2), kind=kOutput, calls=%fused_computation.18 | convolution fusion | flops 237338880 | bytes 3260416 | tf_op jit(solution)/shard_map/nak,nbk->nab/dot_general | solution.py:142
  84.6 4.2 %fusion.10 = f32[48,80,80]{2,1,0:T(8,128)S(1)} fusion(f32[80,80]{0,1:T(8,128)S(1)} %fusion.37, f32[48,80,80]{1,2,0:T(8,128)} %get-tuple-element.22, f32[48]{0:T(128)S(1)} %reduce_max.9, f32[80,80]{0,1:T(8,128)S(1)} %fusion.36), kind=kOutput, calls=%fused_computation.17 | convolution fusion | flops 149299200 | bytes 2508992 | tf_op jit(solution)/shard_map/nab,nbc->nac/dot_general | solution.py:154
  88.8 1.9 %multiply_subtract_fusion.1 = f32[48,80,80]{1,2,0:T(8,128)S(1)} fusion(f32[48,80,80]{2,1,0:T(8,128)S(1)} %fusion.10, f32[80,80]{0,1:T(8,128)S(1)} %fusion.37, f32[48,80,80]{1,2,0:T(8,128)S(1)} %copy-done.1, f32[48]{0:T(128)S(1)} %reduce_max.9, f32[80,80]{0,1:T(8,128)S(1)} %fusion.36), kind=kOutput, calls=%fused_computation.13 | convolution fusion | flops 149299200 | bytes 3737792 | tf_op jit(solution)/shard_map/nab,nbc->nac/dot_general | solution.py:152
  90.7 1.7 fusion.48
  92.4 1.9 %fusion.8 = f32[48,80,80]{2,1,0:T(8,128)S(1)} fusion(f32[48,80,80]{1,2,0:T(8,128)S(1)} %multiply_subtract_fusion.1, f32[80,80]{0,1:T(8,128)S(1)} %fusion.37, f32[48,80,80]{1,2,0:T(8,128)S(1)} %copy-done.1, f32[48]{0:T(128)S(1)} %reduce_max.9, f32[80,80]{0,1:T(8,128)S(1)} %fusion.36), kind=kOutput, calls=%fused_computation.15 | convolution fusion | flops 148684800 | bytes 3737792 | tf_op jit(solution)/shard_map/nab,nbc->nac/dot_general | solution.py:155
  94.3 1.7 fusion.49
  96.0 2.0 %fusion.14 = f32[48,80,80]{2,1,0:T(8,128)S(1)} fusion(f32[48,80,80]{2,1,0:T(8,128)S(1)} %fusion.8, f32[48,80,80]{1,2,0:T(8,128)S(1)} %fusion.49, f32[80,80]{0,1:T(8,128)S(1)} %fusion.37), kind=kOutput, calls=%fused_computation.21 | convolution fusion | flops 148070400 | bytes 3712000 | tf_op jit(solution)/shard_map/nab,nbc->nac/dot_general | solution.py:155
  98.0 1.7 fusion.13
  99.8 1.7 fusion.50
  101.5 2.0 %fusion.16 = f32[48,80,80]{2,1,0:T(8,128)S(1)} fusion(f32[48,80,80]{2,1,0:T(8,128)S(1)} %fusion.14, f32[48,80,80]{1,2,0:T(8,128)S(1)} %fusion.50, f32[48]{0:T(128)S(1)} %sqrt.8, f32[80,80]{0,1:T(8,128)S(1)} %fusion.37), kind=kOutput, calls=%fused_computation.23 | convolution fusion | flops 148377600 | bytes 3712192 | tf_op jit(solution)/shard_map/nab,nbc->nac/dot_general | solution.py:155
  105.1 1.6 fusion.51
  107.4 18.8 %all-to-all-done.2 = bf16[16,5,48,256]{3,2,1,0:T(8,128)(2,1)} async-done(((bf16[16,5,48,256]{3,2,1,0:T(8,128)(2,1)}), bf16[16,5,48,256]{3,2,1,0:T(8,128)(2,1)}, u32[]{:S(2)}, u32[]{:S(2)}) %all-to-all-start.2) | async-done | bytes 1966112 | tf_op jit(solution)/shard_map/all_to_all | solution.py:183
  126.2 3.1 %convert_bitcast_fusion = bf16[80,48,256]{2,0,1:T(8,128)(2,1)S(1)} fusion(bf16[80,48,256]{2,1,0:T(8,128)(2,1)} %bitcast.13, f32[48,80,80]{2,1,0:T(8,128)S(1)} %fusion.16, f32[48,80]{1,0:T(8,128)S(1)} %broadcast_multiply_fusion, f32[48,80]{1,0:T(8,128)S(1)} %bitcast.49), kind=kOutput, calls=%fused_computation.6 | convolution fusion | flops 159805440 | bytes 5191680 | tf_op jit(solution)/shard_map/inc,nij->jnc/dot_general | solution.py:200
  130.0 52.6 %all_to_all.20 = bf16[16,5,48,256]{3,2,1,0:T(8,128)(2,1)S(1)} all-to-all(bf16[16,5,48,256]{3,2,1,0:T(8,128)(2,1)S(1)} %bitcast.45), channel_id=1, replica_groups=mesh['region'=2,'member_0'=8,'member_1'=2,'space'=8] {'member_0','member..., dimensions={0} | all-to-all | bytes 3932160 | tf_op jit(solution)/shard_map/all_to_all | solution.py:203
  (29 shorter events, 11.7 us)
Async XLA Ops:
  1.4 34.4 %all-to-all-start = ((bf16[16,5,768]{2,1,0:T(8,128)(2,1)}), bf16[16,5,768]{2,1,0:T(8,128)(2,1)S(1)}, u32[]{:S(2)}, u32[]{:S(2)}) async-start(bf16[16,5,768]{2,1,0:T(8,128)(2,1)} %broadcast_in_dim.6), calls=%async_computation | async-start | bytes 393216 | tf_op jit(solution)/shard_map/all_to_all | solution.py:17
  36.0 10.0 %collective-permute-start.1 = (bf16[82,320]{1,0:T(8,128)(2,1)S(1)}, bf16[82,320]{1,0:T(8,128)(2,1)S(1)}, u32[]{:S(2)}, u32[]{:S(2)}) collective-permute-start(bf16[82,320]{1,0:T(8,128)(2,1)S(1)} %get-tuple-element.17), channel_id=1, source_target_pairs={{1,0},{2,1},{3,2},{4,3},{5,4},{6,5},{7,6},{9,8},{10,9},{11,10},{12... | collective-permute-start | bytes 157448 | tf_op jit(solution)/shard_map/ppermute | solution.py:25
  37.3 8.7 %collective-permute-start = (bf16[82,320]{1,0:T(8,128)(2,1)S(1)}, bf16[82,320]{1,0:T(8,128)(2,1)S(1)}, u32[]{:S(2)}, u32[]{:S(2)}) collective-permute-start(bf16[82,320]{1,0:T(8,128)(2,1)S(1)} %get-tuple-element.18), channel_id=1, source_target_pairs={{0,1},{1,2},{2,3},{3,4},{4,5},{5,6},{6,7},{8,9},{9,10},{10,11},{11... | collective-permute-start | bytes 157448 | tf_op jit(solution)/shard_map/ppermute | solution.py:24
  64.2 9.9 %all-to-all-start.1 = ((f32[8,2,128]{2,1,0:T(2,128)}), f32[8,2,128]{2,1,0:T(2,128)S(1)}, u32[]{:S(2)}, u32[]{:S(2)}) async-start(f32[8,2,128]{2,1,0:T(2,128)} %broadcast_in_dim.8), calls=%async_computation.1 | async-start | bytes 16384 | tf_op jit(solution)/shard_map/all_to_all | solution.py:17
  70.2 11.2 %copy-start = (f32[48,80,128]{2,1,0:T(8,128)S(1)}, f32[48,80,128]{2,1,0:T(8,128)}, u32[]{:S(2)}) copy-start(f32[48,80,128]{2,1,0:T(8,128)} %get-tuple-element.12) | copy-start | bytes 5898244
  70.2 11.2 %copy-start.2 = (f32[48,128]{1,0:T(8,128)S(1)}, f32[48,128]{1,0:T(8,128)}, u32[]{:S(2)}) copy-start(f32[48,128]{1,0:T(8,128)} %get-tuple-element.13) | copy-start | bytes 73732
  74.1 52.1 %all-to-all-start.2 = ((bf16[16,5,48,256]{3,2,1,0:T(8,128)(2,1)}), bf16[16,5,48,256]{3,2,1,0:T(8,128)(2,1)}, u32[]{:S(2)}, u32[]{:S(2)}) async-start(bf16[16,5,48,256]{3,2,1,0:T(8,128)(2,1)} %copy.108), calls=%async_computation.2 | async-start | bytes 3932160 | tf_op jit(solution)/shard_map/all_to_all | solution.py:183
  84.5 4.3 %copy-start.1 = (f32[48,80,80]{1,2,0:T(8,128)S(1)}, f32[48,80,80]{1,2,0:T(8,128)}, u32[]{:S(2)}) copy-start(f32[48,80,80]{1,2,0:T(8,128)} %get-tuple-element.22) | copy-start | bytes 3686404
where the time goes:
time: 185 us; the launch traced here: 184 us
  blocking collectives  52.6 us (28%)
  starting transfers between devices  38 us (21%)
  waiting for transfers between devices  32 us (17%)
  matrix products  28.2 us (15%)
  Pallas kernels  16 us (9%)
  local copies, waits for them, and re-layouts  12.4 us (7%)
  other arithmetic  3.34 us (2%)
    all_to_all x1, blocking collectives, per_device(): lax.all_to_all(updated.reshape(groups, held, domains, quantities), MEMBER...  52.6 us
    all_to_all x2, starting transfers between devices, spread_copies(): return lax.all_to_all(copies, axis, split_axis=0, concat_axis=0, tiled=True)  27.3 us
    all_to_all x1, waiting for transfers between devices, per_device(): lax.all_to_all(outgoing, MEMBER, split_axis=0, concat_axis=0, tiled=True)  18.8 us
    pallas_call x1, Pallas kernels, select_domains(): pl.pallas_call(make_table_kernel(members, halo), in_specs=[pl.BlockSpec(m...  16 us
    all_to_all x2, waiting for transfers between devices, spread_copies(): return lax.all_to_all(copies, axis, split_axis=0, concat_axis=0, tiled=True)  13.2 us
    dot_general x3, matrix products, transform(): root_iter = jnp.einsum('nab,nbc->nac', root_iter, factor, precision=exact)  7.66 us
    dot_general x3, matrix products, transform(): jnp.einsum('nab,nbc->nac', factor, inverse, precision=exact)  5.88 us
    all_to_all x1, starting transfers between devices, per_device(): lax.all_to_all(outgoing, MEMBER, split_axis=0, concat_axis=0, tiled=True)  5.41 us
  transfers between devices with their start and end apart: 5, of which 3 were waited for; matrix products, arithmetic and copies ran while one was open for 19% of the time, Pallas kernels for 0%

commit v1 on v0

v1 whole, which is shorter than its diff:
```python
import jax
import jax.numpy as jnp
from jax import lax
from jax.experimental import pallas as pl
from jax.experimental.pallas import tpu as pltpu
from jax.sharding import Mesh
from jax.sharding import PartitionSpec as P


MEMBER = ("member_0", "member_1")
LANES = 128
SUB = 8
SPAN = 6
BATCH = 16
f32, bf16 = jnp.float32, jnp.bfloat16
NT = (((1,), (1,)), ((), ()))


def vmem():
    return pl.BlockSpec(memory_space=pltpu.VMEM)


def smem():
    return pl.BlockSpec(memory_space=pltpu.SMEM)


def spread_copies(value, axis):
    copies = jnp.broadcast_to(value, (lax.axis_size(axis), *value.shape))
    return lax.all_to_all(copies, axis, split_axis=0, concat_axis=0, tiled=True)


def shifted(value, axis, step):
    count = lax.axis_size(axis)
    return lax.ppermute(value, axis, [(i, (i + step) % count) for i in range(count)])


def with_halo(value, axis, width):
    count, length = lax.axis_size(axis), value.shape[1]
    up = [(i, i + 1) for i in range(count - 1)]
    down = [(j, i) for i, j in up]
    before = lax.ppermute(value[:, length - width :], axis, up)
    after = lax.ppermute(value[:, :width], axis, down)
    return jnp.concatenate([before, value, after], axis=1)


def decay_of(index, start, tiers, halo):
    column = start + lax.broadcasted_iota(jnp.int32, index.shape, 0)
    radius = (tiers.astype(f32) + 2.0) * (0.5 * LANES)
    distance = jnp.abs(index - halo - column).astype(f32) / radius
    return jnp.exp(-2.0 * distance * distance)


def sums_kernel(members, halo):
    def kernel(window_ref, lists_ref, tiers_ref, sums_ref, flat):
        for t in range(window_ref.shape[0]):
            raw = window_ref[t].astype(f32)
            observ = raw[:members]
            mean = jnp.sum(observ, axis=0, keepdims=True) * (1.0 / members)
            anomaly = observ - mean
            innov = raw[members : members + 1] - mean
            noise = raw[members + 1 : members + 2]
            energy = jnp.sum(anomaly * anomaly, axis=0, keepdims=True)
            flat[t, 0:SUB] = jnp.broadcast_to(innov * innov / noise, (SUB, LANES))
            flat[t, SUB : 2 * SUB] = jnp.broadcast_to(energy / noise, (SUB, LANES))

        def tile_sum(tile, carry):
            fit, spread = carry
            fit_rows = [flat[tile + t, 0:SUB] for t in range(SPAN)]
            spread_rows = [flat[tile + t, SUB : 2 * SUB] for t in range(SPAN)]
            for s in range(LANES // SUB):
                start = pl.multiple_of(tile * LANES + s * SUB, SUB)
                rows = pl.ds(start, SUB)
                index = lists_ref[rows, :]
                local = index - tile * LANES
                low, high = local & (LANES - 1), local >> 7
                decay = decay_of(index, start, tiers_ref[rows, :], halo)
                a = b = jnp.zeros((SUB, LANES), f32)
                for t in range(SPAN):
                    here = high == t
                    fits = jnp.take_along_axis(fit_rows[t], low, axis=1, mode="promise_in_bounds")
                    spreads = jnp.take_along_axis(spread_rows[t], low, axis=1, mode="promise_in_bounds")
                    a, b = jnp.where(here, fits, a), jnp.where(here, spreads, b)
                fit, spread = fit + decay * a, spread + decay * b
            return fit, spread

        zero = jnp.zeros((SUB, LANES), f32)
        fit, spread = lax.fori_loop(0, lists_ref.shape[0] // LANES, tile_sum, (zero, zero))
        sums_ref[0:1, :] = jnp.sum(fit, axis=0, keepdims=True)
        sums_ref[1:2, :] = jnp.sum(spread, axis=0, keepdims=True)

    return kernel


def block_sums(window, lists, tiers, members, halo):
    return pl.pallas_call(
        sums_kernel(members, halo),
        in_specs=[vmem()] * 3,
        out_specs=vmem(),
        out_shape=jax.ShapeDtypeStruct((2, LANES), f32),
        scratch_shapes=[pltpu.VMEM((window.shape[0], 2 * SUB, LANES), f32)],
        cost_estimate=pl.CostEstimate(flops=10_000_000, bytes_accessed=1_000_000, transcendentals=100_000),
        name="block_sums",
    )(window, lists, tiers)


def split(value):
    high = value.astype(bf16)
    return high, (value - high.astype(f32)).astype(bf16)


def gram_kernel(members, halo):
    def kernel(first_ref, window_ref, lists_ref, tiers_ref, gram_ref):
        def block(b, unused):
            rows = pl.ds(pl.multiple_of(b * SUB, SUB), SUB)
            start = first_ref[0] + b * SUB
            index = lists_ref[rows, :]
            decay = decay_of(index, start, tiers_ref[rows, :], halo)
            tile = start // LANES
            local = index - tile * LANES
            table = jnp.concatenate([window_ref[tile + t] for t in range(SPAN)], axis=1)
            place = lax.broadcasted_iota(jnp.int32, (SPAN * LANES, LANES), 0)
            for s in range(SUB):
                chosen = jnp.where(place == local[s : s + 1], 1.0, 0.0).astype(bf16)
                picked = jnp.dot(table, chosen, preferred_element_type=f32)
                mean = jnp.sum(picked[:members], axis=0, keepdims=True) * (1.0 / members)
                anomaly = picked - mean
                weight = decay[s : s + 1] / picked[members + 1 : members + 2]
                high, low = split(anomaly)
                weighted_high, weighted_low = split(anomaly[:members] * weight)
                left = jnp.concatenate([weighted_high, weighted_high, weighted_low], axis=1)
                right = jnp.concatenate([high, low, high], axis=1)
                gram_ref[b * SUB + s] = lax.dot_general(left, right, NT, preferred_element_type=f32)
            return unused

        lax.fori_loop(0, gram_ref.shape[0] // SUB, block, 0)

    return kernel


def grams(first, window, lists, tiers, members, halo):
    own = lists.shape[0]
    return pl.pallas_call(
        gram_kernel(members, halo),
        in_specs=[smem(), vmem(), vmem(), vmem()],
        out_specs=vmem(),
        out_shape=jax.ShapeDtypeStruct((own, members, members + SUB), f32),
        cost_estimate=pl.CostEstimate(flops=own * 60_000_000, bytes_accessed=own * 40_000, transcendentals=own * LANES),
        name="grams",
    )(first, window, lists, tiers)


def product(a, b):
    size = a.shape[0]
    pad = LANES - size
    (ah, al), (bh, bl) = split(a), split(b)
    wide, tall = jnp.zeros((size, pad), bf16), jnp.zeros((pad, size), bf16)
    left = jnp.concatenate([ah, wide, al, wide, ah, wide], axis=1)
    right = jnp.concatenate([bh, tall, bh, tall, bl, tall], axis=0)
    return jnp.dot(left, right, preferred_element_type=f32)


def root_kernel(members, parts):
    def kernel(mine_ref, other_ref, *refs):
        gram_refs, trans_ref = refs[:parts], refs[parts]
        total = mine_ref[...] + other_ref[...]
        ridge = jnp.sum(total[1:2], axis=1, keepdims=True) / jnp.sum(total[0:1], axis=1, keepdims=True)
        row = lax.broadcasted_iota(jnp.int32, (members, members), 0)
        col = lax.broadcasted_iota(jnp.int32, (members, members), 1)
        eye = jnp.where(row == col, 1.0, 0.0)
        offset = 0
        for gram_ref in gram_refs:
            own = gram_ref.shape[0]

            def block(b, unused, gram_ref=gram_ref, offset=offset):
                at = [b * BATCH + s for s in range(BATCH)]
                raw = [gram_ref[n] for n in at]
                mats = [r[:, :members] + ridge * eye for r in raw]
                bounds = [
                    jnp.max(jnp.sum(jnp.abs(m), axis=0, keepdims=True), axis=1, keepdims=True) for m in mats
                ]
                s0 = [m * (1.0 / bound) for m, bound in zip(mats, bounds)]
                q0 = [product(s, s) for s in s0]
                s1 = [2.25 * s + (product(q, 0.25 * s) - 1.5 * q) for s, q in zip(s0, q0)]
                q1 = [product(s, s) for s in s1]
                a = [0.25 * product(s, r) - 0.75 * (s + r) for s, r in zip(s0, s1)]
                s2 = [2.25 * s + (product(q, 0.25 * s) - 1.5 * q) for s, q in zip(s1, q1)]
                q2 = [product(s, s) for s in s2]
                c = [1.6875 * q - 2.4375 * s + product(q, 0.0625 * q - 0.5625 * s) for s, q in zip(s2, q2)]
                z = [5.0625 * eye + 2.25 * (x + y) + product(x, y) for x, y in zip(a, c)]
                root = [v / jnp.sqrt(bound) for v, bound in zip(z, bounds)]
                half = [jnp.sum(r * g[:, members : members + 1], axis=0, keepdims=True) for r, g in zip(root, raw)]
                gain = [jnp.sum(r * h, axis=1, keepdims=True) for r, h in zip(root, half)]
                for n, r, g in zip(at, root, gain):
                    full = r * ((members - 1.0) ** 0.5) + g
                    full = full - (jnp.sum(full, axis=0, keepdims=True) - 1.0) * (1.0 / members)
                    trans_ref[offset + n] = full.astype(bf16)
                return unused

            lax.fori_loop(0, own // BATCH, block, 0)
            offset += own

    return kernel


def roots(mine, other, pieces, members):
    own = sum(p.shape[0] for p in pieces)
    return pl.pallas_call(
        root_kernel(members, len(pieces)),
        in_specs=[vmem()] * (2 + len(pieces)),
        out_specs=vmem(),
        out_shape=jax.ShapeDtypeStruct((own, members, members), bf16),
        cost_estimate=pl.CostEstimate(flops=own * 60_000_000, bytes_accessed=own * 50_000, transcendentals=0),
        name="roots",
    )(mine, other, *pieces)


def per_device(
    prior_trials,
    prior_at_sensors,
    sensor_readings,
    sensor_noise_spread,
    nearby_readings,
    subarea_cutoff_level,
):
    held, patch_cells, quantities = prior_trials.shape
    obs_count = nearby_readings.shape[1]
    halo_cells = 5 * obs_count // 2
    groups = lax.axis_size(MEMBER)
    members = held * groups
    domains = patch_cells // groups

    gathered = spread_copies(prior_at_sensors, MEMBER).reshape(members, patch_cells)
    outgoing = prior_trials.reshape(held, groups, domains, quantities).transpose(1, 0, 2, 3)
    incoming = lax.all_to_all(outgoing, MEMBER, split_axis=0, concat_axis=0, tiled=True)
    incoming = incoming.reshape(members, domains, quantities)

    obs_rows = jnp.stack([sensor_readings, sensor_noise_spread], axis=0)
    window = with_halo(jnp.concatenate([gathered, obs_rows], axis=0), "space", halo_cells)
    tiles = patch_cells // LANES + SPAN
    window = jnp.pad(window, ((0, SUB - 2), (0, tiles * LANES - window.shape[1])))
    window = window.reshape(members + SUB, tiles, LANES).transpose(1, 0, 2)

    tiers = subarea_cutoff_level[:, None]
    first = (lax.axis_index(MEMBER) * domains).astype(jnp.int32)
    own_lists = lax.dynamic_slice_in_dim(nearby_readings, first, domains, 0)
    own_tiers = lax.dynamic_slice_in_dim(tiers, first, domains, 0)
    mine = block_sums(window, nearby_readings, tiers, members, halo_cells)
    share = domains // 3
    pieces = []
    for r in range(3):
        other = shifted(mine, "space", 1 << r)
        part = slice(r * share, (r + 1) * share)
        start = (first + r * share).reshape(1)
        pieces.append(grams(start, window, own_lists[part], own_tiers[part], members, halo_cells))
        if r < 2:
            mine = mine + other
    trans_w = roots(mine, other, pieces, members)

    updated = jnp.einsum("inc,nij->jnc", incoming, trans_w, preferred_element_type=f32).astype(bf16)
    returned = lax.all_to_all(
        updated.reshape(groups, held, domains, quantities), MEMBER, split_axis=0, concat_axis=0, tiled=True
    )
    return returned.transpose(1, 0, 2, 3).reshape(held, patch_cells, quantities)


def solution(mesh):
    finer = Mesh(
        mesh.devices.reshape(mesh.shape["region"], mesh.shape["member"] // 2, 2, mesh.shape["space"]),
        ("region", "member_0", "member_1", "space"),
    )
    return jax.shard_map(
        per_device,
        mesh=finer,
        in_specs=(
            P(MEMBER, ("region", "space"), None),
            P(MEMBER, ("region", "space")),
            P(("region", "space")),
            P(("region", "space")),
            P(("region", "space"), None),
            P(("region", "space")),
        ),
        out_specs=P(MEMBER, ("region", "space"), None),
        check_vma=False,
    )
```

time: 185 us -> 151 us (0.82)
  the two profiles are of different devices: /device:TPU:513 before, /device:TPU:515 now
where the time goes in v1:
time: 151 us; the launch traced here: 150 us
  blocking collectives  55.8 us (37%)
  starting transfers between devices  37.4 us (25%)
  Pallas kernels  34.9 us (23%)
  local copies, waits for them, and re-layouts  12.6 us (8%)
  waiting for transfers between devices  7.27 us (5%)
  matrix products  2.04 us (1%)
    all_to_all x1, blocking collectives, per_device(): lax.all_to_all(updated.reshape(groups, held, domains, quantities), MEMBER...  55.8 us
    pallas_call x3, Pallas kernels, grams(): pl.pallas_call(gram_kernel(members, halo), in_specs=[smem(), vmem(), vmem...  17.5 us
    all_to_all x1, starting transfers between devices, spread_copies(): return lax.all_to_all(copies, axis, split_axis=0, concat_axis=0, tiled=True)  13.8 us
    pallas_call x1, Pallas kernels, roots(): pl.pallas_call(root_kernel(members, len(pieces)), in_specs=[vmem()] * (2...  13.3 us
    ppermute x1, starting transfers between devices, with_halo(): after = lax.ppermute(value[:, :width], axis, down)  11.6 us
    all_to_all x1, waiting for transfers between devices, spread_copies(): return lax.all_to_all(copies, axis, split_axis=0, concat_axis=0, tiled=True)  7.25 us
    ppermute x3, starting transfers between devices, shifted(): lax.ppermute(value, axis, [(i, (i + step) % count) for i in range(count)])  6.15 us
    pallas_call x1, Pallas kernels, block_sums(): pl.pallas_call(sums_kernel(members, halo), in_specs=[vmem()] * 3, out_spe...  4.13 us
  transfers between devices with their start and end apart: 7, of which 1 were waited for; matrix products, arithmetic and copies ran while one was open for 6% of the time, Pallas kernels for 23%

profile of v1, /device:TPU:515, one launch (start us, length us, event | category | flops | bytes accessed | tf_op | source)
XLA Modules:
  0.0 150.2 jit_solution(14306170445251203030)
XLA Ops:
  0.0 1.4 broadcast_in_dim.6
  1.4 13.8 %all-to-all-start = ((bf16[16,5,768]{2,1,0:T(8,128)(2,1)}), bf16[16,5,768]{2,1,0:T(8,128)(2,1)S(1)}, u32[]{:S(2)}, u32[]{:S(2)}) async-start(bf16[16,5,768]{2,1,0:T(8,128)(2,1)} %broadcast_in_dim.6), calls=%async_computation | async-start | bytes 393216 | tf_op jit(solution)/shard_map/all_to_all | solution.py:29
  15.2 2.9 %copy.36 = bf16[16,5,48,256]{3,2,1,0:T(8,128)(2,1)} copy(bf16[16,5,48,256]{3,2,0,1:T(8,128)(2,1)} %bitcast.29) | data formatting | bytes 3932160 | tf_op jit(solution)/shard_map/transpose | solution.py:233
  18.1 7.3 %all-to-all-done = bf16[16,5,768]{2,1,0:T(8,128)(2,1)S(1)} async-done(((bf16[16,5,768]{2,1,0:T(8,128)(2,1)}), bf16[16,5,768]{2,1,0:T(8,128)(2,1)S(1)}, u32[]{:S(2)}, u32[]{:S(2)}) %all-to-all-start) | async-done | bytes 122912 | tf_op jit(solution)/shard_map/all_to_all | solution.py:29
  25.4 3.9 %all-to-all-start.1 = ((bf16[16,5,48,256]{3,2,1,0:T(8,128)(2,1)}), bf16[16,5,48,256]{3,2,1,0:T(8,128)(2,1)S(1)}, u32[]{:S(2)}, u32[]{:S(2)}) async-start(bf16[16,5,48,256]{3,2,1,0:T(8,128)(2,1)} %copy.36), calls=%async_computation.1 | async-start | bytes 3932160 | tf_op jit(solution)/shard_map/all_to_all | solution.py:234
  29.6 11.6 %collective-permute-start.1 = (bf16[82,320]{1,0:T(8,128)(2,1)S(1)}, bf16[82,320]{1,0:T(8,128)(2,1)S(1)}, u32[]{:S(2)}, u32[]{:S(2)}) collective-permute-start(bf16[82,320]{1,0:T(8,128)(2,1)S(1)} %get-tuple-element.8), channel_id=1, source_target_pairs={{1,0},{2,1},{3,2},{4,3},{5,4},{6,5},{7,6},{9,8},{10,9},{11,10},{12... | collective-permute-start | bytes 157448 | tf_op jit(solution)/shard_map/ppermute | solution.py:42
  41.3 2.0 %collective-permute-start = (bf16[82,320]{1,0:T(8,128)(2,1)S(1)}, bf16[82,320]{1,0:T(8,128)(2,1)S(1)}, u32[]{:S(2)}, u32[]{:S(2)}) collective-permute-start(bf16[82,320]{1,0:T(8,128)(2,1)S(1)} %get-tuple-element.9), channel_id=1, source_target_pairs={{0,1},{1,2},{2,3},{3,4},{4,5},{5,6},{6,7},{8,9},{9,10},{10,11},{11... | collective-permute-start | bytes 157448 | tf_op jit(solution)/shard_map/ppermute | solution.py:41
  43.2 1.4 constant_dynamic-slice_fusion.2
  44.6 0.9 broadcast_in_dim.8.tiers_ref
  45.5 0.7 copy.35.tiers_ref
  46.2 0.7 copy.34.tiers_ref
  46.9 0.7 copy.33.tiers_ref
  47.8 0.8 bitcast_bitcast_fusion.window_ref
  48.5 4.1 %block_sums.1 = f32[2,128]{1,0:T(2,128)} custom-call(bf16[12,88,128]{2,1,0:T(8,128)(2,1)} %bitcast_bitcast_fusion.window_ref, s32[768,128]{1,0:T(8,128)} %lists_ref.1, s32[768,1]{1,0:T(8,128)} %broadcast_in_dim.8.tiers_ref), custom_call_target="tpu_custom_call" | custom-call | flops 10000000 | bytes 1000000 | tf_op jit(solution)/shard_map/block_sums/pallas_call | solution.py:95
  52.6 5.8 %grams.5.refs_2_ = f32[16,80,88]{2,1,0:T(8,128)} custom-call(s32[1]{0:T(128)} %bitcast.5.first_ref, bf16[12,88,128]{2,1,0:T(8,128)(2,1)} %bitcast_bitcast_fusion.window_ref, s32[16,128]{1,0:T(8,128)} %get-tuple-element.5.lists_ref, s32[16,1]{1,0:T(8,128)} %copy.35.tiers_ref), custom_call_target="tpu_custom_call" | custom-call | flops 960000000 | bytes 640000 | tf_op jit(solution)/shard_map/grams/pallas_call | solution.py:142
  58.6 5.8 %grams.4.refs_1_ = f32[16,80,88]{2,1,0:T(8,128)} custom-call(s32[1]{0:T(128)} %bitcast.3.first_ref, bf16[12,88,128]{2,1,0:T(8,128)(2,1)} %bitcast_bitcast_fusion.window_ref, s32[16,128]{1,0:T(8,128)} %get-tuple-element.6.lists_ref, s32[16,1]{1,0:T(8,128)} %copy.34.tiers_ref), custom_call_target="tpu_custom_call" | custom-call | flops 960000000 | bytes 640000 | tf_op jit(solution)/shard_map/grams/pallas_call | solution.py:142
  64.4 6.0 %collective-permute-start.4 = (f32[2,128]{1,0:T(2,128)S(1)}, f32[2,128]{1,0:T(2,128)S(1)}, u32[]{:S(2)}, u32[]{:S(2)}) collective-permute-start(f32[2,128]{1,0:T(2,128)S(1)} %add.22.mine_ref), channel_id=1, source_target_pairs={{0,4},{1,5},{2,6},{3,7},{4,0},{5,1},{6,2},{7,3},{8,12},{9,13},{10,... | collective-permute-start | bytes 3080 | tf_op jit(solution)/shard_map/ppermute | solution.py:34
  70.4 5.9 %grams.3.refs_0_ = f32[16,80,88]{2,1,0:T(8,128)} custom-call(s32[1]{0:T(128)} %bitcast.1.first_ref, bf16[12,88,128]{2,1,0:T(8,128)(2,1)} %bitcast_bitcast_fusion.window_ref, s32[16,128]{1,0:T(8,128)} %get-tuple-element.7.lists_ref, s32[16,1]{1,0:T(8,128)} %copy.33.tiers_ref), custom_call_target="tpu_custom_call" | custom-call | flops 960000000 | bytes 640000 | tf_op jit(solution)/shard_map/grams/pallas_call | solution.py:142
  76.3 0.6 copy-done.5
  76.9 13.3 %roots.1 = bf16[48,80,80]{2,1,0:T(8,128)(2,1)} custom-call(f32[2,128]{1,0:T(2,128)} %copy-done.4, f32[2,128]{1,0:T(2,128)} %copy-done.5, f32[16,80,88]{2,1,0:T(8,128)} %grams.3.refs_0_, f32[16,80,88]{2,1,0:T(8,128)} %grams.4.refs_1_, f32[16,80,88]{2,1,0:T(8,128)} %grams.5.refs_2_), custom_call_target="tpu_custom_call" | custom-call | flops 2880000000 | bytes 2400000 | tf_op jit(solution)/shard_map/roots/pallas_call | solution.py:207
  90.2 2.0 %convert_bitcast_fusion = bf16[80,48,256]{2,0,1:T(8,128)(2,1)S(1)} fusion(bf16[48,80,80]{2,1,0:T(8,128)(2,1)} %roots.1, bf16[80,48,256]{2,1,0:T(8,128)(2,1)S(1)} %bitcast.26), kind=kOutput, calls=%fused_computation.2 | convolution fusion | flops 158269440 | bytes 4546560 | tf_op jit(solution)/shard_map/inc,nij->jnc/dot_general | solution.py:259
  92.2 0.7 copy.39
  92.9 55.8 %all_to_all.15 = bf16[16,5,48,256]{3,2,1,0:T(8,128)(2,1)S(1)} all-to-all(bf16[16,5,48,256]{3,2,1,0:T(8,128)(2,1)S(1)} %bitcast.27), channel_id=1, replica_groups=mesh['region'=2,'member_0'=8,'member_1'=2,'space'=8] {'member_0','member..., dimensions={0} | all-to-all | bytes 3932160 | tf_op jit(solution)/shard_map/all_to_all | solution.py:260
  148.8 1.5 copy.40
  (29 shorter events, 0.7 us)
Async XLA Ops:
  1.4 24.0 %all-to-all-start = ((bf16[16,5,768]{2,1,0:T(8,128)(2,1)}), bf16[16,5,768]{2,1,0:T(8,128)(2,1)S(1)}, u32[]{:S(2)}, u32[]{:S(2)}) async-start(bf16[16,5,768]{2,1,0:T(8,128)(2,1)} %broadcast_in_dim.6), calls=%async_computation | async-start | bytes 393216 | tf_op jit(solution)/shard_map/all_to_all | solution.py:29
  18.1 11.2 %copy-start = (s32[768]{0:T(1024)S(1)}, s32[768]{0:T(1024)}, u32[]{:S(2)}) copy-start(s32[768]{0:T(1024)} %param.11) | copy-start | bytes 9220
  18.1 11.2 %copy-start.2 = (bf16[768]{0:T(1024)(128)(2,1)S(1)}, bf16[768]{0:T(1024)(128)(2,1)}, u32[]{:S(2)}) copy-start(bf16[768]{0:T(1024)(128)(2,1)} %param.8) | copy-start | bytes 4612
  18.1 11.2 %copy-start.3 = (bf16[768]{0:T(1024)(128)(2,1)S(1)}, bf16[768]{0:T(1024)(128)(2,1)}, u32[]{:S(2)}) copy-start(bf16[768]{0:T(1024)(128)(2,1)} %param.9) | copy-start | bytes 4612
  25.4 64.8 %all-to-all-start.1 = ((bf16[16,5,48,256]{3,2,1,0:T(8,128)(2,1)}), bf16[16,5,48,256]{3,2,1,0:T(8,128)(2,1)S(1)}, u32[]{:S(2)}, u32[]{:S(2)}) async-start(bf16[16,5,48,256]{3,2,1,0:T(8,128)(2,1)} %copy.36), calls=%async_computation.1 | async-start | bytes 3932160 | tf_op jit(solution)/shard_map/all_to_all | solution.py:234
  29.6 17.9 %collective-permute-start.1 = (bf16[82,320]{1,0:T(8,128)(2,1)S(1)}, bf16[82,320]{1,0:T(8,128)(2,1)S(1)}, u32[]{:S(2)}, u32[]{:S(2)}) collective-permute-start(bf16[82,320]{1,0:T(8,128)(2,1)S(1)} %get-tuple-element.8), channel_id=1, source_target_pairs={{1,0},{2,1},{3,2},{4,3},{5,4},{6,5},{7,6},{9,8},{10,9},{11,10},{12... | collective-permute-start | bytes 157448 | tf_op jit(solution)/shard_map/ppermute | solution.py:42
  41.3 6.3 %collective-permute-start = (bf16[82,320]{1,0:T(8,128)(2,1)S(1)}, bf16[82,320]{1,0:T(8,128)(2,1)S(1)}, u32[]{:S(2)}, u32[]{:S(2)}) collective-permute-start(bf16[82,320]{1,0:T(8,128)(2,1)S(1)} %get-tuple-element.9), channel_id=1, source_target_pairs={{0,1},{1,2},{2,3},{3,4},{4,5},{5,6},{6,7},{8,9},{9,10},{10,11},{11... | collective-permute-start | bytes 157448 | tf_op jit(solution)/shard_map/ppermute | solution.py:41
  52.6 5.8 %copy-start.1 = (f32[2,128]{1,0:T(2,128)S(1)}, f32[2,128]{1,0:T(2,128)}, u32[]{:S(2)}) copy-start(f32[2,128]{1,0:T(2,128)} %block_sums.1) | copy-start | bytes 3076
  52.6 5.8 %collective-permute-start.2 = (f32[2,128]{1,0:T(2,128)}, f32[2,128]{1,0:T(2,128)S(1)}, u32[]{:S(2)}, u32[]{:S(2)}) collective-permute-start(f32[2,128]{1,0:T(2,128)} %block_sums.1), channel_id=1, source_target_pairs={{0,1},{1,2},{2,3},{3,4},{4,5},{5,6},{6,7},{7,0},{8,9},{9,10},{10,1... | collective-permute-start | bytes 3080 | tf_op jit(solution)/shard_map/ppermute | solution.py:34
  58.5 5.9 %collective-permute-start.3 = (f32[2,128]{1,0:T(2,128)S(1)}, f32[2,128]{1,0:T(2,128)S(1)}, u32[]{:S(2)}, u32[]{:S(2)}) collective-permute-start(f32[2,128]{1,0:T(2,128)S(1)} %add.21), channel_id=1, source_target_pairs={{0,2},{1,3},{2,4},{3,5},{4,6},{5,7},{6,0},{7,1},{8,10},{9,11},{10,... | collective-permute-start | bytes 3080 | tf_op jit(solution)/shard_map/ppermute | solution.py:34
  64.4 12.0 %copy-start.4 = (f32[2,128]{1,0:T(2,128)}, f32[2,128]{1,0:T(2,128)S(1)}, u32[]{:S(2)}) copy-start(f32[2,128]{1,0:T(2,128)S(1)} %add.22.mine_ref) | copy-start | bytes 3076
  64.4 12.0 %collective-permute-start.4 = (f32[2,128]{1,0:T(2,128)S(1)}, f32[2,128]{1,0:T(2,128)S(1)}, u32[]{:S(2)}, u32[]{:S(2)}) collective-permute-start(f32[2,128]{1,0:T(2,128)S(1)} %add.22.mine_ref), channel_id=1, source_target_pairs={{0,4},{1,5},{2,6},{3,7},{4,0},{5,1},{6,2},{7,3},{8,12},{9,13},{10,... | collective-permute-start | bytes 3080 | tf_op jit(solution)/shard_map/ppermute | solution.py:34
  76.3 0.6 copy-start.5

commit v2 on v1

--- a/solution.py
+++ b/solution.py
@@ -43,25 +43,38 @@
     return jnp.concatenate([before, value, after], axis=1)
 
 
-def decay_of(index, start, tiers, halo):
-    column = start + lax.broadcasted_iota(jnp.int32, index.shape, 0)
-    radius = (tiers.astype(f32) + 2.0) * (0.5 * LANES)
-    distance = jnp.abs(index - halo - column).astype(f32) / radius
-    return jnp.exp(-2.0 * distance * distance)
-
-
 def sums_kernel(members, halo):
-    def kernel(window_ref, lists_ref, tiers_ref, sums_ref, flat):
+    def kernel(first_ref, tiers_ref, window_ref, lists_ref, sums_ref, local_ref, decay_ref, flat):
+        sub = lax.broadcasted_iota(jnp.int32, (SUB, LANES), 0)
+
+        def decay_at(index, start):
+            tier = jnp.zeros((SUB, LANES), jnp.int32)
+            for s in range(SUB):
+                tier = jnp.where(sub == s, tiers_ref[start + s], tier)
+            radius = (tier.astype(f32) + 2.0) * (0.5 * LANES)
+            distance = jnp.abs(index - halo - start - sub).astype(f32) / radius
+            return jnp.exp(-2.0 * distance * distance)
+
         for t in range(window_ref.shape[0]):
             raw = window_ref[t].astype(f32)
             observ = raw[:members]
             mean = jnp.sum(observ, axis=0, keepdims=True) * (1.0 / members)
             anomaly = observ - mean
             innov = raw[members : members + 1] - mean
-            noise = raw[members + 1 : members + 2]
+            scale = 1.0 / raw[members + 1 : members + 2]
             energy = jnp.sum(anomaly * anomaly, axis=0, keepdims=True)
-            flat[t, 0:SUB] = jnp.broadcast_to(innov * innov / noise, (SUB, LANES))
-            flat[t, SUB : 2 * SUB] = jnp.broadcast_to(energy / noise, (SUB, LANES))
+            flat[t, 0:SUB] = jnp.broadcast_to(innov * innov * scale, (SUB, LANES))
+            flat[t, SUB : 2 * SUB] = jnp.broadcast_to(energy * scale, (SUB, LANES))
+
+        def own_rows(b, unused):
+            start = pl.multiple_of(first_ref[0] + b * SUB, SUB)
+            rows = pl.ds(pl.multiple_of(b * SUB, SUB), SUB)
+            index = lists_ref[pl.ds(start, SUB), :]
+            local_ref[rows, :] = index - start // LANES * LANES
+            decay_ref[rows, :] = decay_at(index, start)
+            return unused
+
+        lax.fori_loop(0, local_ref.shape[0] // SUB, own_rows, 0)
 
         def tile_sum(tile, carry):
             fit, spread = carry
@@ -69,11 +82,10 @@
             spread_rows = [flat[tile + t, SUB : 2 * SUB] for t in range(SPAN)]
             for s in range(LANES // SUB):
                 start = pl.multiple_of(tile * LANES + s * SUB, SUB)
-                rows = pl.ds(start, SUB)
-                index = lists_ref[rows, :]
+                index = lists_ref[pl.ds(start, SUB), :]
                 local = index - tile * LANES
                 low, high = local & (LANES - 1), local >> 7
-                decay = decay_of(index, start, tiers_ref[rows, :], halo)
+                decay = decay_at(index, start)
                 a = b = jnp.zeros((SUB, LANES), f32)
                 for t in range(SPAN):
                     here = high == t
@@ -91,16 +103,20 @@
     return kernel
 
 
-def block_sums(window, lists, tiers, members, halo):
+def block_sums(first, tiers, window, lists, members, own, halo):
     return pl.pallas_call(
         sums_kernel(members, halo),
-        in_specs=[vmem()] * 3,
-        out_specs=vmem(),
-        out_shape=jax.ShapeDtypeStruct((2, LANES), f32),
+        in_specs=[smem(), smem(), vmem(), vmem()],
+        out_specs=[vmem()] * 3,
+        out_shape=[
+            jax.ShapeDtypeStruct((2, LANES), f32),
+            jax.ShapeDtypeStruct((own, LANES), jnp.int32),
+            jax.ShapeDtypeStruct((own, LANES), f32),
+        ],
         scratch_shapes=[pltpu.VMEM((window.shape[0], 2 * SUB, LANES), f32)],
         cost_estimate=pl.CostEstimate(flops=10_000_000, bytes_accessed=1_000_000, transcendentals=100_000),
         name="block_sums",
-    )(window, lists, tiers)
+    )(first, tiers, window, lists)
 
 
 def split(value):
@@ -108,28 +124,29 @@
     return high, (value - high.astype(f32)).astype(bf16)
 
 
-def gram_kernel(members, halo):
-    def kernel(first_ref, window_ref, lists_ref, tiers_ref, gram_ref):
+def gram_kernel(members, skip):
+    def kernel(first_ref, window_ref, local_ref, decay_ref, gram_ref, place):
+        place[...] = lax.broadcasted_iota(jnp.int32, (SPAN * LANES, LANES), 0)
+
         def block(b, unused):
+            tile = (first_ref[0] + skip + b * SUB) // LANES
             rows = pl.ds(pl.multiple_of(b * SUB, SUB), SUB)
-            start = first_ref[0] + b * SUB
-            index = lists_ref[rows, :]
-            decay = decay_of(index, start, tiers_ref[rows, :], halo)
-            tile = start // LANES
-            local = index - tile * LANES
+            local, decay = local_ref[rows, :], decay_ref[rows, :]
             table = jnp.concatenate([window_ref[tile + t] for t in range(SPAN)], axis=1)
-            place = lax.broadcasted_iota(jnp.int32, (SPAN * LANES, LANES), 0)
-            for s in range(SUB):
-                chosen = jnp.where(place == local[s : s + 1], 1.0, 0.0).astype(bf16)
-                picked = jnp.dot(table, chosen, preferred_element_type=f32)
-                mean = jnp.sum(picked[:members], axis=0, keepdims=True) * (1.0 / members)
-                anomaly = picked - mean
-                weight = decay[s : s + 1] / picked[members + 1 : members + 2]
-                high, low = split(anomaly)
-                weighted_high, weighted_low = split(anomaly[:members] * weight)
-                left = jnp.concatenate([weighted_high, weighted_high, weighted_low], axis=1)
-                right = jnp.concatenate([high, low, high], axis=1)
-                gram_ref[b * SUB + s] = lax.dot_general(left, right, NT, preferred_element_type=f32)
+            for s in range(0, SUB, 2):
+                chosen = [jnp.where(place[...] == local[n : n + 1], 1.0, 0.0).astype(bf16) for n in (s, s + 1)]
+                both = jnp.dot(table, jnp.concatenate(chosen, axis=1), preferred_element_type=f32)
+                for i in range(2):
+                    n = s + i
+                    picked = both[:, i * LANES : (i + 1) * LANES]
+                    mean = jnp.sum(picked[:members], axis=0, keepdims=True) * (1.0 / members)
+                    anomaly = picked - mean
+                    weight = decay[n : n + 1] / picked[members + 1 : members + 2]
+                    high, low = split(anomaly)
+                    weighted_high, weighted_low = split(anomaly[:members] * weight)
+                    left = jnp.concatenate([weighted_high, weighted_high, weighted_low], axis=1)
+                    right = jnp.concatenate([high, low, high], axis=1)
+                    gram_ref[b * SUB + n] = lax.dot_general(left, right, NT, preferred_element_type=f32)
             return unused
 
         lax.fori_loop(0, gram_ref.shape[0] // SUB, block, 0)
@@ -137,32 +154,46 @@
     return kernel
 
 
-def grams(first, window, lists, tiers, members, halo):
-    own = lists.shape[0]
+def grams(first, window, local, decay, members, part, parts):
+    own = local.shape[0] // parts
     return pl.pallas_call(
-        gram_kernel(members, halo),
-        in_specs=[smem(), vmem(), vmem(), vmem()],
-        out_specs=vmem(),
+        gram_kernel(members, part * own),
+        grid=(1,),
+        in_specs=[
+            smem(),
+            pl.BlockSpec(window.shape, lambda i: (0, 0, 0)),
+            pl.BlockSpec((own, LANES), lambda i: (part, 0)),
+            pl.BlockSpec((own, LANES), lambda i: (part, 0)),
+        ],
+        out_specs=pl.BlockSpec((own, members, members + SUB), lambda i: (0, 0, 0)),
         out_shape=jax.ShapeDtypeStruct((own, members, members + SUB), f32),
-        cost_estimate=pl.CostEstimate(flops=own * 60_000_000, bytes_accessed=own * 40_000, transcendentals=own * LANES),
+        scratch_shapes=[pltpu.VMEM((SPAN * LANES, LANES), jnp.int32)],
+        cost_estimate=pl.CostEstimate(flops=own * 60_000_000, bytes_accessed=own * 40_000, transcendentals=0),
         name="grams",
-    )(first, window, lists, tiers)
-
-
-def product(a, b):
-    size = a.shape[0]
-    pad = LANES - size
-    (ah, al), (bh, bl) = split(a), split(b)
-    wide, tall = jnp.zeros((size, pad), bf16), jnp.zeros((pad, size), bf16)
-    left = jnp.concatenate([ah, wide, al, wide, ah, wide], axis=1)
-    right = jnp.concatenate([bh, tall, bh, tall, bl, tall], axis=0)
-    return jnp.dot(left, right, preferred_element_type=f32)
+    )(first, window, local, decay)
+
+
+def products(left, right):
+    size = left[0].shape[0]
+    gap = jnp.zeros((3 * size, LANES - size), bf16)
+    results = []
+    for i in range(0, len(left), 2):
+        rows, columns = [], []
+        for a, b in zip(left[i : i + 2], right[i : i + 2]):
+            (ah, al), (bh, bl) = split(a), split(b)
+            rows.append(jnp.concatenate([ah, al, ah], axis=1))
+            columns += [jnp.concatenate([bh, bh, bl], axis=0), gap]
+        both = jnp.dot(
+            jnp.concatenate(rows, axis=0), jnp.concatenate(columns, axis=1), preferred_element_type=f32
+        )
+        results += [both[:size, :size], both[size:, LANES : LANES + size]]
+    return results
 
 
 def root_kernel(members, parts):
-    def kernel(mine_ref, other_ref, *refs):
+    def kernel(sums_ref, other_ref, *refs):
         gram_refs, trans_ref = refs[:parts], refs[parts]
-        total = mine_ref[...] + other_ref[...]
+        total = sums_ref[...] + other_ref[...]
         ridge = jnp.sum(total[1:2], axis=1, keepdims=True) / jnp.sum(total[0:1], axis=1, keepdims=True)
         row = lax.broadcasted_iota(jnp.int32, (members, members), 0)
         col = lax.broadcasted_iota(jnp.int32, (members, members), 1)
@@ -179,14 +210,15 @@
                     jnp.max(jnp.sum(jnp.abs(m), axis=0, keepdims=True), axis=1, keepdims=True) for m in mats
                 ]
                 s0 = [m * (1.0 / bound) for m, bound in zip(mats, bounds)]
-                q0 = [product(s, s) for s in s0]
-                s1 = [2.25 * s + (product(q, 0.25 * s) - 1.5 * q) for s, q in zip(s0, q0)]
-                q1 = [product(s, s) for s in s1]
-                a = [0.25 * product(s, r) - 0.75 * (s + r) for s, r in zip(s0, s1)]
-                s2 = [2.25 * s + (product(q, 0.25 * s) - 1.5 * q) for s, q in zip(s1, q1)]
-                q2 = [product(s, s) for s in s2]
-                c = [1.6875 * q - 2.4375 * s + product(q, 0.0625 * q - 0.5625 * s) for s, q in zip(s2, q2)]
-                z = [5.0625 * eye + 2.25 * (x + y) + product(x, y) for x, y in zip(a, c)]
+                q0 = products(s0, s0)
+                s1 = [2.25 * s + (x - 1.5 * q) for s, q, x in zip(s0, q0, products(q0, [0.25 * s for s in s0]))]
+                q1 = products(s1, s1)
+                a = [0.25 * x - 0.75 * (s + r) for s, r, x in zip(s0, s1, products(s0, s1))]
+                s2 = [2.25 * s + (x - 1.5 * q) for s, q, x in zip(s1, q1, products(q1, [0.25 * s for s in s1]))]
+                q2 = products(s2, s2)
+                rest = products(q2, [0.0625 * q - 0.5625 * s for s, q in zip(s2, q2)])
+                c = [1.6875 * q - 2.4375 * s + x for s, q, x in zip(s2, q2, rest)]
+                z = [5.0625 * eye + 2.25 * (x + y) + w for x, y, w in zip(a, c, products(a, c))]
                 root = [v / jnp.sqrt(bound) for v, bound in zip(z, bounds)]
                 half = [jnp.sum(r * g[:, members : members + 1], axis=0, keepdims=True) for r, g in zip(root, raw)]
                 gain = [jnp.sum(r * h, axis=1, keepdims=True) for r, h in zip(root, half)]
@@ -240,18 +272,12 @@
     window = jnp.pad(window, ((0, SUB - 2), (0, tiles * LANES - window.shape[1])))
     window = window.reshape(members + SUB, tiles, LANES).transpose(1, 0, 2)
 
-    tiers = subarea_cutoff_level[:, None]
-    first = (lax.axis_index(MEMBER) * domains).astype(jnp.int32)
-    own_lists = lax.dynamic_slice_in_dim(nearby_readings, first, domains, 0)
-    own_tiers = lax.dynamic_slice_in_dim(tiers, first, domains, 0)
-    mine = block_sums(window, nearby_readings, tiers, members, halo_cells)
-    share = domains // 3
+    first = (lax.axis_index(MEMBER) * domains).astype(jnp.int32).reshape(1)
+    mine, local, decay = block_sums(first, subarea_cutoff_level, window, nearby_readings, members, domains, halo_cells)
     pieces = []
     for r in range(3):
         other = shifted(mine, "space", 1 << r)
-        part = slice(r * share, (r + 1) * share)
-        start = (first + r * share).reshape(1)
-        pieces.append(grams(start, window, own_lists[part], own_tiers[part], members, halo_cells))
+        pieces.append(grams(first, window, local, decay, members, r, 3))
         if r < 2:
             mine = mine + other
     trans_w = roots(mine, other, pieces, members)

time: 151 us -> 143 us (0.947)
  the two profiles are of different devices: /device:TPU:515 before, /device:TPU:513 now
where the time goes in v2:
time: 143 us; the launch traced here: 142 us
  blocking collectives  53.3 us (37%)
  starting transfers between devices  35.4 us (25%)
  Pallas kernels  24.2 us (17%)
  waiting for transfers between devices  18.9 us (13%)
  local copies, waits for them, and re-layouts  8.19 us (6%)
  matrix products  2.04 us (1%)
    all_to_all x1, blocking collectives, per_device(): lax.all_to_all(updated.reshape(groups, held, domains, quantities), MEMBER...  53.3 us
    all_to_all x1, starting transfers between devices, spread_copies(): return lax.all_to_all(copies, axis, split_axis=0, concat_axis=0, tiled=True)  23.7 us
    pallas_call x3, Pallas kernels, grams(): pl.pallas_call(gram_kernel(members, part * own), grid=(1,), in_specs=[sme...  10.5 us
    pallas_call x1, Pallas kernels, roots(): pl.pallas_call(root_kernel(members, len(pieces)), in_specs=[vmem()] * (2...  9.77 us
    all_to_all x1, waiting for transfers between devices, spread_copies(): return lax.all_to_all(copies, axis, split_axis=0, concat_axis=0, tiled=True)  7.7 us
    all_to_all x1, waiting for transfers between devices, per_device(): lax.all_to_all(outgoing, MEMBER, split_axis=0, concat_axis=0, tiled=True)  5.73 us
    ppermute x3, waiting for transfers between devices, shifted(): lax.ppermute(value, axis, [(i, (i + step) % count) for i in range(count)])  4.16 us
    ppermute x1, starting transfers between devices, with_halo(): before = lax.ppermute(value[:, length - width:], axis, up)  4.04 us
  transfers between devices with their start and end apart: 7, of which 6 were waited for; matrix products, arithmetic and copies ran while one was open for 3% of the time, Pallas kernels for 17%

profile of v2, /device:TPU:513, one launch (start us, length us, event | category | flops | bytes accessed | tf_op | source)
XLA Modules:
  0.0 142.2 jit_solution(6616188061014638603)
XLA Ops:
  0.0 1.4 broadcast_in_dim.3
  1.4 23.7 %all-to-all-start = ((bf16[16,5,768]{2,1,0:T(8,128)(2,1)}), bf16[16,5,768]{2,1,0:T(8,128)(2,1)S(1)}, u32[]{:S(2)}, u32[]{:S(2)}) async-start(bf16[16,5,768]{2,1,0:T(8,128)(2,1)} %broadcast_in_dim.3), calls=%async_computation | async-start | bytes 393216 | tf_op jit(solution)/shard_map/all_to_all | solution.py:29
  25.1 2.9 %copy.21 = bf16[16,5,48,256]{3,2,1,0:T(8,128)(2,1)} copy(bf16[16,5,48,256]{3,2,0,1:T(8,128)(2,1)} %bitcast.21) | data formatting | bytes 3932160 | tf_op jit(solution)/shard_map/transpose | solution.py:265
  28.1 7.7 %all-to-all-done = bf16[16,5,768]{2,1,0:T(8,128)(2,1)S(1)} async-done(((bf16[16,5,768]{2,1,0:T(8,128)(2,1)}), bf16[16,5,768]{2,1,0:T(8,128)(2,1)S(1)}, u32[]{:S(2)}, u32[]{:S(2)}) %all-to-all-start) | async-done | bytes 122912 | tf_op jit(solution)/shard_map/all_to_all | solution.py:29
  35.8 3.9 %all-to-all-start.1 = ((bf16[16,5,48,256]{3,2,1,0:T(8,128)(2,1)}), bf16[16,5,48,256]{3,2,1,0:T(8,128)(2,1)S(1)}, u32[]{:S(2)}, u32[]{:S(2)}) async-start(bf16[16,5,48,256]{3,2,1,0:T(8,128)(2,1)} %copy.21), calls=%async_computation.1 | async-start | bytes 3932160 | tf_op jit(solution)/shard_map/all_to_all | solution.py:266
  39.9 1.3 collective-permute-start.1
  41.2 4.0 %collective-permute-start = (bf16[82,320]{1,0:T(8,128)(2,1)S(1)}, bf16[82,320]{1,0:T(8,128)(2,1)S(1)}, u32[]{:S(2)}, u32[]{:S(2)}) collective-permute-start(bf16[82,320]{1,0:T(8,128)(2,1)S(1)} %get-tuple-element.12), channel_id=1, source_target_pairs={{0,1},{1,2},{2,3},{3,4},{4,5},{5,6},{6,7},{8,9},{9,10},{10,11},{11... | collective-permute-start | bytes 157448 | tf_op jit(solution)/shard_map/ppermute | solution.py:41
  45.3 0.4 collective-permute-done.1
  45.7 0.9 collective-permute-done
  46.8 0.7 bitcast_bitcast_fusion.window_ref
  47.5 4.0 %block_sums.1 = (f32[2,128]{1,0:T(2,128)}, s32[48,128]{1,0:T(8,128)}, f32[48,128]{1,0:T(8,128)}) custom-call(s32[1]{0:T(128)} %bitcast.first_ref, s32[768]{0:T(1024)} %tiers_ref.1, bf16[12,88,128]{2,1,0:T(8,128)(2,1)} %bitcast_bitcast_fusion.window_ref, s32[768,128]{1,0:T(8,128)} %lists_ref.1), custom_call_target="tpu_custom_call" | custom-call | flops 10000000 | bytes 1000000 | tf_op jit(solution)/shard_map/block_sums/pallas_call | solution.py:107
  51.6 2.3 %collective-permute-start.2 = (f32[2,128]{1,0:T(2,128)}, f32[2,128]{1,0:T(2,128)S(1)}, u32[]{:S(2)}, u32[]{:S(2)}) collective-permute-start(f32[2,128]{1,0:T(2,128)} %get-tuple-element.8), channel_id=1, source_target_pairs={{0,1},{1,2},{2,3},{3,4},{4,5},{5,6},{6,7},{7,0},{8,9},{9,10},{10,1... | collective-permute-start | bytes 3080 | tf_op jit(solution)/shard_map/ppermute | solution.py:34
  53.8 3.5 %grams.5.refs_2_ = f32[16,80,88]{2,1,0:T(8,128)} custom-call(s32[1]{0:T(128)} %bitcast.first_ref, bf16[12,88,128]{2,1,0:T(8,128)(2,1)} %bitcast_bitcast_fusion.window_ref, s32[48,128]{1,0:T(8,128)} %get-tuple-element.9.local_ref, f32[48,128]{1,0:T(8,128)} %get-tuple-element.10.decay_ref), custom_call_target="tpu_custom_call" | custom-call | flops 960000000 | bytes 640000 | tf_op jit(solution)/shard_map/grams/pallas_call | solution.py:159
  57.5 3.5 %grams.4.refs_1_ = f32[16,80,88]{2,1,0:T(8,128)} custom-call(s32[1]{0:T(128)} %bitcast.first_ref, bf16[12,88,128]{2,1,0:T(8,128)(2,1)} %bitcast_bitcast_fusion.window_ref, s32[48,128]{1,0:T(8,128)} %get-tuple-element.9.local_ref, f32[48,128]{1,0:T(8,128)} %get-tuple-element.10.decay_ref), custom_call_target="tpu_custom_call" | custom-call | flops 960000000 | bytes 640000 | tf_op jit(solution)/shard_map/grams/pallas_call | solution.py:159
  61.0 1.3 collective-permute-done.3
  62.3 3.5 %grams.3.refs_0_ = f32[16,80,88]{2,1,0:T(8,128)} custom-call(s32[1]{0:T(128)} %bitcast.first_ref, bf16[12,88,128]{2,1,0:T(8,128)(2,1)} %bitcast_bitcast_fusion.window_ref, s32[48,128]{1,0:T(8,128)} %get-tuple-element.9.local_ref, f32[48,128]{1,0:T(8,128)} %get-tuple-element.10.decay_ref), custom_call_target="tpu_custom_call" | custom-call | flops 960000000 | bytes 640000 | tf_op jit(solution)/shard_map/grams/pallas_call | solution.py:159
  65.8 2.8 %collective-permute-done.4.other_ref = f32[2,128]{1,0:T(2,128)S(1)} collective-permute-done((f32[2,128]{1,0:T(2,128)S(1)}, f32[2,128]{1,0:T(2,128)S(1)}, u32[]{:S(2)}, u32[]{:S(2)}) %collective-permute-start.4) | collective-permute-done | bytes 1056 | tf_op jit(solution)/shard_map/ppermute | solution.py:34
  68.6 0.6 copy-done.4
  69.2 9.8 %roots.1 = bf16[48,80,80]{2,1,0:T(8,128)(2,1)} custom-call(f32[2,128]{1,0:T(2,128)} %copy-done.2, f32[2,128]{1,0:T(2,128)} %copy-done.4, f32[16,80,88]{2,1,0:T(8,128)} %grams.3.refs_0_, f32[16,80,88]{2,1,0:T(8,128)} %grams.4.refs_1_, f32[16,80,88]{2,1,0:T(8,128)} %grams.5.refs_2_), custom_call_target="tpu_custom_call" | custom-call | flops 2880000000 | bytes 2400000 | tf_op jit(solution)/shard_map/roots/pallas_call | solution.py:239
  79.0 5.7 %all-to-all-done.1 = bf16[16,5,48,256]{3,2,1,0:T(8,128)(2,1)S(1)} async-done(((bf16[16,5,48,256]{3,2,1,0:T(8,128)(2,1)}), bf16[16,5,48,256]{3,2,1,0:T(8,128)(2,1)S(1)}, u32[]{:S(2)}, u32[]{:S(2)}) %all-to-all-start.1) | async-done | bytes 1966112 | tf_op jit(solution)/shard_map/all_to_all | solution.py:266
  84.7 2.0 %convert_bitcast_fusion = bf16[80,48,256]{2,0,1:T(8,128)(2,1)S(1)} fusion(bf16[48,80,80]{2,1,0:T(8,128)(2,1)} %roots.1, bf16[80,48,256]{2,1,0:T(8,128)(2,1)S(1)} %bitcast.18), kind=kOutput, calls=%fused_computation.2 | convolution fusion | flops 158269440 | bytes 4546560 | tf_op jit(solution)/shard_map/inc,nij->jnc/dot_general | solution.py:285
  86.7 0.7 copy.24
  87.4 53.3 %all_to_all.15 = bf16[16,5,48,256]{3,2,1,0:T(8,128)(2,1)S(1)} all-to-all(bf16[16,5,48,256]{3,2,1,0:T(8,128)(2,1)S(1)} %bitcast.19), channel_id=1, replica_groups=mesh['region'=2,'member_0'=8,'member_1'=2,'space'=8] {'member_0','member..., dimensions={0} | all-to-all | bytes 3932160 | tf_op jit(solution)/shard_map/all_to_all | solution.py:286
  140.7 1.5 %copy.25 = bf16[5,16,48,256]{3,2,1,0:T(8,128)(2,1)} copy(bf16[5,16,48,256]{3,2,0,1:T(8,128)(2,1)S(1)} %bitcast.20) | data formatting | bytes 3932160 | tf_op jit(solution)/shard_map/transpose | solution.py:289
  (20 shorter events, 0.5 us)
Async XLA Ops:
  1.4 34.4 %all-to-all-start = ((bf16[16,5,768]{2,1,0:T(8,128)(2,1)}), bf16[16,5,768]{2,1,0:T(8,128)(2,1)S(1)}, u32[]{:S(2)}, u32[]{:S(2)}) async-start(bf16[16,5,768]{2,1,0:T(8,128)(2,1)} %broadcast_in_dim.3), calls=%async_computation | async-start | bytes 393216 | tf_op jit(solution)/shard_map/all_to_all | solution.py:29
  28.1 11.6 %copy-start = (bf16[768]{0:T(1024)(128)(2,1)S(1)}, bf16[768]{0:T(1024)(128)(2,1)}, u32[]{:S(2)}) copy-start(bf16[768]{0:T(1024)(128)(2,1)} %param.8) | copy-start | bytes 4612
  28.1 11.6 %copy-start.1 = (bf16[768]{0:T(1024)(128)(2,1)S(1)}, bf16[768]{0:T(1024)(128)(2,1)}, u32[]{:S(2)}) copy-start(bf16[768]{0:T(1024)(128)(2,1)} %param.9) | copy-start | bytes 4612
  35.8 48.9 %all-to-all-start.1 = ((bf16[16,5,48,256]{3,2,1,0:T(8,128)(2,1)}), bf16[16,5,48,256]{3,2,1,0:T(8,128)(2,1)S(1)}, u32[]{:S(2)}, u32[]{:S(2)}) async-start(bf16[16,5,48,256]{3,2,1,0:T(8,128)(2,1)} %copy.21), calls=%async_computation.1 | async-start | bytes 3932160 | tf_op jit(solution)/shard_map/all_to_all | solution.py:266
  39.9 5.8 %collective-permute-start.1 = (bf16[82,320]{1,0:T(8,128)(2,1)S(1)}, bf16[82,320]{1,0:T(8,128)(2,1)S(1)}, u32[]{:S(2)}, u32[]{:S(2)}) collective-permute-start(bf16[82,320]{1,0:T(8,128)(2,1)S(1)} %get-tuple-element.11), channel_id=1, source_target_pairs={{1,0},{2,1},{3,2},{4,3},{5,4},{6,5},{7,6},{9,8},{10,9},{11,10},{12... | collective-permute-start | bytes 157448 | tf_op jit(solution)/shard_map/ppermute | solution.py:42
  41.2 5.4 %collective-permute-start = (bf16[82,320]{1,0:T(8,128)(2,1)S(1)}, bf16[82,320]{1,0:T(8,128)(2,1)S(1)}, u32[]{:S(2)}, u32[]{:S(2)}) collective-permute-start(bf16[82,320]{1,0:T(8,128)(2,1)S(1)} %get-tuple-element.12), channel_id=1, source_target_pairs={{0,1},{1,2},{2,3},{3,4},{4,5},{5,6},{6,7},{8,9},{9,10},{10,11},{11... | collective-permute-start | bytes 157448 | tf_op jit(solution)/shard_map/ppermute | solution.py:41
  51.6 5.8 %copy-start.3 = (f32[2,128]{1,0:T(2,128)S(1)}, f32[2,128]{1,0:T(2,128)}, u32[]{:S(2)}) copy-start(f32[2,128]{1,0:T(2,128)} %get-tuple-element.8) | copy-start | bytes 3076
  51.6 5.8 %collective-permute-start.2 = (f32[2,128]{1,0:T(2,128)}, f32[2,128]{1,0:T(2,128)S(1)}, u32[]{:S(2)}, u32[]{:S(2)}) collective-permute-start(f32[2,128]{1,0:T(2,128)} %get-tuple-element.8), channel_id=1, source_target_pairs={{0,1},{1,2},{2,3},{3,4},{4,5},{5,6},{6,7},{7,0},{8,9},{9,10},{10,1... | collective-permute-start | bytes 3080 | tf_op jit(solution)/shard_map/ppermute | solution.py:34
  57.3 4.9 %collective-permute-start.3 = (f32[2,128]{1,0:T(2,128)S(1)}, f32[2,128]{1,0:T(2,128)S(1)}, u32[]{:S(2)}, u32[]{:S(2)}) collective-permute-start(f32[2,128]{1,0:T(2,128)S(1)} %add.12), channel_id=1, source_target_pairs={{0,2},{1,3},{2,4},{3,5},{4,6},{5,7},{6,0},{7,1},{8,10},{9,11},{10,... | collective-permute-start | bytes 3080 | tf_op jit(solution)/shard_map/ppermute | solution.py:34
  62.3 6.3 %copy-start.2 = (f32[2,128]{1,0:T(2,128)}, f32[2,128]{1,0:T(2,128)S(1)}, u32[]{:S(2)}) copy-start(f32[2,128]{1,0:T(2,128)S(1)} %add.13.sums_ref) | copy-start | bytes 3076
  62.3 6.3 %collective-permute-start.4 = (f32[2,128]{1,0:T(2,128)S(1)}, f32[2,128]{1,0:T(2,128)S(1)}, u32[]{:S(2)}, u32[]{:S(2)}) collective-permute-start(f32[2,128]{1,0:T(2,128)S(1)} %add.13.sums_ref), channel_id=1, source_target_pairs={{0,4},{1,5},{2,6},{3,7},{4,0},{5,1},{6,2},{7,3},{8,12},{9,13},{10,... | collective-permute-start | bytes 3080 | tf_op jit(solution)/shard_map/ppermute | solution.py:34
  68.6 0.6 copy-start.4

commit v3 on v2

--- a/solution.py
+++ b/solution.py
@@ -261,7 +261,12 @@
     members = held * groups
     domains = patch_cells // groups
 
-    gathered = spread_copies(prior_at_sensors, MEMBER).reshape(members, patch_cells)
+    chunks = patch_cells // LANES
+    dense = prior_at_sensors.reshape(held, chunks, LANES).transpose(1, 0, 2).reshape(-1, LANES)
+    lines = dense.shape[0]
+    dense = jnp.pad(dense, ((0, -lines % (2 * SUB)), (0, 0)))
+    gathered = spread_copies(dense, MEMBER).reshape(groups, -1, LANES)[:, :lines]
+    gathered = gathered.reshape(groups, chunks, held, LANES).transpose(0, 2, 1, 3).reshape(members, patch_cells)
     outgoing = prior_trials.reshape(held, groups, domains, quantities).transpose(1, 0, 2, 3)
     incoming = lax.all_to_all(outgoing, MEMBER, split_axis=0, concat_axis=0, tiled=True)
     incoming = incoming.reshape(members, domains, quantities)

time: 143 us -> 141 us (0.986)
  no operation moved by 1% of the time
where the time goes in v3:
time: 141 us
  blocking collectives  52.8 us (37%)
  starting transfers between devices  35.2 us (25%)
  Pallas kernels  24.2 us (17%)
  waiting for transfers between devices  18.1 us (13%)
  local copies, waits for them, and re-layouts  8.25 us (6%)
  matrix products  2.04 us (1%)
    all_to_all x1, blocking collectives, per_device(): lax.all_to_all(updated.reshape(groups, held, domains, quantities), MEMBER...  52.8 us
    all_to_all x1, starting transfers between devices, spread_copies(): return lax.all_to_all(copies, axis, split_axis=0, concat_axis=0, tiled=True)  23.7 us
    pallas_call x3, Pallas kernels, grams(): pl.pallas_call(gram_kernel(members, part * own), grid=(1,), in_specs=[sme...  10.4 us
    pallas_call x1, Pallas kernels, roots(): pl.pallas_call(root_kernel(members, len(pieces)), in_specs=[vmem()] * (2...  9.77 us
    all_to_all x1, waiting for transfers between devices, per_device(): lax.all_to_all(outgoing, MEMBER, split_axis=0, concat_axis=0, tiled=True)  6.32 us
    all_to_all x1, waiting for transfers between devices, spread_copies(): return lax.all_to_all(copies, axis, split_axis=0, concat_axis=0, tiled=True)  6.31 us
    ppermute x3, waiting for transfers between devices, shifted(): lax.ppermute(value, axis, [(i, (i + step) % count) for i in range(count)])  4.16 us
    ppermute x1, starting transfers between devices, with_halo(): before = lax.ppermute(value[:, length - width:], axis, up)  4.04 us
  transfers between devices with their start and end apart: 7, of which 6 were waited for; matrix products, arithmetic and copies ran while one was open for 3% of the time, Pallas kernels for 17%

profile of v3, /device:TPU:513, one launch (start us, length us, event | category | flops | bytes accessed | tf_op | source)
XLA Modules:
  0.0 140.9 jit_solution(4058851576217111095)
XLA Ops:
  0.0 0.7 reshape.32
  0.7 0.7 broadcast_in_dim.3
  1.4 23.7 %all-to-all-start = ((bf16[16,32,128]{2,1,0:T(8,128)(2,1)}), bf16[16,32,128]{2,1,0:T(8,128)(2,1)S(1)}, u32[]{:S(2)}, u32[]{:S(2)}) async-start(bf16[16,32,128]{2,1,0:T(8,128)(2,1)} %broadcast_in_dim.3), calls=%async_computation | async-start | bytes 262144 | tf_op jit(solution)/shard_map/all_to_all | solution.py:29
  25.1 2.9 %copy.28 = bf16[16,5,48,256]{3,2,1,0:T(8,128)(2,1)} copy(bf16[16,5,48,256]{3,2,0,1:T(8,128)(2,1)} %bitcast.33) | data formatting | bytes 3932160 | tf_op jit(solution)/shard_map/transpose | solution.py:270
  28.1 6.3 %all-to-all-done = bf16[16,32,128]{2,1,0:T(8,128)(2,1)S(1)} async-done(((bf16[16,32,128]{2,1,0:T(8,128)(2,1)}), bf16[16,32,128]{2,1,0:T(8,128)(2,1)S(1)}, u32[]{:S(2)}, u32[]{:S(2)}) %all-to-all-start) | async-done | bytes 131104 | tf_op jit(solution)/shard_map/all_to_all | solution.py:29
  34.4 3.9 %all-to-all-start.1 = ((bf16[16,5,48,256]{3,2,1,0:T(8,128)(2,1)}), bf16[16,5,48,256]{3,2,1,0:T(8,128)(2,1)S(1)}, u32[]{:S(2)}, u32[]{:S(2)}) async-start(bf16[16,5,48,256]{3,2,1,0:T(8,128)(2,1)} %copy.28), calls=%async_computation.1 | async-start | bytes 3932160 | tf_op jit(solution)/shard_map/all_to_all | solution.py:271
  38.6 1.3 collective-permute-start.1
  39.9 4.0 %collective-permute-start = (bf16[82,320]{1,0:T(8,128)(2,1)S(1)}, bf16[82,320]{1,0:T(8,128)(2,1)S(1)}, u32[]{:S(2)}, u32[]{:S(2)}) collective-permute-start(bf16[82,320]{1,0:T(8,128)(2,1)S(1)} %get-tuple-element.12), channel_id=1, source_target_pairs={{0,1},{1,2},{2,3},{3,4},{4,5},{5,6},{6,7},{8,9},{9,10},{10,11},{11... | collective-permute-start | bytes 157448 | tf_op jit(solution)/shard_map/ppermute | solution.py:41
  44.3 1.0 collective-permute-done
  45.5 0.7 bitcast_bitcast_fusion.window_ref
  46.2 4.0 %block_sums.1 = (f32[2,128]{1,0:T(2,128)}, s32[48,128]{1,0:T(8,128)}, f32[48,128]{1,0:T(8,128)}) custom-call(s32[1]{0:T(128)} %bitcast.first_ref, s32[768]{0:T(1024)} %tiers_ref.1, bf16[12,88,128]{2,1,0:T(8,128)(2,1)} %bitcast_bitcast_fusion.window_ref, s32[768,128]{1,0:T(8,128)} %lists_ref.1), custom_call_target="tpu_custom_call" | custom-call | flops 10000000 | bytes 1000000 | tf_op jit(solution)/shard_map/block_sums/pallas_call | solution.py:107
  50.3 2.1 %collective-permute-start.2 = (f32[2,128]{1,0:T(2,128)}, f32[2,128]{1,0:T(2,128)S(1)}, u32[]{:S(2)}, u32[]{:S(2)}) collective-permute-start(f32[2,128]{1,0:T(2,128)} %get-tuple-element.8), channel_id=1, source_target_pairs={{0,1},{1,2},{2,3},{3,4},{4,5},{5,6},{6,7},{7,0},{8,9},{9,10},{10,1... | collective-permute-start | bytes 3080 | tf_op jit(solution)/shard_map/ppermute | solution.py:34
  52.4 3.5 %grams.5.refs_2_ = f32[16,80,88]{2,1,0:T(8,128)} custom-call(s32[1]{0:T(128)} %bitcast.first_ref, bf16[12,88,128]{2,1,0:T(8,128)(2,1)} %bitcast_bitcast_fusion.window_ref, s32[48,128]{1,0:T(8,128)} %get-tuple-element.9.local_ref, f32[48,128]{1,0:T(8,128)} %get-tuple-element.10.decay_ref), custom_call_target="tpu_custom_call" | custom-call | flops 960000000 | bytes 640000 | tf_op jit(solution)/shard_map/grams/pallas_call | solution.py:159
  56.0 3.5 %grams.4.refs_1_ = f32[16,80,88]{2,1,0:T(8,128)} custom-call(s32[1]{0:T(128)} %bitcast.first_ref, bf16[12,88,128]{2,1,0:T(8,128)(2,1)} %bitcast_bitcast_fusion.window_ref, s32[48,128]{1,0:T(8,128)} %get-tuple-element.9.local_ref, f32[48,128]{1,0:T(8,128)} %get-tuple-element.10.decay_ref), custom_call_target="tpu_custom_call" | custom-call | flops 960000000 | bytes 640000 | tf_op jit(solution)/shard_map/grams/pallas_call | solution.py:159
  59.5 1.3 collective-permute-done.3
  60.9 3.5 %grams.3.refs_0_ = f32[16,80,88]{2,1,0:T(8,128)} custom-call(s32[1]{0:T(128)} %bitcast.first_ref, bf16[12,88,128]{2,1,0:T(8,128)(2,1)} %bitcast_bitcast_fusion.window_ref, s32[48,128]{1,0:T(8,128)} %get-tuple-element.9.local_ref, f32[48,128]{1,0:T(8,128)} %get-tuple-element.10.decay_ref), custom_call_target="tpu_custom_call" | custom-call | flops 960000000 | bytes 640000 | tf_op jit(solution)/shard_map/grams/pallas_call | solution.py:159
  64.3 2.8 %collective-permute-done.4.other_ref = f32[2,128]{1,0:T(2,128)S(1)} collective-permute-done((f32[2,128]{1,0:T(2,128)S(1)}, f32[2,128]{1,0:T(2,128)S(1)}, u32[]{:S(2)}, u32[]{:S(2)}) %collective-permute-start.4) | collective-permute-done | bytes 1056 | tf_op jit(solution)/shard_map/ppermute | solution.py:34
  67.2 0.6 copy-done.4
  67.7 9.8 %roots.1 = bf16[48,80,80]{2,1,0:T(8,128)(2,1)} custom-call(f32[2,128]{1,0:T(2,128)} %copy-done.2, f32[2,128]{1,0:T(2,128)} %copy-done.4, f32[16,80,88]{2,1,0:T(8,128)} %grams.3.refs_0_, f32[16,80,88]{2,1,0:T(8,128)} %grams.4.refs_1_, f32[16,80,88]{2,1,0:T(8,128)} %grams.5.refs_2_), custom_call_target="tpu_custom_call" | custom-call | flops 2880000000 | bytes 2400000 | tf_op jit(solution)/shard_map/roots/pallas_call | solution.py:239
  77.5 6.3 %all-to-all-done.1 = bf16[16,5,48,256]{3,2,1,0:T(8,128)(2,1)S(1)} async-done(((bf16[16,5,48,256]{3,2,1,0:T(8,128)(2,1)}), bf16[16,5,48,256]{3,2,1,0:T(8,128)(2,1)S(1)}, u32[]{:S(2)}, u32[]{:S(2)}) %all-to-all-start.1) | async-done | bytes 1966112 | tf_op jit(solution)/shard_map/all_to_all | solution.py:271
  83.8 2.0 %convert_bitcast_fusion = bf16[80,48,256]{2,0,1:T(8,128)(2,1)S(1)} fusion(bf16[48,80,80]{2,1,0:T(8,128)(2,1)} %roots.1, bf16[80,48,256]{2,1,0:T(8,128)(2,1)S(1)} %bitcast.30), kind=kOutput, calls=%fused_computation.2 | convolution fusion | flops 158269440 | bytes 4546560 | tf_op jit(solution)/shard_map/inc,nij->jnc/dot_general | solution.py:290
  85.9 0.7 copy.31
  86.6 52.8 %all_to_all.15 = bf16[16,5,48,256]{3,2,1,0:T(8,128)(2,1)S(1)} all-to-all(bf16[16,5,48,256]{3,2,1,0:T(8,128)(2,1)S(1)} %bitcast.31), channel_id=1, replica_groups=mesh['region'=2,'member_0'=8,'member_1'=2,'space'=8] {'member_0','member..., dimensions={0} | all-to-all | bytes 3932160 | tf_op jit(solution)/shard_map/all_to_all | solution.py:291
  139.4 1.5 %copy.32 = bf16[5,16,48,256]{3,2,1,0:T(8,128)(2,1)} copy(bf16[5,16,48,256]{3,2,0,1:T(8,128)(2,1)S(1)} %bitcast.32) | data formatting | bytes 3932160 | tf_op jit(solution)/shard_map/transpose | solution.py:294
  (24 shorter events, 0.9 us)
Async XLA Ops:
  1.4 33.0 %all-to-all-start = ((bf16[16,32,128]{2,1,0:T(8,128)(2,1)}), bf16[16,32,128]{2,1,0:T(8,128)(2,1)S(1)}, u32[]{:S(2)}, u32[]{:S(2)}) async-start(bf16[16,32,128]{2,1,0:T(8,128)(2,1)} %broadcast_in_dim.3), calls=%async_computation | async-start | bytes 262144 | tf_op jit(solution)/shard_map/all_to_all | solution.py:29
  28.1 10.2 %copy-start = (bf16[768]{0:T(1024)(128)(2,1)S(1)}, bf16[768]{0:T(1024)(128)(2,1)}, u32[]{:S(2)}) copy-start(bf16[768]{0:T(1024)(128)(2,1)} %param.8) | copy-start | bytes 4612
  28.1 10.2 %copy-start.1 = (bf16[768]{0:T(1024)(128)(2,1)S(1)}, bf16[768]{0:T(1024)(128)(2,1)}, u32[]{:S(2)}) copy-start(bf16[768]{0:T(1024)(128)(2,1)} %param.9) | copy-start | bytes 4612
  34.4 49.4 %all-to-all-start.1 = ((bf16[16,5,48,256]{3,2,1,0:T(8,128)(2,1)}), bf16[16,5,48,256]{3,2,1,0:T(8,128)(2,1)S(1)}, u32[]{:S(2)}, u32[]{:S(2)}) async-start(bf16[16,5,48,256]{3,2,1,0:T(8,128)(2,1)} %copy.28), calls=%async_computation.1 | async-start | bytes 3932160 | tf_op jit(solution)/shard_map/all_to_all | solution.py:271
  38.6 5.7 %collective-permute-start.1 = (bf16[82,320]{1,0:T(8,128)(2,1)S(1)}, bf16[82,320]{1,0:T(8,128)(2,1)S(1)}, u32[]{:S(2)}, u32[]{:S(2)}) collective-permute-start(bf16[82,320]{1,0:T(8,128)(2,1)S(1)} %get-tuple-element.11), channel_id=1, source_target_pairs={{1,0},{2,1},{3,2},{4,3},{5,4},{6,5},{7,6},{9,8},{10,9},{11,10},{12... | collective-permute-start | bytes 157448 | tf_op jit(solution)/shard_map/ppermute | solution.py:42
  39.9 5.4 %collective-permute-start = (bf16[82,320]{1,0:T(8,128)(2,1)S(1)}, bf16[82,320]{1,0:T(8,128)(2,1)S(1)}, u32[]{:S(2)}, u32[]{:S(2)}) collective-permute-start(bf16[82,320]{1,0:T(8,128)(2,1)S(1)} %get-tuple-element.12), channel_id=1, source_target_pairs={{0,1},{1,2},{2,3},{3,4},{4,5},{5,6},{6,7},{8,9},{9,10},{10,11},{11... | collective-permute-start | bytes 157448 | tf_op jit(solution)/shard_map/ppermute | solution.py:41
  50.2 5.6 %copy-start.3 = (f32[2,128]{1,0:T(2,128)S(1)}, f32[2,128]{1,0:T(2,128)}, u32[]{:S(2)}) copy-start(f32[2,128]{1,0:T(2,128)} %get-tuple-element.8) | copy-start | bytes 3076
  50.3 5.6 %collective-permute-start.2 = (f32[2,128]{1,0:T(2,128)}, f32[2,128]{1,0:T(2,128)S(1)}, u32[]{:S(2)}, u32[]{:S(2)}) collective-permute-start(f32[2,128]{1,0:T(2,128)} %get-tuple-element.8), channel_id=1, source_target_pairs={{0,1},{1,2},{2,3},{3,4},{4,5},{5,6},{6,7},{7,0},{8,9},{9,10},{10,1... | collective-permute-start | bytes 3080 | tf_op jit(solution)/shard_map/ppermute | solution.py:34
  55.9 4.9 %collective-permute-start.3 = (f32[2,128]{1,0:T(2,128)S(1)}, f32[2,128]{1,0:T(2,128)S(1)}, u32[]{:S(2)}, u32[]{:S(2)}) collective-permute-start(f32[2,128]{1,0:T(2,128)S(1)} %add.14), channel_id=1, source_target_pairs={{0,2},{1,3},{2,4},{3,5},{4,6},{5,7},{6,0},{7,1},{8,10},{9,11},{10,... | collective-permute-start | bytes 3080 | tf_op jit(solution)/shard_map/ppermute | solution.py:34
  60.8 6.3 %copy-start.2 = (f32[2,128]{1,0:T(2,128)}, f32[2,128]{1,0:T(2,128)S(1)}, u32[]{:S(2)}) copy-start(f32[2,128]{1,0:T(2,128)S(1)} %add.15.sums_ref) | copy-start | bytes 3076
  60.8 6.3 %collective-permute-start.4 = (f32[2,128]{1,0:T(2,128)S(1)}, f32[2,128]{1,0:T(2,128)S(1)}, u32[]{:S(2)}, u32[]{:S(2)}) collective-permute-start(f32[2,128]{1,0:T(2,128)S(1)} %add.15.sums_ref), channel_id=1, source_target_pairs={{0,4},{1,5},{2,6},{3,7},{4,0},{5,1},{6,2},{7,3},{8,12},{9,13},{10,... | collective-permute-start | bytes 3080 | tf_op jit(solution)/shard_map/ppermute | solution.py:34
  67.2 0.6 copy-start.4

commit v4 on v3

--- a/solution.py
+++ b/solution.py
@@ -12,6 +12,7 @@
 SUB = 8
 SPAN = 6
 BATCH = 16
+LATE = 6
 f32, bf16 = jnp.float32, jnp.bfloat16
 NT = (((1,), (1,)), ((), ()))
 
@@ -191,8 +192,9 @@
 
 
 def root_kernel(members, parts):
-    def kernel(sums_ref, other_ref, *refs):
+    def kernel(sums_ref, other_ref, order_ref, *refs):
         gram_refs, trans_ref = refs[:parts], refs[parts]
+        order = order_ref[...]
         total = sums_ref[...] + other_ref[...]
         ridge = jnp.sum(total[1:2], axis=1, keepdims=True) / jnp.sum(total[0:1], axis=1, keepdims=True)
         row = lax.broadcasted_iota(jnp.int32, (members, members), 0)
@@ -225,7 +227,8 @@
                 for n, r, g in zip(at, root, gain):
                     full = r * ((members - 1.0) ** 0.5) + g
                     full = full - (jnp.sum(full, axis=0, keepdims=True) - 1.0) * (1.0 / members)
-                    trans_ref[offset + n] = full.astype(bf16)
+                    turned = jnp.dot(full.astype(bf16), order, preferred_element_type=f32)
+                    trans_ref[offset + n] = turned.astype(bf16)
                 return unused
 
             lax.fori_loop(0, own // BATCH, block, 0)
@@ -234,16 +237,62 @@
     return kernel
 
 
-def roots(mine, other, pieces, members):
+def roots(mine, other, order, pieces, members):
     own = sum(p.shape[0] for p in pieces)
     return pl.pallas_call(
         root_kernel(members, len(pieces)),
-        in_specs=[vmem()] * (2 + len(pieces)),
+        in_specs=[vmem()] * (3 + len(pieces)),
         out_specs=vmem(),
         out_shape=jax.ShapeDtypeStruct((own, members, members), bf16),
         cost_estimate=pl.CostEstimate(flops=own * 60_000_000, bytes_accessed=own * 50_000, transcendentals=0),
         name="roots",
-    )(mine, other, *pieces)
+    )(mine, other, order, *pieces)
+
+
+def place_kernel(skip, count):
+    def kernel(starts_ref, *refs):
+        block_refs, (out_ref, sems) = refs[:count], refs[-2:]
+        width = block_refs[0].shape[1]
+        copies = []
+        for k, ref in enumerate(block_refs):
+            columns = pl.ds(pl.multiple_of(starts_ref[skip + k], SUB), width)
+            copies.append(pltpu.make_async_copy(ref, out_ref.at[:, columns, :], sems.at[k]))
+            copies[-1].start()
+        for copy in copies:
+            copy.wait()
+
+    return kernel
+
+
+def place(starts, blocks, skip, size, into=()):
+    held, _, quantities = blocks[0].shape
+    anywhere = pl.BlockSpec(memory_space=pl.ANY)
+    count = len(blocks)
+    return pl.pallas_call(
+        place_kernel(skip, count),
+        in_specs=[smem()] + [vmem()] * count + [anywhere] * len(into),
+        out_specs=anywhere,
+        out_shape=jax.ShapeDtypeStruct((held, size, quantities), blocks[0].dtype),
+        scratch_shapes=[pltpu.SemaphoreType.DMA((count,))],
+        input_output_aliases={1 + count: 0} if into else {},
+        cost_estimate=pl.CostEstimate(flops=1_000_000, bytes_accessed=count * 300_000, transcendentals=0),
+        name="place",
+    )(starts, *blocks, *into)
+
+
+def routes(chips):
+    steps = []
+    for far in range(chips // 2, 0, -1):
+        steps += [far] if 2 * far == chips else [far, -far]
+    return [(0, 0)] + [(step, flip) for step in steps for flip in (0, 1)] + [(0, 1)]
+
+
+def sent(value, step, flip):
+    chips = lax.axis_size(MEMBER[0])
+    pairs = [
+        (2 * chip + core, 2 * ((chip + step) % chips) + (core ^ flip)) for chip in range(chips) for core in (0, 1)
+    ]
+    return lax.ppermute(value, MEMBER, pairs)
 
 
 def per_device(
@@ -285,13 +334,26 @@
         pieces.append(grams(first, window, local, decay, members, r, 3))
         if r < 2:
             mine = mine + other
-    trans_w = roots(mine, other, pieces, members)
+    row, core = (lax.axis_index(name) for name in MEMBER)
+    chips = lax.axis_size(MEMBER[0])
+    paths = routes(chips)
+    steps, flips = (jnp.array(values, jnp.int32) for values in zip(*paths))
+    target = 2 * lax.rem(row + steps + chips, chips) + lax.rem(core + flips, 2)
+    source = 2 * lax.rem(row - steps + chips, chips) + lax.rem(core + flips, 2)
+    member = jnp.arange(members, dtype=jnp.int32)
+    wanted = (target[:, None] * held + jnp.arange(held, dtype=jnp.int32)[None]).reshape(members)
+    order = (member[:, None] == wanted[None]).astype(bf16)
+    trans_w = roots(mine, other, order, pieces, members)
 
     updated = jnp.einsum("inc,nij->jnc", incoming, trans_w, preferred_element_type=f32).astype(bf16)
-    returned = lax.all_to_all(
-        updated.reshape(groups, held, domains, quantities), MEMBER, split_axis=0, concat_axis=0, tiled=True
-    )
-    return returned.transpose(1, 0, 2, 3).reshape(held, patch_cells, quantities)
+    slots = updated.reshape(groups, held, domains, quantities)
+    arrived = [slots[0]]
+    for k, (step, flip) in enumerate(paths[1:], 1):
+        arrived.append(sent(slots[k], step, flip))
+    starts = source * domains
+    early = len(arrived) - LATE
+    result = place(starts, arrived[:early], 0, patch_cells)
+    return place(starts, arrived[early:], early, patch_cells, (result,))
 
 
 def solution(mesh):

time: 141 us -> 146 us (1.035)
  blocking collectives: 52.8 us -> 0 us
  starting transfers between devices: 35.2 us -> 66.3 us
  waiting for transfers between devices: 18.1 us -> 37.7 us
  Pallas kernels: 24.2 us -> 29 us
    all_to_all x1 -> x0, blocking collectives: 52.8 us -> none  [per_device(): lax.all_to_all(updated.reshape(groups, held, domains, quantities), MEMBER...]
    ppermute x0 -> x15, starting transfers between devices: none -> 31.1 us  [sent(): return lax.ppermute(value, MEMBER, pairs)]
    ppermute x0 -> x15, waiting for transfers between devices: none -> 20.6 us  [sent(): return lax.ppermute(value, MEMBER, pairs)]
    pallas_call x1 -> x3, Pallas kernels: 9.77 us -> 14.5 us  [the longest x1 9.91 us: roots(): pl.pallas_call(root_kernel(members, len(pieces)), in_specs=[vmem()] * (3...]
  transfers between devices with their start and end apart: 7 -> 22, of which waited for: 6 -> 11; matrix products, arithmetic and copies ran while one was open for 3% -> 4% of each run, Pallas kernels for 17% -> 19%
where the time goes in v4:
time: 146 us; the launch traced here: 145 us
  starting transfers between devices  66.3 us (45%)
  waiting for transfers between devices  37.7 us (26%)
  Pallas kernels  29 us (20%)
  local copies, waits for them, and re-layouts  8.34 us (6%)
  matrix products  2.04 us (1%)
    ppermute x15, starting transfers between devices, sent(): return lax.ppermute(value, MEMBER, pairs)  31.1 us
    all_to_all x1, starting transfers between devices, spread_copies(): return lax.all_to_all(copies, axis, split_axis=0, concat_axis=0, tiled=True)  23.7 us
    ppermute x15, waiting for transfers between devices, sent(): return lax.ppermute(value, MEMBER, pairs)  20.6 us
    pallas_call x3, Pallas kernels, grams(): pl.pallas_call(gram_kernel(members, part * own), grid=(1,), in_specs=[sme...  10.5 us
    pallas_call x1, Pallas kernels, roots(): pl.pallas_call(root_kernel(members, len(pieces)), in_specs=[vmem()] * (3...  9.91 us
    all_to_all x1, waiting for transfers between devices, spread_copies(): return lax.all_to_all(copies, axis, split_axis=0, concat_axis=0, tiled=True)  6.3 us
    all_to_all x1, waiting for transfers between devices, per_device(): lax.all_to_all(outgoing, MEMBER, split_axis=0, concat_axis=0, tiled=True)  5.97 us
    pallas_call x2, Pallas kernels, place(): pl.pallas_call(place_kernel(skip, count), in_specs=[smem()] + [vmem()] *...  4.58 us
  transfers between devices with their start and end apart: 22, of which 11 were waited for; matrix products, arithmetic and copies ran while one was open for 4% of the time, Pallas kernels for 19%

profile of v4, /device:TPU:513, one launch (start us, length us, event | category | flops | bytes accessed | tf_op | source)
XLA Modules:
  0.0 145.2 jit_solution(4696338005257464015)
XLA Ops:
  1.4 23.7 %all-to-all-start = ((bf16[16,32,128]{2,1,0:T(8,128)(2,1)}), bf16[16,32,128]{2,1,0:T(8,128)(2,1)S(1)}, u32[]{:S(2)}, u32[]{:S(2)}) async-start(bf16[16,32,128]{2,1,0:T(8,128)(2,1)} %broadcast_in_dim.2), calls=%async_computation | async-start | bytes 262144 | tf_op jit(solution)/shard_map/all_to_all | solution.py:30
  25.1 2.9 %copy.30 = bf16[16,5,48,256]{3,2,1,0:T(8,128)(2,1)} copy(bf16[16,5,48,256]{3,2,0,1:T(8,128)(2,1)} %bitcast.30) | data formatting | bytes 3932160 | tf_op jit(solution)/shard_map/transpose | solution.py:319
  28.1 6.3 %all-to-all-done = bf16[16,32,128]{2,1,0:T(8,128)(2,1)S(1)} async-done(((bf16[16,32,128]{2,1,0:T(8,128)(2,1)}), bf16[16,32,128]{2,1,0:T(8,128)(2,1)S(1)}, u32[]{:S(2)}, u32[]{:S(2)}) %all-to-all-start) | async-done | bytes 131104 | tf_op jit(solution)/shard_map/all_to_all | solution.py:30
  34.4 3.9 %all-to-all-start.1 = ((bf16[16,5,48,256]{3,2,1,0:T(8,128)(2,1)}), bf16[16,5,48,256]{3,2,1,0:T(8,128)(2,1)S(1)}, u32[]{:S(2)}, u32[]{:S(2)}) async-start(bf16[16,5,48,256]{3,2,1,0:T(8,128)(2,1)} %copy.30), calls=%async_computation.1 | async-start | bytes 3932160 | tf_op jit(solution)/shard_map/all_to_all | solution.py:320
  40.1 4.0 %collective-permute-start = (bf16[82,320]{1,0:T(8,128)(2,1)S(1)}, bf16[82,320]{1,0:T(8,128)(2,1)S(1)}, u32[]{:S(2)}, u32[]{:S(2)}) collective-permute-start(bf16[82,320]{1,0:T(8,128)(2,1)S(1)} %get-tuple-element.30), channel_id=1, source_target_pairs={{0,1},{1,2},{2,3},{3,4},{4,5},{5,6},{6,7},{8,9},{9,10},{10,11},{11... | collective-permute-start | bytes 157448 | tf_op jit(solution)/shard_map/ppermute | solution.py:42
  46.4 4.0 %block_sums.1 = (f32[2,128]{1,0:T(2,128)}, s32[48,128]{1,0:T(8,128)}, f32[48,128]{1,0:T(8,128)}) custom-call(s32[1]{0:T(128)} %bitcast.first_ref, s32[768]{0:T(1024)} %tiers_ref.1, bf16[12,88,128]{2,1,0:T(8,128)(2,1)} %bitcast_bitcast_fusion.window_ref, s32[768,128]{1,0:T(8,128)} %lists_ref.1), custom_call_target="tpu_custom_call" | custom-call | flops 10000000 | bytes 1000000 | tf_op jit(solution)/shard_map/block_sums/pallas_call | solution.py:108
  52.6 3.5 %grams.5.refs_2_ = f32[16,80,88]{2,1,0:T(8,128)} custom-call(s32[1]{0:T(128)} %bitcast.first_ref, bf16[12,88,128]{2,1,0:T(8,128)(2,1)} %bitcast_bitcast_fusion.window_ref, s32[48,128]{1,0:T(8,128)} %get-tuple-element.9.local_ref, f32[48,128]{1,0:T(8,128)} %get-tuple-element.10.decay_ref), custom_call_target="tpu_custom_call" | custom-call | flops 960000000 | bytes 640000 | tf_op jit(solution)/shard_map/grams/pallas_call | solution.py:160
  56.2 3.5 %grams.4.refs_1_ = f32[16,80,88]{2,1,0:T(8,128)} custom-call(s32[1]{0:T(128)} %bitcast.first_ref, bf16[12,88,128]{2,1,0:T(8,128)(2,1)} %bitcast_bitcast_fusion.window_ref, s32[48,128]{1,0:T(8,128)} %get-tuple-element.9.local_ref, f32[48,128]{1,0:T(8,128)} %get-tuple-element.10.decay_ref), custom_call_target="tpu_custom_call" | custom-call | flops 960000000 | bytes 640000 | tf_op jit(solution)/shard_map/grams/pallas_call | solution.py:160
  61.0 3.5 %grams.3.refs_0_ = f32[16,80,88]{2,1,0:T(8,128)} custom-call(s32[1]{0:T(128)} %bitcast.first_ref, bf16[12,88,128]{2,1,0:T(8,128)(2,1)} %bitcast_bitcast_fusion.window_ref, s32[48,128]{1,0:T(8,128)} %get-tuple-element.9.local_ref, f32[48,128]{1,0:T(8,128)} %get-tuple-element.10.decay_ref), custom_call_target="tpu_custom_call" | custom-call | flops 960000000 | bytes 640000 | tf_op jit(solution)/shard_map/grams/pallas_call | solution.py:160
  64.5 2.8 %collective-permute-done.4.other_ref = f32[2,128]{1,0:T(2,128)S(1)} collective-permute-done((f32[2,128]{1,0:T(2,128)S(1)}, f32[2,128]{1,0:T(2,128)S(1)}, u32[]{:S(2)}, u32[]{:S(2)}) %collective-permute-start.4) | collective-permute-done | bytes 1056 | tf_op jit(solution)/shard_map/ppermute | solution.py:35
  67.9 9.9 %roots.1 = bf16[48,80,80]{2,1,0:T(8,128)(2,1)} custom-call(f32[2,128]{1,0:T(2,128)} %copy-done.17, f32[2,128]{1,0:T(2,128)} %copy-done.22, bf16[80,80]{1,0:T(8,128)(2,1)} %fusion.3.order_ref, f32[16,80,88]{2,1,0:T(8,128)} %grams.3.refs_0_, f32[16,80,88]{2,1,0:T(8,128)} %grams.4.refs_1_, f32[16,80,88]{2,1,0:T(8,128)} %grams.5.refs_2_), custom_call_target="tpu_custom_call" | custom-call | flops 2880000000 | bytes 2400000 | tf_op jit(solution)/shard_map/roots/pallas_call | solution.py:242
  77.9 6.0 %all-to-all-done.1 = bf16[16,5,48,256]{3,2,1,0:T(8,128)(2,1)S(1)} async-done(((bf16[16,5,48,256]{3,2,1,0:T(8,128)(2,1)}), bf16[16,5,48,256]{3,2,1,0:T(8,128)(2,1)S(1)}, u32[]{:S(2)}, u32[]{:S(2)}) %all-to-all-start.1) | async-done | bytes 1966112 | tf_op jit(solution)/shard_map/all_to_all | solution.py:320
  92.0 2.3 %collective-permute-start.16 = (bf16[5,48,256]{2,1,0:T(8,128)(2,1)S(1)}, bf16[5,48,256]{2,1,0:T(8,128)(2,1)S(1)}, u32[]{:S(2)}, u32[]{:S(2)}) collective-permute-start(bf16[5,48,256]{2,1,0:T(8,128)(2,1)S(1)} %get-tuple-element.16), channel_id=1, source_target_pairs={{0,88},{8,80},{16,104},{24,96},{32,120},{40,112},{48,8},{56,0},{64... | collective-permute-start | bytes 368648 | tf_op jit(solution)/shard_map/ppermute | solution.py:295
  94.3 2.5 %collective-permute-start.15 = (bf16[5,48,256]{2,1,0:T(8,128)(2,1)S(1)}, bf16[5,48,256]{2,1,0:T(8,128)(2,1)S(1)}, u32[]{:S(2)}, u32[]{:S(2)}) collective-permute-start(bf16[5,48,256]{2,1,0:T(8,128)(2,1)S(1)} %get-tuple-element.17), channel_id=1, source_target_pairs={{0,80},{8,88},{16,96},{24,104},{32,112},{40,120},{48,0},{56,8},{64... | collective-permute-start | bytes 368648 | tf_op jit(solution)/shard_map/ppermute | solution.py:295
  96.8 3.4 %collective-permute-start.14 = (bf16[5,48,256]{2,1,0:T(8,128)(2,1)S(1)}, bf16[5,48,256]{2,1,0:T(8,128)(2,1)S(1)}, u32[]{:S(2)}, u32[]{:S(2)}) collective-permute-start(bf16[5,48,256]{2,1,0:T(8,128)(2,1)S(1)} %get-tuple-element.18), channel_id=1, source_target_pairs={{0,56},{8,48},{16,72},{24,64},{32,88},{40,80},{48,104},{56,96},{64... | collective-permute-start | bytes 368648 | tf_op jit(solution)/shard_map/ppermute | solution.py:295
  102.3 3.9 %collective-permute-start.12 = (bf16[5,48,256]{2,1,0:T(8,128)(2,1)S(1)}, bf16[5,48,256]{2,1,0:T(8,128)(2,1)S(1)}, u32[]{:S(2)}, u32[]{:S(2)}) collective-permute-start(bf16[5,48,256]{2,1,0:T(8,128)(2,1)S(1)} %get-tuple-element.20), channel_id=1, source_target_pairs={{0,72},{8,64},{16,88},{24,80},{32,104},{40,96},{48,120},{56,112},{... | collective-permute-start | bytes 368648 | tf_op jit(solution)/shard_map/ppermute | solution.py:295
  106.2 2.3 %collective-permute-start.11 = (bf16[5,48,256]{2,1,0:T(8,128)(2,1)S(1)}, bf16[5,48,256]{2,1,0:T(8,128)(2,1)S(1)}, u32[]{:S(2)}, u32[]{:S(2)}) collective-permute-start(bf16[5,48,256]{2,1,0:T(8,128)(2,1)S(1)} %get-tuple-element.21), channel_id=1, source_target_pairs={{0,64},{8,72},{16,80},{24,88},{32,96},{40,104},{48,112},{56,120},{... | collective-permute-start | bytes 368648 | tf_op jit(solution)/shard_map/ppermute | solution.py:295
  108.5 3.1 %collective-permute-done.15.refs_5_ = bf16[5,48,256]{2,1,0:T(8,128)(2,1)S(1)} collective-permute-done((bf16[5,48,256]{2,1,0:T(8,128)(2,1)S(1)}, bf16[5,48,256]{2,1,0:T(8,128)(2,1)S(1)}, u32[]{:S(2)}, u32[]{:S(2)}) %collective-permute-start.15) | collective-permute-done | bytes 122912 | tf_op jit(solution)/shard_map/ppermute | solution.py:295
  112.6 5.9 %collective-permute-start.9 = (bf16[5,48,256]{2,1,0:T(8,128)(2,1)S(1)}, bf16[5,48,256]{2,1,0:T(8,128)(2,1)S(1)}, u32[]{:S(2)}, u32[]{:S(2)}) collective-permute-start(bf16[5,48,256]{2,1,0:T(8,128)(2,1)S(1)} %get-tuple-element.24), channel_id=1, source_target_pairs={{0,120},{8,112},{16,8},{24,0},{32,24},{40,16},{48,40},{56,32},{64,... | collective-permute-start | bytes 368648 | tf_op jit(solution)/shard_map/ppermute | solution.py:295
  120.2 7.4 %collective-permute-done.12.refs_2_ = bf16[5,48,256]{2,1,0:T(8,128)(2,1)S(1)} collective-permute-done((bf16[5,48,256]{2,1,0:T(8,128)(2,1)S(1)}, bf16[5,48,256]{2,1,0:T(8,128)(2,1)S(1)}, u32[]{:S(2)}, u32[]{:S(2)}) %collective-permute-start.12) | collective-permute-done | bytes 122912 | tf_op jit(solution)/shard_map/ppermute | solution.py:295
  127.6 5.7 %collective-permute-done.11.refs_1_ = bf16[5,48,256]{2,1,0:T(8,128)(2,1)S(1)} collective-permute-done((bf16[5,48,256]{2,1,0:T(8,128)(2,1)S(1)}, bf16[5,48,256]{2,1,0:T(8,128)(2,1)S(1)}, u32[]{:S(2)}, u32[]{:S(2)}) %collective-permute-start.11) | collective-permute-done | bytes 122912 | tf_op jit(solution)/shard_map/ppermute | solution.py:295
  133.3 3.1 %collective-permute-start.5 = (bf16[5,48,256]{2,1,0:T(8,128)(2,1)S(1)}, bf16[5,48,256]{2,1,0:T(8,128)(2,1)S(1)}, u32[]{:S(2)}, u32[]{:S(2)}) collective-permute-start(bf16[5,48,256]{2,1,0:T(8,128)(2,1)S(1)} %get-tuple-element.28), channel_id=1, source_target_pairs={{0,104},{8,96},{16,120},{24,112},{32,8},{40,0},{48,24},{56,16},{64... | collective-permute-start | bytes 368648 | tf_op jit(solution)/shard_map/ppermute | solution.py:295
  137.1 2.5 %place.2.refs_6_ = bf16[5,768,256]{2,1,0:T(8,128)(2,1)} custom-call(s32[16]{0:T(128)} %fusion.11.starts_ref, bf16[5,48,256]{2,1,0:T(8,128)(2,1)} %get-tuple-element.22.refs_0_, bf16[5,48,256]{2,1,0:T(8,128)(2,1)} %copy-done.14, bf16[5,48,256]{2,1,0:T(8,128)(2,1)} %copy-done.13, bf16[5,48,256]{2,1,0:T(8,128)(2,1)} %copy-done.12, ...), custom_call_target="tpu_custom_call" | custom-call | flops 1000000 | bytes 3000000 | tf_op jit(solution)/shard_map/place/pallas_call | solution.py:271
  139.9 2.3 %collective-permute-done.5.refs_0_ = bf16[5,48,256]{2,1,0:T(8,128)(2,1)S(1)} collective-permute-done((bf16[5,48,256]{2,1,0:T(8,128)(2,1)S(1)}, bf16[5,48,256]{2,1,0:T(8,128)(2,1)S(1)}, u32[]{:S(2)}, u32[]{:S(2)}) %collective-permute-start.5) | collective-permute-done | bytes 122912 | tf_op jit(solution)/shard_map/ppermute | solution.py:295
  (96 shorter events, 26.2 us)
Async XLA Ops:
  1.4 33.0 %all-to-all-start = ((bf16[16,32,128]{2,1,0:T(8,128)(2,1)}), bf16[16,32,128]{2,1,0:T(8,128)(2,1)S(1)}, u32[]{:S(2)}, u32[]{:S(2)}) async-start(bf16[16,32,128]{2,1,0:T(8,128)(2,1)} %broadcast_in_dim.2), calls=%async_computation | async-start | bytes 262144 | tf_op jit(solution)/shard_map/all_to_all | solution.py:30
  34.4 49.4 %all-to-all-start.1 = ((bf16[16,5,48,256]{3,2,1,0:T(8,128)(2,1)}), bf16[16,5,48,256]{3,2,1,0:T(8,128)(2,1)S(1)}, u32[]{:S(2)}, u32[]{:S(2)}) async-start(bf16[16,5,48,256]{3,2,1,0:T(8,128)(2,1)} %copy.30), calls=%async_computation.1 | async-start | bytes 3932160 | tf_op jit(solution)/shard_map/all_to_all | solution.py:320
  38.8 6.0 %collective-permute-start.1 = (bf16[82,320]{1,0:T(8,128)(2,1)S(1)}, bf16[82,320]{1,0:T(8,128)(2,1)S(1)}, u32[]{:S(2)}, u32[]{:S(2)}) collective-permute-start(bf16[82,320]{1,0:T(8,128)(2,1)S(1)} %get-tuple-element.29), channel_id=1, source_target_pairs={{1,0},{2,1},{3,2},{4,3},{5,4},{6,5},{7,6},{9,8},{10,9},{11,10},{12... | collective-permute-start | bytes 157448 | tf_op jit(solution)/shard_map/ppermute | solution.py:43
  40.1 5.4 %collective-permute-start = (bf16[82,320]{1,0:T(8,128)(2,1)S(1)}, bf16[82,320]{1,0:T(8,128)(2,1)S(1)}, u32[]{:S(2)}, u32[]{:S(2)}) collective-permute-start(bf16[82,320]{1,0:T(8,128)(2,1)S(1)} %get-tuple-element.30), channel_id=1, source_target_pairs={{0,1},{1,2},{2,3},{3,4},{4,5},{5,6},{6,7},{8,9},{9,10},{10,11},{11... | collective-permute-start | bytes 157448 | tf_op jit(solution)/shard_map/ppermute | solution.py:42
  50.4 5.6 %collective-permute-start.2 = (f32[2,128]{1,0:T(2,128)}, f32[2,128]{1,0:T(2,128)S(1)}, u32[]{:S(2)}, u32[]{:S(2)}) collective-permute-start(f32[2,128]{1,0:T(2,128)} %get-tuple-element.8), channel_id=1, source_target_pairs={{0,1},{1,2},{2,3},{3,4},{4,5},{5,6},{6,7},{7,0},{8,9},{9,10},{10,1... | collective-permute-start | bytes 3080 | tf_op jit(solution)/shard_map/ppermute | solution.py:35
  56.1 4.9 %collective-permute-start.3 = (f32[2,128]{1,0:T(2,128)S(1)}, f32[2,128]{1,0:T(2,128)S(1)}, u32[]{:S(2)}, u32[]{:S(2)}) collective-permute-start(f32[2,128]{1,0:T(2,128)S(1)} %add.62), channel_id=1, source_target_pairs={{0,2},{1,3},{2,4},{3,5},{4,6},{5,7},{6,0},{7,1},{8,10},{9,11},{10,... | collective-permute-start | bytes 3080 | tf_op jit(solution)/shard_map/ppermute | solution.py:35
  61.0 6.3 %collective-permute-start.4 = (f32[2,128]{1,0:T(2,128)S(1)}, f32[2,128]{1,0:T(2,128)S(1)}, u32[]{:S(2)}, u32[]{:S(2)}) collective-permute-start(f32[2,128]{1,0:T(2,128)S(1)} %add.63.sums_ref), channel_id=1, source_target_pairs={{0,4},{1,5},{2,6},{3,7},{4,0},{5,1},{6,2},{7,3},{8,12},{9,13},{10,... | collective-permute-start | bytes 3080 | tf_op jit(solution)/shard_map/ppermute | solution.py:35
  86.5 49.9 %copy-start.19 = (s32[16]{0:T(128)S(1)}, s32[16]{0:T(128)}, u32[]{:S(2)}) copy-start(s32[16]{0:T(128)} %constant.45) | copy-start | bytes 196
  87.3 9.5 %collective-permute-start.19 = (bf16[5,48,256]{2,1,0:T(8,128)(2,1)S(1)}, bf16[5,48,256]{2,1,0:T(8,128)(2,1)S(1)}, u32[]{:S(2)}, u32[]{:S(2)}) collective-permute-start(bf16[5,48,256]{2,1,0:T(8,128)(2,1)S(1)} %get-tuple-element.13), channel_id=1, source_target_pairs={{0,96},{8,104},{16,112},{24,120},{32,0},{40,8},{48,16},{56,24},{64... | collective-permute-start | bytes 368648 | tf_op jit(solution)/shard_map/ppermute | solution.py:295
  89.0 11.3 %collective-permute-start.18 = (bf16[5,48,256]{2,1,0:T(8,128)(2,1)S(1)}, bf16[5,48,256]{2,1,0:T(8,128)(2,1)S(1)}, u32[]{:S(2)}, u32[]{:S(2)}) collective-permute-start(bf16[5,48,256]{2,1,0:T(8,128)(2,1)S(1)} %get-tuple-element.14), channel_id=1, source_target_pairs={{0,40},{8,32},{16,56},{24,48},{32,72},{40,64},{48,88},{56,80},{64,... | collective-permute-start | bytes 368648 | tf_op jit(solution)/shard_map/ppermute | solution.py:295
  90.4 11.9 %collective-permute-start.17 = (bf16[5,48,256]{2,1,0:T(8,128)(2,1)S(1)}, bf16[5,48,256]{2,1,0:T(8,128)(2,1)S(1)}, u32[]{:S(2)}, u32[]{:S(2)}) collective-permute-start(bf16[5,48,256]{2,1,0:T(8,128)(2,1)S(1)} %get-tuple-element.15), channel_id=1, source_target_pairs={{0,32},{8,40},{16,48},{24,56},{32,64},{40,72},{48,80},{56,88},{64,... | collective-permute-start | bytes 368648 | tf_op jit(solution)/shard_map/ppermute | solution.py:295
  92.0 14.2 %collective-permute-start.16 = (bf16[5,48,256]{2,1,0:T(8,128)(2,1)S(1)}, bf16[5,48,256]{2,1,0:T(8,128)(2,1)S(1)}, u32[]{:S(2)}, u32[]{:S(2)}) collective-permute-start(bf16[5,48,256]{2,1,0:T(8,128)(2,1)S(1)} %get-tuple-element.16), channel_id=1, source_target_pairs={{0,88},{8,80},{16,104},{24,96},{32,120},{40,112},{48,8},{56,0},{64... | collective-permute-start | bytes 368648 | tf_op jit(solution)/shard_map/ppermute | solution.py:295
  94.3 17.3 %collective-permute-start.15 = (bf16[5,48,256]{2,1,0:T(8,128)(2,1)S(1)}, bf16[5,48,256]{2,1,0:T(8,128)(2,1)S(1)}, u32[]{:S(2)}, u32[]{:S(2)}) collective-permute-start(bf16[5,48,256]{2,1,0:T(8,128)(2,1)S(1)} %get-tuple-element.17), channel_id=1, source_target_pairs={{0,80},{8,88},{16,96},{24,104},{32,112},{40,120},{48,0},{56,8},{64... | collective-permute-start | bytes 368648 | tf_op jit(solution)/shard_map/ppermute | solution.py:295
  96.8 40.2 %copy-start.6 = (bf16[5,48,256]{2,1,0:T(8,128)(2,1)}, bf16[5,48,256]{2,1,0:T(8,128)(2,1)S(1)}, u32[]{:S(2)}) copy-start(bf16[5,48,256]{2,1,0:T(8,128)(2,1)S(1)} %collective-permute-done.19.refs_9_) | copy-start | bytes 368644
  96.8 15.8 %collective-permute-start.14 = (bf16[5,48,256]{2,1,0:T(8,128)(2,1)S(1)}, bf16[5,48,256]{2,1,0:T(8,128)(2,1)S(1)}, u32[]{:S(2)}, u32[]{:S(2)}) collective-permute-start(bf16[5,48,256]{2,1,0:T(8,128)(2,1)S(1)} %get-tuple-element.18), channel_id=1, source_target_pairs={{0,56},{8,48},{16,72},{24,64},{32,88},{40,80},{48,104},{56,96},{64... | collective-permute-start | bytes 368648 | tf_op jit(solution)/shard_map/ppermute | solution.py:295
  100.2 20.0 %collective-permute-start.13 = (bf16[5,48,256]{2,1,0:T(8,128)(2,1)S(1)}, bf16[5,48,256]{2,1,0:T(8,128)(2,1)S(1)}, u32[]{:S(2)}, u32[]{:S(2)}) collective-permute-start(bf16[5,48,256]{2,1,0:T(8,128)(2,1)S(1)} %get-tuple-element.19), channel_id=1, source_target_pairs={{0,48},{8,56},{16,64},{24,72},{32,80},{40,88},{48,96},{56,104},{64... | collective-permute-start | bytes 368648 | tf_op jit(solution)/shard_map/ppermute | solution.py:295
  102.3 25.3 %collective-permute-start.12 = (bf16[5,48,256]{2,1,0:T(8,128)(2,1)S(1)}, bf16[5,48,256]{2,1,0:T(8,128)(2,1)S(1)}, u32[]{:S(2)}, u32[]{:S(2)}) collective-permute-start(bf16[5,48,256]{2,1,0:T(8,128)(2,1)S(1)} %get-tuple-element.20), channel_id=1, source_target_pairs={{0,72},{8,64},{16,88},{24,80},{32,104},{40,96},{48,120},{56,112},{... | collective-permute-start | bytes 368648 | tf_op jit(solution)/shard_map/ppermute | solution.py:295
  106.2 27.1 %collective-permute-start.11 = (bf16[5,48,256]{2,1,0:T(8,128)(2,1)S(1)}, bf16[5,48,256]{2,1,0:T(8,128)(2,1)S(1)}, u32[]{:S(2)}, u32[]{:S(2)}) collective-permute-start(bf16[5,48,256]{2,1,0:T(8,128)(2,1)S(1)} %get-tuple-element.21), channel_id=1, source_target_pairs={{0,64},{8,72},{16,80},{24,88},{32,96},{40,104},{48,112},{56,120},{... | collective-permute-start | bytes 368648 | tf_op jit(solution)/shard_map/ppermute | solution.py:295
  111.6 21.7 %collective-permute-start.10 = (bf16[5,48,256]{2,1,0:T(8,128)(2,1)S(1)}, bf16[5,48,256]{2,1,0:T(8,128)(2,1)S(1)}, u32[]{:S(2)}, u32[]{:S(2)}) collective-permute-start(bf16[5,48,256]{2,1,0:T(8,128)(2,1)S(1)} %get-tuple-element.23), channel_id=1, source_target_pairs={{0,8},{8,0},{16,24},{24,16},{32,40},{40,32},{48,56},{56,48},{64,72... | collective-permute-start | bytes 368648 | tf_op jit(solution)/shard_map/ppermute | solution.py:295
  112.6 26.9 %collective-permute-start.9 = (bf16[5,48,256]{2,1,0:T(8,128)(2,1)S(1)}, bf16[5,48,256]{2,1,0:T(8,128)(2,1)S(1)}, u32[]{:S(2)}, u32[]{:S(2)}) collective-permute-start(bf16[5,48,256]{2,1,0:T(8,128)(2,1)S(1)} %get-tuple-element.24), channel_id=1, source_target_pairs={{0,120},{8,112},{16,8},{24,0},{32,24},{40,16},{48,40},{56,32},{64,... | collective-permute-start | bytes 368648 | tf_op jit(solution)/shard_map/ppermute | solution.py:295
  120.2 19.3 %collective-permute-start.8 = (bf16[5,48,256]{2,1,0:T(8,128)(2,1)S(1)}, bf16[5,48,256]{2,1,0:T(8,128)(2,1)S(1)}, u32[]{:S(2)}, u32[]{:S(2)}) collective-permute-start(bf16[5,48,256]{2,1,0:T(8,128)(2,1)S(1)} %get-tuple-element.25), channel_id=1, source_target_pairs={{0,112},{8,120},{16,0},{24,8},{32,16},{40,24},{48,32},{56,40},{64,... | collective-permute-start | bytes 368648 | tf_op jit(solution)/shard_map/ppermute | solution.py:295
  127.6 12.0 %collective-permute-start.7 = (bf16[5,48,256]{2,1,0:T(8,128)(2,1)S(1)}, bf16[5,48,256]{2,1,0:T(8,128)(2,1)S(1)}, u32[]{:S(2)}, u32[]{:S(2)}) collective-permute-start(bf16[5,48,256]{2,1,0:T(8,128)(2,1)S(1)} %get-tuple-element.26), channel_id=1, source_target_pairs={{0,24},{8,16},{16,40},{24,32},{32,56},{40,48},{48,72},{56,64},{64,... | collective-permute-start | bytes 368648 | tf_op jit(solution)/shard_map/ppermute | solution.py:295
  133.3 6.6 %collective-permute-start.6 = (bf16[5,48,256]{2,1,0:T(8,128)(2,1)S(1)}, bf16[5,48,256]{2,1,0:T(8,128)(2,1)S(1)}, u32[]{:S(2)}, u32[]{:S(2)}) collective-permute-start(bf16[5,48,256]{2,1,0:T(8,128)(2,1)S(1)} %get-tuple-element.27), channel_id=1, source_target_pairs={{0,16},{8,24},{16,32},{24,40},{32,48},{40,56},{48,64},{56,72},{64,... | collective-permute-start | bytes 368648 | tf_op jit(solution)/shard_map/ppermute | solution.py:295
  133.3 8.9 %collective-permute-start.5 = (bf16[5,48,256]{2,1,0:T(8,128)(2,1)S(1)}, bf16[5,48,256]{2,1,0:T(8,128)(2,1)S(1)}, u32[]{:S(2)}, u32[]{:S(2)}) collective-permute-start(bf16[5,48,256]{2,1,0:T(8,128)(2,1)S(1)} %get-tuple-element.28), channel_id=1, source_target_pairs={{0,104},{8,96},{16,120},{24,112},{32,8},{40,0},{48,24},{56,16},{64... | collective-permute-start | bytes 368648 | tf_op jit(solution)/shard_map/ppermute | solution.py:295
  (21 other events, 255.6 us)

commit v5 on v4

--- a/solution.py
+++ b/solution.py
@@ -345,8 +345,13 @@
     order = (member[:, None] == wanted[None]).astype(bf16)
     trans_w = roots(mine, other, order, pieces, members)
 
-    updated = jnp.einsum("inc,nij->jnc", incoming, trans_w, preferred_element_type=f32).astype(bf16)
-    slots = updated.reshape(groups, held, domains, quantities)
+    def mixed(low, high):
+        part = trans_w[:, :, low * held : high * held]
+        part = jnp.einsum("inc,nij->jnc", incoming, part, preferred_element_type=f32).astype(bf16)
+        return list(part.reshape(high - low, held, domains, quantities))
+
+    slots = mixed(0, 3)
+    slots = slots + mixed(3, groups)
     arrived = [slots[0]]
     for k, (step, flip) in enumerate(paths[1:], 1):
         arrived.append(sent(slots[k], step, flip))

time: 146 us -> 144 us (0.986)
  starting transfers between devices: 66.3 us -> 64.7 us
    ppermute x15, starting transfers between devices: 31.1 us -> 29.4 us  [sent(): return lax.ppermute(value, MEMBER, pairs)]
    dot_general x1 -> x2, matrix products: 2.04 us -> 3.47 us  [mixed(): jnp.einsum('inc,nij->jnc', incoming, part, preferred_element_type=f32)]
where the time goes in v5:
time: 144 us
  starting transfers between devices  64.7 us (45%)
  waiting for transfers between devices  36.8 us (26%)
  Pallas kernels  28.9 us (20%)
  local copies, waits for them, and re-layouts  8.09 us (6%)
  matrix products  3.47 us (2%)
    ppermute x15, starting transfers between devices, sent(): return lax.ppermute(value, MEMBER, pairs)  29.4 us
    all_to_all x1, starting transfers between devices, spread_copies(): return lax.all_to_all(copies, axis, split_axis=0, concat_axis=0, tiled=True)  23.7 us
    ppermute x15, waiting for transfers between devices, sent(): return lax.ppermute(value, MEMBER, pairs)  19.5 us
    pallas_call x3, Pallas kernels, grams(): pl.pallas_call(gram_kernel(members, part * own), grid=(1,), in_specs=[sme...  10.4 us
    pallas_call x1, Pallas kernels, roots(): pl.pallas_call(root_kernel(members, len(pieces)), in_specs=[vmem()] * (3...  9.89 us
    all_to_all x1, waiting for transfers between devices, spread_copies(): return lax.all_to_all(copies, axis, split_axis=0, concat_axis=0, tiled=True)  6.3 us
    all_to_all x1, waiting for transfers between devices, per_device(): lax.all_to_all(outgoing, MEMBER, split_axis=0, concat_axis=0, tiled=True)  6.07 us
    pallas_call x2, Pallas kernels, place(): pl.pallas_call(place_kernel(skip, count), in_specs=[smem()] + [vmem()] *...  4.58 us
  transfers between devices with their start and end apart: 22, of which 11 were waited for; matrix products, arithmetic and copies ran while one was open for 4% of the time, Pallas kernels for 19%

profile of v5, /device:TPU:513, one launch (start us, length us, event | category | flops | bytes accessed | tf_op | source)
XLA Modules:
  0.0 143.7 jit_solution(17479900619170694120)
XLA Ops:
  1.4 23.7 %all-to-all-start = ((bf16[16,32,128]{2,1,0:T(8,128)(2,1)}), bf16[16,32,128]{2,1,0:T(8,128)(2,1)S(1)}, u32[]{:S(2)}, u32[]{:S(2)}) async-start(bf16[16,32,128]{2,1,0:T(8,128)(2,1)} %broadcast_in_dim.2), calls=%async_computation | async-start | bytes 262144 | tf_op jit(solution)/shard_map/all_to_all | solution.py:30
  25.1 2.9 %copy.38 = bf16[16,5,48,256]{3,2,1,0:T(8,128)(2,1)} copy(bf16[16,5,48,256]{3,2,0,1:T(8,128)(2,1)} %bitcast.33) | data formatting | bytes 3932160 | tf_op jit(solution)/shard_map/transpose | solution.py:319
  28.1 6.3 %all-to-all-done = bf16[16,32,128]{2,1,0:T(8,128)(2,1)S(1)} async-done(((bf16[16,32,128]{2,1,0:T(8,128)(2,1)}), bf16[16,32,128]{2,1,0:T(8,128)(2,1)S(1)}, u32[]{:S(2)}, u32[]{:S(2)}) %all-to-all-start) | async-done | bytes 131104 | tf_op jit(solution)/shard_map/all_to_all | solution.py:30
  34.4 3.9 %all-to-all-start.1 = ((bf16[16,5,48,256]{3,2,1,0:T(8,128)(2,1)}), bf16[16,5,48,256]{3,2,1,0:T(8,128)(2,1)S(1)}, u32[]{:S(2)}, u32[]{:S(2)}) async-start(bf16[16,5,48,256]{3,2,1,0:T(8,128)(2,1)} %copy.38), calls=%async_computation.1 | async-start | bytes 3932160 | tf_op jit(solution)/shard_map/all_to_all | solution.py:320
  40.1 4.0 %collective-permute-start = (bf16[82,320]{1,0:T(8,128)(2,1)S(1)}, bf16[82,320]{1,0:T(8,128)(2,1)S(1)}, u32[]{:S(2)}, u32[]{:S(2)}) collective-permute-start(bf16[82,320]{1,0:T(8,128)(2,1)S(1)} %get-tuple-element.30), channel_id=1, source_target_pairs={{0,1},{1,2},{2,3},{3,4},{4,5},{5,6},{6,7},{8,9},{9,10},{10,11},{11... | collective-permute-start | bytes 157448 | tf_op jit(solution)/shard_map/ppermute | solution.py:42
  46.4 4.0 %block_sums.1 = (f32[2,128]{1,0:T(2,128)}, s32[48,128]{1,0:T(8,128)}, f32[48,128]{1,0:T(8,128)}) custom-call(s32[1]{0:T(128)} %bitcast.first_ref, s32[768]{0:T(1024)} %tiers_ref.1, bf16[12,88,128]{2,1,0:T(8,128)(2,1)} %bitcast_bitcast_fusion.window_ref, s32[768,128]{1,0:T(8,128)} %lists_ref.1), custom_call_target="tpu_custom_call" | custom-call | flops 10000000 | bytes 1000000 | tf_op jit(solution)/shard_map/block_sums/pallas_call | solution.py:108
  50.4 2.1 %collective-permute-start.2 = (f32[2,128]{1,0:T(2,128)}, f32[2,128]{1,0:T(2,128)S(1)}, u32[]{:S(2)}, u32[]{:S(2)}) collective-permute-start(f32[2,128]{1,0:T(2,128)} %get-tuple-element.8), channel_id=1, source_target_pairs={{0,1},{1,2},{2,3},{3,4},{4,5},{5,6},{6,7},{7,0},{8,9},{9,10},{10,1... | collective-permute-start | bytes 3080 | tf_op jit(solution)/shard_map/ppermute | solution.py:35
  52.6 3.5 %grams.5.refs_2_ = f32[16,80,88]{2,1,0:T(8,128)} custom-call(s32[1]{0:T(128)} %bitcast.first_ref, bf16[12,88,128]{2,1,0:T(8,128)(2,1)} %bitcast_bitcast_fusion.window_ref, s32[48,128]{1,0:T(8,128)} %get-tuple-element.9.local_ref, f32[48,128]{1,0:T(8,128)} %get-tuple-element.10.decay_ref), custom_call_target="tpu_custom_call" | custom-call | flops 960000000 | bytes 640000 | tf_op jit(solution)/shard_map/grams/pallas_call | solution.py:160
  56.2 3.5 %grams.4.refs_1_ = f32[16,80,88]{2,1,0:T(8,128)} custom-call(s32[1]{0:T(128)} %bitcast.first_ref, bf16[12,88,128]{2,1,0:T(8,128)(2,1)} %bitcast_bitcast_fusion.window_ref, s32[48,128]{1,0:T(8,128)} %get-tuple-element.9.local_ref, f32[48,128]{1,0:T(8,128)} %get-tuple-element.10.decay_ref), custom_call_target="tpu_custom_call" | custom-call | flops 960000000 | bytes 640000 | tf_op jit(solution)/shard_map/grams/pallas_call | solution.py:160
  61.0 3.5 %grams.3.refs_0_ = f32[16,80,88]{2,1,0:T(8,128)} custom-call(s32[1]{0:T(128)} %bitcast.first_ref, bf16[12,88,128]{2,1,0:T(8,128)(2,1)} %bitcast_bitcast_fusion.window_ref, s32[48,128]{1,0:T(8,128)} %get-tuple-element.9.local_ref, f32[48,128]{1,0:T(8,128)} %get-tuple-element.10.decay_ref), custom_call_target="tpu_custom_call" | custom-call | flops 960000000 | bytes 640000 | tf_op jit(solution)/shard_map/grams/pallas_call | solution.py:160
  64.5 2.8 %collective-permute-done.4.other_ref = f32[2,128]{1,0:T(2,128)S(1)} collective-permute-done((f32[2,128]{1,0:T(2,128)S(1)}, f32[2,128]{1,0:T(2,128)S(1)}, u32[]{:S(2)}, u32[]{:S(2)}) %collective-permute-start.4) | collective-permute-done | bytes 1056 | tf_op jit(solution)/shard_map/ppermute | solution.py:35
  67.9 9.9 %roots.1 = bf16[48,80,80]{2,1,0:T(8,128)(2,1)} custom-call(f32[2,128]{1,0:T(2,128)} %copy-done.18, f32[2,128]{1,0:T(2,128)} %copy-done.23, bf16[80,80]{1,0:T(8,128)(2,1)} %fusion.8.order_ref, f32[16,80,88]{2,1,0:T(8,128)} %grams.3.refs_0_, f32[16,80,88]{2,1,0:T(8,128)} %grams.4.refs_1_, f32[16,80,88]{2,1,0:T(8,128)} %grams.5.refs_2_), custom_call_target="tpu_custom_call" | custom-call | flops 2880000000 | bytes 2400000 | tf_op jit(solution)/shard_map/roots/pallas_call | solution.py:242
  77.8 6.1 %all-to-all-done.1 = bf16[16,5,48,256]{3,2,1,0:T(8,128)(2,1)S(1)} async-done(((bf16[16,5,48,256]{3,2,1,0:T(8,128)(2,1)}), bf16[16,5,48,256]{3,2,1,0:T(8,128)(2,1)S(1)}, u32[]{:S(2)}, u32[]{:S(2)}) %all-to-all-start.1) | async-done | bytes 1966112 | tf_op jit(solution)/shard_map/all_to_all | solution.py:320
  92.6 2.3 %collective-permute-start.16 = (bf16[5,48,256]{2,1,0:T(8,128)(2,1)S(1)}, bf16[5,48,256]{2,1,0:T(8,128)(2,1)S(1)}, u32[]{:S(2)}, u32[]{:S(2)}) collective-permute-start(bf16[5,48,256]{2,1,0:T(8,128)(2,1)S(1)} %get-tuple-element.16), channel_id=1, source_target_pairs={{0,88},{8,80},{16,104},{24,96},{32,120},{40,112},{48,8},{56,0},{64... | collective-permute-start | bytes 368648 | tf_op jit(solution)/shard_map/ppermute | solution.py:295
  94.9 2.5 %collective-permute-start.15 = (bf16[5,48,256]{2,1,0:T(8,128)(2,1)S(1)}, bf16[5,48,256]{2,1,0:T(8,128)(2,1)S(1)}, u32[]{:S(2)}, u32[]{:S(2)}) collective-permute-start(bf16[5,48,256]{2,1,0:T(8,128)(2,1)S(1)} %get-tuple-element.17), channel_id=1, source_target_pairs={{0,80},{8,88},{16,96},{24,104},{32,112},{40,120},{48,0},{56,8},{64... | collective-permute-start | bytes 368648 | tf_op jit(solution)/shard_map/ppermute | solution.py:295
  98.2 2.7 %collective-permute-start.14 = (bf16[5,48,256]{2,1,0:T(8,128)(2,1)S(1)}, bf16[5,48,256]{2,1,0:T(8,128)(2,1)S(1)}, u32[]{:S(2)}, u32[]{:S(2)}) collective-permute-start(bf16[5,48,256]{2,1,0:T(8,128)(2,1)S(1)} %get-tuple-element.18), channel_id=1, source_target_pairs={{0,56},{8,48},{16,72},{24,64},{32,88},{40,80},{48,104},{56,96},{64... | collective-permute-start | bytes 368648 | tf_op jit(solution)/shard_map/ppermute | solution.py:295
  100.9 2.4 %collective-permute-start.13 = (bf16[5,48,256]{2,1,0:T(8,128)(2,1)S(1)}, bf16[5,48,256]{2,1,0:T(8,128)(2,1)S(1)}, u32[]{:S(2)}, u32[]{:S(2)}) collective-permute-start(bf16[5,48,256]{2,1,0:T(8,128)(2,1)S(1)} %get-tuple-element.19), channel_id=1, source_target_pairs={{0,48},{8,56},{16,64},{24,72},{32,80},{40,88},{48,96},{56,104},{64... | collective-permute-start | bytes 368648 | tf_op jit(solution)/shard_map/ppermute | solution.py:295
  103.4 4.8 %collective-permute-start.12 = (bf16[5,48,256]{2,1,0:T(8,128)(2,1)S(1)}, bf16[5,48,256]{2,1,0:T(8,128)(2,1)S(1)}, u32[]{:S(2)}, u32[]{:S(2)}) collective-permute-start(bf16[5,48,256]{2,1,0:T(8,128)(2,1)S(1)} %get-tuple-element.26), channel_id=1, source_target_pairs={{0,72},{8,64},{16,88},{24,80},{32,104},{40,96},{48,120},{56,112},{... | collective-permute-start | bytes 368648 | tf_op jit(solution)/shard_map/ppermute | solution.py:295
  108.2 4.1 %collective-permute-done.15.refs_5_ = bf16[5,48,256]{2,1,0:T(8,128)(2,1)S(1)} collective-permute-done((bf16[5,48,256]{2,1,0:T(8,128)(2,1)S(1)}, bf16[5,48,256]{2,1,0:T(8,128)(2,1)S(1)}, u32[]{:S(2)}, u32[]{:S(2)}) %collective-permute-start.15) | collective-permute-done | bytes 122912 | tf_op jit(solution)/shard_map/ppermute | solution.py:295
  112.4 6.7 %collective-permute-start.9 = (bf16[5,48,256]{2,1,0:T(8,128)(2,1)S(1)}, bf16[5,48,256]{2,1,0:T(8,128)(2,1)S(1)}, u32[]{:S(2)}, u32[]{:S(2)}) collective-permute-start(bf16[5,48,256]{2,1,0:T(8,128)(2,1)S(1)} %get-tuple-element.21), channel_id=1, source_target_pairs={{0,120},{8,112},{16,8},{24,0},{32,24},{40,16},{48,40},{56,32},{64,... | collective-permute-start | bytes 368648 | tf_op jit(solution)/shard_map/ppermute | solution.py:295
  121.2 2.3 %collective-permute-start.7 = (bf16[5,48,256]{2,1,0:T(8,128)(2,1)S(1)}, bf16[5,48,256]{2,1,0:T(8,128)(2,1)S(1)}, u32[]{:S(2)}, u32[]{:S(2)}) collective-permute-start(bf16[5,48,256]{2,1,0:T(8,128)(2,1)S(1)} %get-tuple-element.23), channel_id=1, source_target_pairs={{0,24},{8,16},{16,40},{24,32},{32,56},{40,48},{48,72},{56,64},{64,... | collective-permute-start | bytes 368648 | tf_op jit(solution)/shard_map/ppermute | solution.py:295
  123.4 7.1 %collective-permute-done.12.refs_2_ = bf16[5,48,256]{2,1,0:T(8,128)(2,1)S(1)} collective-permute-done((bf16[5,48,256]{2,1,0:T(8,128)(2,1)S(1)}, bf16[5,48,256]{2,1,0:T(8,128)(2,1)S(1)}, u32[]{:S(2)}, u32[]{:S(2)}) %collective-permute-start.12) | collective-permute-done | bytes 122912 | tf_op jit(solution)/shard_map/ppermute | solution.py:295
  130.5 3.8 %collective-permute-done.11.refs_1_ = bf16[5,48,256]{2,1,0:T(8,128)(2,1)S(1)} collective-permute-done((bf16[5,48,256]{2,1,0:T(8,128)(2,1)S(1)}, bf16[5,48,256]{2,1,0:T(8,128)(2,1)S(1)}, u32[]{:S(2)}, u32[]{:S(2)}) %collective-permute-start.11) | collective-permute-done | bytes 122912 | tf_op jit(solution)/shard_map/ppermute | solution.py:295
  135.6 2.5 %place.2.refs_6_ = bf16[5,768,256]{2,1,0:T(8,128)(2,1)} custom-call(s32[16]{0:T(128)} %fusion.16.starts_ref, bf16[5,48,256]{2,1,0:T(8,128)(2,1)} %get-tuple-element.28.refs_0_, bf16[5,48,256]{2,1,0:T(8,128)(2,1)} %copy-done.15, bf16[5,48,256]{2,1,0:T(8,128)(2,1)} %copy-done.14, bf16[5,48,256]{2,1,0:T(8,128)(2,1)} %copy-done.13, ...), custom_call_target="tpu_custom_call" | custom-call | flops 1000000 | bytes 3000000 | tf_op jit(solution)/shard_map/place/pallas_call | solution.py:271
  (101 shorter events, 25.6 us)
Async XLA Ops:
  1.4 33.0 %all-to-all-start = ((bf16[16,32,128]{2,1,0:T(8,128)(2,1)}), bf16[16,32,128]{2,1,0:T(8,128)(2,1)S(1)}, u32[]{:S(2)}, u32[]{:S(2)}) async-start(bf16[16,32,128]{2,1,0:T(8,128)(2,1)} %broadcast_in_dim.2), calls=%async_computation | async-start | bytes 262144 | tf_op jit(solution)/shard_map/all_to_all | solution.py:30
  34.4 49.4 %all-to-all-start.1 = ((bf16[16,5,48,256]{3,2,1,0:T(8,128)(2,1)}), bf16[16,5,48,256]{3,2,1,0:T(8,128)(2,1)S(1)}, u32[]{:S(2)}, u32[]{:S(2)}) async-start(bf16[16,5,48,256]{3,2,1,0:T(8,128)(2,1)} %copy.38), calls=%async_computation.1 | async-start | bytes 3932160 | tf_op jit(solution)/shard_map/all_to_all | solution.py:320
  38.8 6.0 %collective-permute-start.1 = (bf16[82,320]{1,0:T(8,128)(2,1)S(1)}, bf16[82,320]{1,0:T(8,128)(2,1)S(1)}, u32[]{:S(2)}, u32[]{:S(2)}) collective-permute-start(bf16[82,320]{1,0:T(8,128)(2,1)S(1)} %get-tuple-element.29), channel_id=1, source_target_pairs={{1,0},{2,1},{3,2},{4,3},{5,4},{6,5},{7,6},{9,8},{10,9},{11,10},{12... | collective-permute-start | bytes 157448 | tf_op jit(solution)/shard_map/ppermute | solution.py:43
  40.1 5.4 %collective-permute-start = (bf16[82,320]{1,0:T(8,128)(2,1)S(1)}, bf16[82,320]{1,0:T(8,128)(2,1)S(1)}, u32[]{:S(2)}, u32[]{:S(2)}) collective-permute-start(bf16[82,320]{1,0:T(8,128)(2,1)S(1)} %get-tuple-element.30), channel_id=1, source_target_pairs={{0,1},{1,2},{2,3},{3,4},{4,5},{5,6},{6,7},{8,9},{9,10},{10,11},{11... | collective-permute-start | bytes 157448 | tf_op jit(solution)/shard_map/ppermute | solution.py:42
  50.4 5.6 %collective-permute-start.2 = (f32[2,128]{1,0:T(2,128)}, f32[2,128]{1,0:T(2,128)S(1)}, u32[]{:S(2)}, u32[]{:S(2)}) collective-permute-start(f32[2,128]{1,0:T(2,128)} %get-tuple-element.8), channel_id=1, source_target_pairs={{0,1},{1,2},{2,3},{3,4},{4,5},{5,6},{6,7},{7,0},{8,9},{9,10},{10,1... | collective-permute-start | bytes 3080 | tf_op jit(solution)/shard_map/ppermute | solution.py:35
  56.0 4.9 %collective-permute-start.3 = (f32[2,128]{1,0:T(2,128)S(1)}, f32[2,128]{1,0:T(2,128)S(1)}, u32[]{:S(2)}, u32[]{:S(2)}) collective-permute-start(f32[2,128]{1,0:T(2,128)S(1)} %add.62), channel_id=1, source_target_pairs={{0,2},{1,3},{2,4},{3,5},{4,6},{5,7},{6,0},{7,1},{8,10},{9,11},{10,... | collective-permute-start | bytes 3080 | tf_op jit(solution)/shard_map/ppermute | solution.py:35
  61.0 6.3 %collective-permute-start.4 = (f32[2,128]{1,0:T(2,128)S(1)}, f32[2,128]{1,0:T(2,128)S(1)}, u32[]{:S(2)}, u32[]{:S(2)}) collective-permute-start(f32[2,128]{1,0:T(2,128)S(1)} %add.63.sums_ref), channel_id=1, source_target_pairs={{0,4},{1,5},{2,6},{3,7},{4,0},{5,1},{6,2},{7,3},{8,12},{9,13},{10,... | collective-permute-start | bytes 3080 | tf_op jit(solution)/shard_map/ppermute | solution.py:35
  87.8 47.3 %copy-start.20 = (s32[16]{0:T(128)S(1)}, s32[16]{0:T(128)}, u32[]{:S(2)}) copy-start(s32[16]{0:T(128)} %constant.45) | copy-start | bytes 196
  87.9 10.3 %collective-permute-start.19 = (bf16[5,48,256]{2,1,0:T(8,128)(2,1)S(1)}, bf16[5,48,256]{2,1,0:T(8,128)(2,1)S(1)}, u32[]{:S(2)}, u32[]{:S(2)}) collective-permute-start(bf16[5,48,256]{2,1,0:T(8,128)(2,1)S(1)} %get-tuple-element.13), channel_id=1, source_target_pairs={{0,96},{8,104},{16,112},{24,120},{32,0},{40,8},{48,16},{56,24},{64... | collective-permute-start | bytes 368648 | tf_op jit(solution)/shard_map/ppermute | solution.py:295
  89.6 11.3 %collective-permute-start.18 = (bf16[5,48,256]{2,1,0:T(8,128)(2,1)S(1)}, bf16[5,48,256]{2,1,0:T(8,128)(2,1)S(1)}, u32[]{:S(2)}, u32[]{:S(2)}) collective-permute-start(bf16[5,48,256]{2,1,0:T(8,128)(2,1)S(1)} %get-tuple-element.14), channel_id=1, source_target_pairs={{0,40},{8,32},{16,56},{24,48},{32,72},{40,64},{48,88},{56,80},{64,... | collective-permute-start | bytes 368648 | tf_op jit(solution)/shard_map/ppermute | solution.py:295
  91.0 12.3 %collective-permute-start.17 = (bf16[5,48,256]{2,1,0:T(8,128)(2,1)S(1)}, bf16[5,48,256]{2,1,0:T(8,128)(2,1)S(1)}, u32[]{:S(2)}, u32[]{:S(2)}) collective-permute-start(bf16[5,48,256]{2,1,0:T(8,128)(2,1)S(1)} %get-tuple-element.15), channel_id=1, source_target_pairs={{0,32},{8,40},{16,48},{24,56},{32,64},{40,72},{48,80},{56,88},{64,... | collective-permute-start | bytes 368648 | tf_op jit(solution)/shard_map/ppermute | solution.py:295
  92.6 10.8 %collective-permute-start.16 = (bf16[5,48,256]{2,1,0:T(8,128)(2,1)S(1)}, bf16[5,48,256]{2,1,0:T(8,128)(2,1)S(1)}, u32[]{:S(2)}, u32[]{:S(2)}) collective-permute-start(bf16[5,48,256]{2,1,0:T(8,128)(2,1)S(1)} %get-tuple-element.16), channel_id=1, source_target_pairs={{0,88},{8,80},{16,104},{24,96},{32,120},{40,112},{48,8},{56,0},{64... | collective-permute-start | bytes 368648 | tf_op jit(solution)/shard_map/ppermute | solution.py:295
  94.9 17.4 %collective-permute-start.15 = (bf16[5,48,256]{2,1,0:T(8,128)(2,1)S(1)}, bf16[5,48,256]{2,1,0:T(8,128)(2,1)S(1)}, u32[]{:S(2)}, u32[]{:S(2)}) collective-permute-start(bf16[5,48,256]{2,1,0:T(8,128)(2,1)S(1)} %get-tuple-element.17), channel_id=1, source_target_pairs={{0,80},{8,88},{16,96},{24,104},{32,112},{40,120},{48,0},{56,8},{64... | collective-permute-start | bytes 368648 | tf_op jit(solution)/shard_map/ppermute | solution.py:295
  98.2 37.4 %copy-start.7 = (bf16[5,48,256]{2,1,0:T(8,128)(2,1)}, bf16[5,48,256]{2,1,0:T(8,128)(2,1)S(1)}, u32[]{:S(2)}) copy-start(bf16[5,48,256]{2,1,0:T(8,128)(2,1)S(1)} %collective-permute-done.19.refs_9_) | copy-start | bytes 368644
  98.2 14.2 %collective-permute-start.14 = (bf16[5,48,256]{2,1,0:T(8,128)(2,1)S(1)}, bf16[5,48,256]{2,1,0:T(8,128)(2,1)S(1)}, u32[]{:S(2)}, u32[]{:S(2)}) collective-permute-start(bf16[5,48,256]{2,1,0:T(8,128)(2,1)S(1)} %get-tuple-element.18), channel_id=1, source_target_pairs={{0,56},{8,48},{16,72},{24,64},{32,88},{40,80},{48,104},{56,96},{64... | collective-permute-start | bytes 368648 | tf_op jit(solution)/shard_map/ppermute | solution.py:295
  100.9 20.2 %collective-permute-start.13 = (bf16[5,48,256]{2,1,0:T(8,128)(2,1)S(1)}, bf16[5,48,256]{2,1,0:T(8,128)(2,1)S(1)}, u32[]{:S(2)}, u32[]{:S(2)}) collective-permute-start(bf16[5,48,256]{2,1,0:T(8,128)(2,1)S(1)} %get-tuple-element.19), channel_id=1, source_target_pairs={{0,48},{8,56},{16,64},{24,72},{32,80},{40,88},{48,96},{56,104},{64... | collective-permute-start | bytes 368648 | tf_op jit(solution)/shard_map/ppermute | solution.py:295
  103.3 17.8 %collective-permute-start.10 = (bf16[5,48,256]{2,1,0:T(8,128)(2,1)S(1)}, bf16[5,48,256]{2,1,0:T(8,128)(2,1)S(1)}, u32[]{:S(2)}, u32[]{:S(2)}) collective-permute-start(bf16[5,48,256]{2,1,0:T(8,128)(2,1)S(1)} %get-tuple-element.20), channel_id=1, source_target_pairs={{0,8},{8,0},{16,24},{24,16},{32,40},{40,32},{48,56},{56,48},{64,72... | collective-permute-start | bytes 368648 | tf_op jit(solution)/shard_map/ppermute | solution.py:295
  103.4 27.1 %collective-permute-start.12 = (bf16[5,48,256]{2,1,0:T(8,128)(2,1)S(1)}, bf16[5,48,256]{2,1,0:T(8,128)(2,1)S(1)}, u32[]{:S(2)}, u32[]{:S(2)}) collective-permute-start(bf16[5,48,256]{2,1,0:T(8,128)(2,1)S(1)} %get-tuple-element.26), channel_id=1, source_target_pairs={{0,72},{8,64},{16,88},{24,80},{32,104},{40,96},{48,120},{56,112},{... | collective-permute-start | bytes 368648 | tf_op jit(solution)/shard_map/ppermute | solution.py:295
  112.3 21.9 %collective-permute-start.11 = (bf16[5,48,256]{2,1,0:T(8,128)(2,1)S(1)}, bf16[5,48,256]{2,1,0:T(8,128)(2,1)S(1)}, u32[]{:S(2)}, u32[]{:S(2)}) collective-permute-start(bf16[5,48,256]{2,1,0:T(8,128)(2,1)S(1)} %get-tuple-element.27), channel_id=1, source_target_pairs={{0,64},{8,72},{16,80},{24,88},{32,96},{40,104},{48,112},{56,120},{... | collective-permute-start | bytes 368648 | tf_op jit(solution)/shard_map/ppermute | solution.py:295
  112.4 25.7 %collective-permute-start.9 = (bf16[5,48,256]{2,1,0:T(8,128)(2,1)S(1)}, bf16[5,48,256]{2,1,0:T(8,128)(2,1)S(1)}, u32[]{:S(2)}, u32[]{:S(2)}) collective-permute-start(bf16[5,48,256]{2,1,0:T(8,128)(2,1)S(1)} %get-tuple-element.21), channel_id=1, source_target_pairs={{0,120},{8,112},{16,8},{24,0},{32,24},{40,16},{48,40},{56,32},{64,... | collective-permute-start | bytes 368648 | tf_op jit(solution)/shard_map/ppermute | solution.py:295
  121.1 16.9 %collective-permute-start.8 = (bf16[5,48,256]{2,1,0:T(8,128)(2,1)S(1)}, bf16[5,48,256]{2,1,0:T(8,128)(2,1)S(1)}, u32[]{:S(2)}, u32[]{:S(2)}) collective-permute-start(bf16[5,48,256]{2,1,0:T(8,128)(2,1)S(1)} %get-tuple-element.22), channel_id=1, source_target_pairs={{0,112},{8,120},{16,0},{24,8},{32,16},{40,24},{48,32},{56,40},{64,... | collective-permute-start | bytes 368648 | tf_op jit(solution)/shard_map/ppermute | solution.py:295
  121.2 16.9 %collective-permute-start.7 = (bf16[5,48,256]{2,1,0:T(8,128)(2,1)S(1)}, bf16[5,48,256]{2,1,0:T(8,128)(2,1)S(1)}, u32[]{:S(2)}, u32[]{:S(2)}) collective-permute-start(bf16[5,48,256]{2,1,0:T(8,128)(2,1)S(1)} %get-tuple-element.23), channel_id=1, source_target_pairs={{0,24},{8,16},{16,40},{24,32},{32,56},{40,48},{48,72},{56,64},{64,... | collective-permute-start | bytes 368648 | tf_op jit(solution)/shard_map/ppermute | solution.py:295
  130.5 8.4 %collective-permute-start.6 = (bf16[5,48,256]{2,1,0:T(8,128)(2,1)S(1)}, bf16[5,48,256]{2,1,0:T(8,128)(2,1)S(1)}, u32[]{:S(2)}, u32[]{:S(2)}) collective-permute-start(bf16[5,48,256]{2,1,0:T(8,128)(2,1)S(1)} %get-tuple-element.24), channel_id=1, source_target_pairs={{0,16},{8,24},{16,32},{24,40},{32,48},{40,56},{48,64},{56,72},{64,... | collective-permute-start | bytes 368648 | tf_op jit(solution)/shard_map/ppermute | solution.py:295
  134.3 6.4 %collective-permute-start.5 = (bf16[5,48,256]{2,1,0:T(8,128)(2,1)S(1)}, bf16[5,48,256]{2,1,0:T(8,128)(2,1)S(1)}, u32[]{:S(2)}, u32[]{:S(2)}) collective-permute-start(bf16[5,48,256]{2,1,0:T(8,128)(2,1)S(1)} %get-tuple-element.25), channel_id=1, source_target_pairs={{0,104},{8,96},{16,120},{24,112},{32,8},{40,0},{48,24},{56,16},{64... | collective-permute-start | bytes 368648 | tf_op jit(solution)/shard_map/ppermute | solution.py:295
  (22 other events, 257.3 us)

commit v6 on v4

--- a/solution.py
+++ b/solution.py
@@ -281,10 +281,11 @@
 
 
 def routes(chips):
-    steps = []
+    others = []
     for far in range(chips // 2, 0, -1):
-        steps += [far] if 2 * far == chips else [far, -far]
-    return [(0, 0)] + [(step, flip) for step in steps for flip in (0, 1)] + [(0, 1)]
+        ways = [far] if 2 * far == chips else [far, -far]
+        others += [(step, flip) for flip in (0, 1) for step in ways]
+    return [(0, 0)] + others + [(0, 1)]
 
 
 def sent(value, step, flip):

time: 146 us -> 143 us (0.979)
  waiting for transfers between devices: 37.7 us -> 22.3 us
  starting transfers between devices: 66.3 us -> 79 us
    ppermute x15, waiting for transfers between devices: 20.6 us -> 5.24 us  [sent(): return lax.ppermute(value, MEMBER, pairs)]
    ppermute x15, starting transfers between devices: 31.1 us -> 43.8 us  [sent(): return lax.ppermute(value, MEMBER, pairs)]
  transfers between devices with their start and end apart: 22 -> 22, of which waited for: 11 -> 10; matrix products, arithmetic and copies ran while one was open for 4% -> 4% of each run, Pallas kernels for 19% -> 19%
where the time goes in v6:
time: 143 us
  starting transfers between devices  79 us (55%)
  Pallas kernels  29 us (20%)
  waiting for transfers between devices  22.3 us (16%)
  local copies, waits for them, and re-layouts  8.35 us (6%)
  matrix products  2.04 us (1%)
    ppermute x15, starting transfers between devices, sent(): return lax.ppermute(value, MEMBER, pairs)  43.8 us
    all_to_all x1, starting transfers between devices, spread_copies(): return lax.all_to_all(copies, axis, split_axis=0, concat_axis=0, tiled=True)  23.7 us
    pallas_call x3, Pallas kernels, grams(): pl.pallas_call(gram_kernel(members, part * own), grid=(1,), in_specs=[sme...  10.5 us
    pallas_call x1, Pallas kernels, roots(): pl.pallas_call(root_kernel(members, len(pieces)), in_specs=[vmem()] * (3...  9.91 us
    all_to_all x1, waiting for transfers between devices, spread_copies(): return lax.all_to_all(copies, axis, split_axis=0, concat_axis=0, tiled=True)  6.3 us
    all_to_all x1, waiting for transfers between devices, per_device(): lax.all_to_all(outgoing, MEMBER, split_axis=0, concat_axis=0, tiled=True)  5.97 us
    ppermute x15, waiting for transfers between devices, sent(): return lax.ppermute(value, MEMBER, pairs)  5.24 us
    pallas_call x2, Pallas kernels, place(): pl.pallas_call(place_kernel(skip, count), in_specs=[smem()] + [vmem()] *...  4.58 us
  transfers between devices with their start and end apart: 22, of which 10 were waited for; matrix products, arithmetic and copies ran while one was open for 4% of the time, Pallas kernels for 19%

profile of v6, /device:TPU:513, one launch (start us, length us, event | category | flops | bytes accessed | tf_op | source)
XLA Modules:
  0.0 142.6 jit_solution(2055583319638501387)
XLA Ops:
  1.4 23.7 %all-to-all-start = ((bf16[16,32,128]{2,1,0:T(8,128)(2,1)}), bf16[16,32,128]{2,1,0:T(8,128)(2,1)S(1)}, u32[]{:S(2)}, u32[]{:S(2)}) async-start(bf16[16,32,128]{2,1,0:T(8,128)(2,1)} %broadcast_in_dim.2), calls=%async_computation | async-start | bytes 262144 | tf_op jit(solution)/shard_map/all_to_all | solution.py:30
  25.1 2.9 %copy.30 = bf16[16,5,48,256]{3,2,1,0:T(8,128)(2,1)} copy(bf16[16,5,48,256]{3,2,0,1:T(8,128)(2,1)} %bitcast.30) | data formatting | bytes 3932160 | tf_op jit(solution)/shard_map/transpose | solution.py:320
  28.1 6.3 %all-to-all-done = bf16[16,32,128]{2,1,0:T(8,128)(2,1)S(1)} async-done(((bf16[16,32,128]{2,1,0:T(8,128)(2,1)}), bf16[16,32,128]{2,1,0:T(8,128)(2,1)S(1)}, u32[]{:S(2)}, u32[]{:S(2)}) %all-to-all-start) | async-done | bytes 131104 | tf_op jit(solution)/shard_map/all_to_all | solution.py:30
  34.4 3.9 %all-to-all-start.1 = ((bf16[16,5,48,256]{3,2,1,0:T(8,128)(2,1)}), bf16[16,5,48,256]{3,2,1,0:T(8,128)(2,1)S(1)}, u32[]{:S(2)}, u32[]{:S(2)}) async-start(bf16[16,5,48,256]{3,2,1,0:T(8,128)(2,1)} %copy.30), calls=%async_computation.1 | async-start | bytes 3932160 | tf_op jit(solution)/shard_map/all_to_all | solution.py:321
  40.1 4.0 %collective-permute-start = (bf16[82,320]{1,0:T(8,128)(2,1)S(1)}, bf16[82,320]{1,0:T(8,128)(2,1)S(1)}, u32[]{:S(2)}, u32[]{:S(2)}) collective-permute-start(bf16[82,320]{1,0:T(8,128)(2,1)S(1)} %get-tuple-element.30), channel_id=1, source_target_pairs={{0,1},{1,2},{2,3},{3,4},{4,5},{5,6},{6,7},{8,9},{9,10},{10,11},{11... | collective-permute-start | bytes 157448 | tf_op jit(solution)/shard_map/ppermute | solution.py:42
  46.4 4.0 %block_sums.1 = (f32[2,128]{1,0:T(2,128)}, s32[48,128]{1,0:T(8,128)}, f32[48,128]{1,0:T(8,128)}) custom-call(s32[1]{0:T(128)} %bitcast.first_ref, s32[768]{0:T(1024)} %tiers_ref.1, bf16[12,88,128]{2,1,0:T(8,128)(2,1)} %bitcast_bitcast_fusion.window_ref, s32[768,128]{1,0:T(8,128)} %lists_ref.1), custom_call_target="tpu_custom_call" | custom-call | flops 10000000 | bytes 1000000 | tf_op jit(solution)/shard_map/block_sums/pallas_call | solution.py:108
  50.4 2.1 %collective-permute-start.2 = (f32[2,128]{1,0:T(2,128)}, f32[2,128]{1,0:T(2,128)S(1)}, u32[]{:S(2)}, u32[]{:S(2)}) collective-permute-start(f32[2,128]{1,0:T(2,128)} %get-tuple-element.8), channel_id=1, source_target_pairs={{0,1},{1,2},{2,3},{3,4},{4,5},{5,6},{6,7},{7,0},{8,9},{9,10},{10,1... | collective-permute-start | bytes 3080 | tf_op jit(solution)/shard_map/ppermute | solution.py:35
  52.6 3.5 %grams.5.refs_2_ = f32[16,80,88]{2,1,0:T(8,128)} custom-call(s32[1]{0:T(128)} %bitcast.first_ref, bf16[12,88,128]{2,1,0:T(8,128)(2,1)} %bitcast_bitcast_fusion.window_ref, s32[48,128]{1,0:T(8,128)} %get-tuple-element.9.local_ref, f32[48,128]{1,0:T(8,128)} %get-tuple-element.10.decay_ref), custom_call_target="tpu_custom_call" | custom-call | flops 960000000 | bytes 640000 | tf_op jit(solution)/shard_map/grams/pallas_call | solution.py:160
  56.2 3.5 %grams.4.refs_1_ = f32[16,80,88]{2,1,0:T(8,128)} custom-call(s32[1]{0:T(128)} %bitcast.first_ref, bf16[12,88,128]{2,1,0:T(8,128)(2,1)} %bitcast_bitcast_fusion.window_ref, s32[48,128]{1,0:T(8,128)} %get-tuple-element.9.local_ref, f32[48,128]{1,0:T(8,128)} %get-tuple-element.10.decay_ref), custom_call_target="tpu_custom_call" | custom-call | flops 960000000 | bytes 640000 | tf_op jit(solution)/shard_map/grams/pallas_call | solution.py:160
  61.0 3.5 %grams.3.refs_0_ = f32[16,80,88]{2,1,0:T(8,128)} custom-call(s32[1]{0:T(128)} %bitcast.first_ref, bf16[12,88,128]{2,1,0:T(8,128)(2,1)} %bitcast_bitcast_fusion.window_ref, s32[48,128]{1,0:T(8,128)} %get-tuple-element.9.local_ref, f32[48,128]{1,0:T(8,128)} %get-tuple-element.10.decay_ref), custom_call_target="tpu_custom_call" | custom-call | flops 960000000 | bytes 640000 | tf_op jit(solution)/shard_map/grams/pallas_call | solution.py:160
  64.5 2.8 %collective-permute-done.4.other_ref = f32[2,128]{1,0:T(2,128)S(1)} collective-permute-done((f32[2,128]{1,0:T(2,128)S(1)}, f32[2,128]{1,0:T(2,128)S(1)}, u32[]{:S(2)}, u32[]{:S(2)}) %collective-permute-start.4) | collective-permute-done | bytes 1056 | tf_op jit(solution)/shard_map/ppermute | solution.py:35
  67.9 9.9 %roots.1 = bf16[48,80,80]{2,1,0:T(8,128)(2,1)} custom-call(f32[2,128]{1,0:T(2,128)} %copy-done.17, f32[2,128]{1,0:T(2,128)} %copy-done.22, bf16[80,80]{1,0:T(8,128)(2,1)} %fusion.3.order_ref, f32[16,80,88]{2,1,0:T(8,128)} %grams.3.refs_0_, f32[16,80,88]{2,1,0:T(8,128)} %grams.4.refs_1_, f32[16,80,88]{2,1,0:T(8,128)} %grams.5.refs_2_), custom_call_target="tpu_custom_call" | custom-call | flops 2880000000 | bytes 2400000 | tf_op jit(solution)/shard_map/roots/pallas_call | solution.py:242
  77.9 6.0 %all-to-all-done.1 = bf16[16,5,48,256]{3,2,1,0:T(8,128)(2,1)S(1)} async-done(((bf16[16,5,48,256]{3,2,1,0:T(8,128)(2,1)}), bf16[16,5,48,256]{3,2,1,0:T(8,128)(2,1)S(1)}, u32[]{:S(2)}, u32[]{:S(2)}) %all-to-all-start.1) | async-done | bytes 1966112 | tf_op jit(solution)/shard_map/all_to_all | solution.py:321
  88.1 3.2 %collective-permute-start.18 = (bf16[5,48,256]{2,1,0:T(8,128)(2,1)S(1)}, bf16[5,48,256]{2,1,0:T(8,128)(2,1)S(1)}, u32[]{:S(2)}, u32[]{:S(2)}) collective-permute-start(bf16[5,48,256]{2,1,0:T(8,128)(2,1)S(1)} %get-tuple-element.14), channel_id=1, source_target_pairs={{0,96},{8,104},{16,112},{24,120},{32,0},{40,8},{48,16},{56,24},{64... | collective-permute-start | bytes 368648 | tf_op jit(solution)/shard_map/ppermute | solution.py:296
  91.3 2.8 %collective-permute-start.16 = (bf16[5,48,256]{2,1,0:T(8,128)(2,1)S(1)}, bf16[5,48,256]{2,1,0:T(8,128)(2,1)S(1)}, u32[]{:S(2)}, u32[]{:S(2)}) collective-permute-start(bf16[5,48,256]{2,1,0:T(8,128)(2,1)S(1)} %get-tuple-element.16), channel_id=1, source_target_pairs={{0,88},{8,80},{16,104},{24,96},{32,120},{40,112},{48,8},{56,0},{64... | collective-permute-start | bytes 368648 | tf_op jit(solution)/shard_map/ppermute | solution.py:296
  95.7 5.7 %collective-permute-start.14 = (bf16[5,48,256]{2,1,0:T(8,128)(2,1)S(1)}, bf16[5,48,256]{2,1,0:T(8,128)(2,1)S(1)}, u32[]{:S(2)}, u32[]{:S(2)}) collective-permute-start(bf16[5,48,256]{2,1,0:T(8,128)(2,1)S(1)} %get-tuple-element.18), channel_id=1, source_target_pairs={{0,80},{8,88},{16,96},{24,104},{32,112},{40,120},{48,0},{56,8},{64... | collective-permute-start | bytes 368648 | tf_op jit(solution)/shard_map/ppermute | solution.py:296
  101.4 7.2 %collective-permute-start.13 = (bf16[5,48,256]{2,1,0:T(8,128)(2,1)S(1)}, bf16[5,48,256]{2,1,0:T(8,128)(2,1)S(1)}, u32[]{:S(2)}, u32[]{:S(2)}) collective-permute-start(bf16[5,48,256]{2,1,0:T(8,128)(2,1)S(1)} %get-tuple-element.19), channel_id=1, source_target_pairs={{0,48},{8,56},{16,64},{24,72},{32,80},{40,88},{48,96},{56,104},{64... | collective-permute-start | bytes 368648 | tf_op jit(solution)/shard_map/ppermute | solution.py:296
  108.7 6.4 %collective-permute-start.11 = (bf16[5,48,256]{2,1,0:T(8,128)(2,1)S(1)}, bf16[5,48,256]{2,1,0:T(8,128)(2,1)S(1)}, u32[]{:S(2)}, u32[]{:S(2)}) collective-permute-start(bf16[5,48,256]{2,1,0:T(8,128)(2,1)S(1)} %get-tuple-element.21), channel_id=1, source_target_pairs={{0,64},{8,72},{16,80},{24,88},{32,96},{40,104},{48,112},{56,120},{... | collective-permute-start | bytes 368648 | tf_op jit(solution)/shard_map/ppermute | solution.py:296
  115.6 5.4 %collective-permute-start.8 = (bf16[5,48,256]{2,1,0:T(8,128)(2,1)S(1)}, bf16[5,48,256]{2,1,0:T(8,128)(2,1)S(1)}, u32[]{:S(2)}, u32[]{:S(2)}) collective-permute-start(bf16[5,48,256]{2,1,0:T(8,128)(2,1)S(1)} %get-tuple-element.25), channel_id=1, source_target_pairs={{0,24},{8,16},{16,40},{24,32},{32,56},{40,48},{48,72},{56,64},{64,... | collective-permute-start | bytes 368648 | tf_op jit(solution)/shard_map/ppermute | solution.py:296
  121.7 3.6 %collective-permute-start.7 = (bf16[5,48,256]{2,1,0:T(8,128)(2,1)S(1)}, bf16[5,48,256]{2,1,0:T(8,128)(2,1)S(1)}, u32[]{:S(2)}, u32[]{:S(2)}) collective-permute-start(bf16[5,48,256]{2,1,0:T(8,128)(2,1)S(1)} %get-tuple-element.26), channel_id=1, source_target_pairs={{0,112},{8,120},{16,0},{24,8},{32,16},{40,24},{48,32},{56,40},{64,... | collective-permute-start | bytes 368648 | tf_op jit(solution)/shard_map/ppermute | solution.py:296
  127.0 7.0 %collective-permute-start.5 = (bf16[5,48,256]{2,1,0:T(8,128)(2,1)S(1)}, bf16[5,48,256]{2,1,0:T(8,128)(2,1)S(1)}, u32[]{:S(2)}, u32[]{:S(2)}) collective-permute-start(bf16[5,48,256]{2,1,0:T(8,128)(2,1)S(1)} %get-tuple-element.28), channel_id=1, source_target_pairs={{0,104},{8,96},{16,120},{24,112},{32,8},{40,0},{48,24},{56,16},{64... | collective-permute-start | bytes 368648 | tf_op jit(solution)/shard_map/ppermute | solution.py:296
  134.6 2.5 %place.2.refs_6_ = bf16[5,768,256]{2,1,0:T(8,128)(2,1)} custom-call(s32[16]{0:T(128)} %fusion.11.starts_ref, bf16[5,48,256]{2,1,0:T(8,128)(2,1)} %get-tuple-element.22.refs_0_, bf16[5,48,256]{2,1,0:T(8,128)(2,1)} %copy-done.14, bf16[5,48,256]{2,1,0:T(8,128)(2,1)} %copy-done.13, bf16[5,48,256]{2,1,0:T(8,128)(2,1)} %copy-done.12, ...), custom_call_target="tpu_custom_call" | custom-call | flops 1000000 | bytes 3000000 | tf_op jit(solution)/shard_map/place/pallas_call | solution.py:271
  137.2 2.4 %collective-permute-done.5.refs_0_ = bf16[5,48,256]{2,1,0:T(8,128)(2,1)S(1)} collective-permute-done((bf16[5,48,256]{2,1,0:T(8,128)(2,1)S(1)}, bf16[5,48,256]{2,1,0:T(8,128)(2,1)S(1)}, u32[]{:S(2)}, u32[]{:S(2)}) %collective-permute-start.5) | collective-permute-done | bytes 122912 | tf_op jit(solution)/shard_map/ppermute | solution.py:296
  140.3 2.1 %place.3 = bf16[5,768,256]{2,1,0:T(8,128)(2,1)} custom-call(s32[16]{0:T(128)} %fusion.11.starts_ref, bf16[5,48,256]{2,1,0:T(8,128)(2,1)} %copy-done.5, bf16[5,48,256]{2,1,0:T(8,128)(2,1)} %copy-done.4, bf16[5,48,256]{2,1,0:T(8,128)(2,1)} %copy-done.3, bf16[5,48,256]{2,1,0:T(8,128)(2,1)} %copy-done.2, ...), custom_call_target="tpu_custom_call", output_to_operand_aliasing={{}: (7, {})} | custom-call | flops 1000000 | bytes 1800000 | tf_op jit(solution)/shard_map/place/pallas_call | solution.py:271
  (96 shorter events, 17.4 us)
Async XLA Ops:
  1.4 33.0 %all-to-all-start = ((bf16[16,32,128]{2,1,0:T(8,128)(2,1)}), bf16[16,32,128]{2,1,0:T(8,128)(2,1)S(1)}, u32[]{:S(2)}, u32[]{:S(2)}) async-start(bf16[16,32,128]{2,1,0:T(8,128)(2,1)} %broadcast_in_dim.2), calls=%async_computation | async-start | bytes 262144 | tf_op jit(solution)/shard_map/all_to_all | solution.py:30
  34.4 49.4 %all-to-all-start.1 = ((bf16[16,5,48,256]{3,2,1,0:T(8,128)(2,1)}), bf16[16,5,48,256]{3,2,1,0:T(8,128)(2,1)S(1)}, u32[]{:S(2)}, u32[]{:S(2)}) async-start(bf16[16,5,48,256]{3,2,1,0:T(8,128)(2,1)} %copy.30), calls=%async_computation.1 | async-start | bytes 3932160 | tf_op jit(solution)/shard_map/all_to_all | solution.py:321
  38.8 6.0 %collective-permute-start.1 = (bf16[82,320]{1,0:T(8,128)(2,1)S(1)}, bf16[82,320]{1,0:T(8,128)(2,1)S(1)}, u32[]{:S(2)}, u32[]{:S(2)}) collective-permute-start(bf16[82,320]{1,0:T(8,128)(2,1)S(1)} %get-tuple-element.29), channel_id=1, source_target_pairs={{1,0},{2,1},{3,2},{4,3},{5,4},{6,5},{7,6},{9,8},{10,9},{11,10},{12... | collective-permute-start | bytes 157448 | tf_op jit(solution)/shard_map/ppermute | solution.py:43
  40.1 5.4 %collective-permute-start = (bf16[82,320]{1,0:T(8,128)(2,1)S(1)}, bf16[82,320]{1,0:T(8,128)(2,1)S(1)}, u32[]{:S(2)}, u32[]{:S(2)}) collective-permute-start(bf16[82,320]{1,0:T(8,128)(2,1)S(1)} %get-tuple-element.30), channel_id=1, source_target_pairs={{0,1},{1,2},{2,3},{3,4},{4,5},{5,6},{6,7},{8,9},{9,10},{10,11},{11... | collective-permute-start | bytes 157448 | tf_op jit(solution)/shard_map/ppermute | solution.py:42
  50.4 5.6 %collective-permute-start.2 = (f32[2,128]{1,0:T(2,128)}, f32[2,128]{1,0:T(2,128)S(1)}, u32[]{:S(2)}, u32[]{:S(2)}) collective-permute-start(f32[2,128]{1,0:T(2,128)} %get-tuple-element.8), channel_id=1, source_target_pairs={{0,1},{1,2},{2,3},{3,4},{4,5},{5,6},{6,7},{7,0},{8,9},{9,10},{10,1... | collective-permute-start | bytes 3080 | tf_op jit(solution)/shard_map/ppermute | solution.py:35
  56.1 4.9 %collective-permute-start.3 = (f32[2,128]{1,0:T(2,128)S(1)}, f32[2,128]{1,0:T(2,128)S(1)}, u32[]{:S(2)}, u32[]{:S(2)}) collective-permute-start(f32[2,128]{1,0:T(2,128)S(1)} %add.62), channel_id=1, source_target_pairs={{0,2},{1,3},{2,4},{3,5},{4,6},{5,7},{6,0},{7,1},{8,10},{9,11},{10,... | collective-permute-start | bytes 3080 | tf_op jit(solution)/shard_map/ppermute | solution.py:35
  61.0 6.3 %collective-permute-start.4 = (f32[2,128]{1,0:T(2,128)S(1)}, f32[2,128]{1,0:T(2,128)S(1)}, u32[]{:S(2)}, u32[]{:S(2)}) collective-permute-start(f32[2,128]{1,0:T(2,128)S(1)} %add.63.sums_ref), channel_id=1, source_target_pairs={{0,4},{1,5},{2,6},{3,7},{4,0},{5,1},{6,2},{7,3},{8,12},{9,13},{10,... | collective-permute-start | bytes 3080 | tf_op jit(solution)/shard_map/ppermute | solution.py:35
  86.5 47.4 %copy-start.19 = (s32[16]{0:T(128)S(1)}, s32[16]{0:T(128)}, u32[]{:S(2)}) copy-start(s32[16]{0:T(128)} %constant.45) | copy-start | bytes 196
  87.3 8.4 %collective-permute-start.19 = (bf16[5,48,256]{2,1,0:T(8,128)(2,1)S(1)}, bf16[5,48,256]{2,1,0:T(8,128)(2,1)S(1)}, u32[]{:S(2)}, u32[]{:S(2)}) collective-permute-start(bf16[5,48,256]{2,1,0:T(8,128)(2,1)S(1)} %get-tuple-element.13), channel_id=1, source_target_pairs={{0,40},{8,32},{16,56},{24,48},{32,72},{40,64},{48,88},{56,80},{64,... | collective-permute-start | bytes 368648 | tf_op jit(solution)/shard_map/ppermute | solution.py:296
  88.1 13.3 %collective-permute-start.18 = (bf16[5,48,256]{2,1,0:T(8,128)(2,1)S(1)}, bf16[5,48,256]{2,1,0:T(8,128)(2,1)S(1)}, u32[]{:S(2)}, u32[]{:S(2)}) collective-permute-start(bf16[5,48,256]{2,1,0:T(8,128)(2,1)S(1)} %get-tuple-element.14), channel_id=1, source_target_pairs={{0,96},{8,104},{16,112},{24,120},{32,0},{40,8},{48,16},{56,24},{64... | collective-permute-start | bytes 368648 | tf_op jit(solution)/shard_map/ppermute | solution.py:296
  91.3 17.3 %collective-permute-start.17 = (bf16[5,48,256]{2,1,0:T(8,128)(2,1)S(1)}, bf16[5,48,256]{2,1,0:T(8,128)(2,1)S(1)}, u32[]{:S(2)}, u32[]{:S(2)}) collective-permute-start(bf16[5,48,256]{2,1,0:T(8,128)(2,1)S(1)} %get-tuple-element.15), channel_id=1, source_target_pairs={{0,32},{8,40},{16,48},{24,56},{32,64},{40,72},{48,80},{56,88},{64,... | collective-permute-start | bytes 368648 | tf_op jit(solution)/shard_map/ppermute | solution.py:296
  91.3 17.3 %collective-permute-start.16 = (bf16[5,48,256]{2,1,0:T(8,128)(2,1)S(1)}, bf16[5,48,256]{2,1,0:T(8,128)(2,1)S(1)}, u32[]{:S(2)}, u32[]{:S(2)}) collective-permute-start(bf16[5,48,256]{2,1,0:T(8,128)(2,1)S(1)} %get-tuple-element.16), channel_id=1, source_target_pairs={{0,88},{8,80},{16,104},{24,96},{32,120},{40,112},{48,8},{56,0},{64... | collective-permute-start | bytes 368648 | tf_op jit(solution)/shard_map/ppermute | solution.py:296
  94.1 21.0 %collective-permute-start.15 = (bf16[5,48,256]{2,1,0:T(8,128)(2,1)S(1)}, bf16[5,48,256]{2,1,0:T(8,128)(2,1)S(1)}, u32[]{:S(2)}, u32[]{:S(2)}) collective-permute-start(bf16[5,48,256]{2,1,0:T(8,128)(2,1)S(1)} %get-tuple-element.17), channel_id=1, source_target_pairs={{0,56},{8,48},{16,72},{24,64},{32,88},{40,80},{48,104},{56,96},{64... | collective-permute-start | bytes 368648 | tf_op jit(solution)/shard_map/ppermute | solution.py:296
  95.7 38.9 %copy-start.6 = (bf16[5,48,256]{2,1,0:T(8,128)(2,1)}, bf16[5,48,256]{2,1,0:T(8,128)(2,1)S(1)}, u32[]{:S(2)}) copy-start(bf16[5,48,256]{2,1,0:T(8,128)(2,1)S(1)} %collective-permute-done.19.refs_9_) | copy-start | bytes 368644
  95.7 19.4 %collective-permute-start.14 = (bf16[5,48,256]{2,1,0:T(8,128)(2,1)S(1)}, bf16[5,48,256]{2,1,0:T(8,128)(2,1)S(1)}, u32[]{:S(2)}, u32[]{:S(2)}) collective-permute-start(bf16[5,48,256]{2,1,0:T(8,128)(2,1)S(1)} %get-tuple-element.18), channel_id=1, source_target_pairs={{0,80},{8,88},{16,96},{24,104},{32,112},{40,120},{48,0},{56,8},{64... | collective-permute-start | bytes 368648 | tf_op jit(solution)/shard_map/ppermute | solution.py:296
  101.4 14.2 %collective-permute-start.13 = (bf16[5,48,256]{2,1,0:T(8,128)(2,1)S(1)}, bf16[5,48,256]{2,1,0:T(8,128)(2,1)S(1)}, u32[]{:S(2)}, u32[]{:S(2)}) collective-permute-start(bf16[5,48,256]{2,1,0:T(8,128)(2,1)S(1)} %get-tuple-element.19), channel_id=1, source_target_pairs={{0,48},{8,56},{16,64},{24,72},{32,80},{40,88},{48,96},{56,104},{64... | collective-permute-start | bytes 368648 | tf_op jit(solution)/shard_map/ppermute | solution.py:296
  108.6 13.0 %collective-permute-start.12 = (bf16[5,48,256]{2,1,0:T(8,128)(2,1)S(1)}, bf16[5,48,256]{2,1,0:T(8,128)(2,1)S(1)}, u32[]{:S(2)}, u32[]{:S(2)}) collective-permute-start(bf16[5,48,256]{2,1,0:T(8,128)(2,1)S(1)} %get-tuple-element.20), channel_id=1, source_target_pairs={{0,72},{8,64},{16,88},{24,80},{32,104},{40,96},{48,120},{56,112},{... | collective-permute-start | bytes 368648 | tf_op jit(solution)/shard_map/ppermute | solution.py:296
  108.7 18.3 %collective-permute-start.11 = (bf16[5,48,256]{2,1,0:T(8,128)(2,1)S(1)}, bf16[5,48,256]{2,1,0:T(8,128)(2,1)S(1)}, u32[]{:S(2)}, u32[]{:S(2)}) collective-permute-start(bf16[5,48,256]{2,1,0:T(8,128)(2,1)S(1)} %get-tuple-element.21), channel_id=1, source_target_pairs={{0,64},{8,72},{16,80},{24,88},{32,96},{40,104},{48,112},{56,120},{... | collective-permute-start | bytes 368648 | tf_op jit(solution)/shard_map/ppermute | solution.py:296
  115.1 11.9 %collective-permute-start.10 = (bf16[5,48,256]{2,1,0:T(8,128)(2,1)S(1)}, bf16[5,48,256]{2,1,0:T(8,128)(2,1)S(1)}, u32[]{:S(2)}, u32[]{:S(2)}) collective-permute-start(bf16[5,48,256]{2,1,0:T(8,128)(2,1)S(1)} %get-tuple-element.23), channel_id=1, source_target_pairs={{0,8},{8,0},{16,24},{24,16},{32,40},{40,32},{48,56},{56,48},{64,72... | collective-permute-start | bytes 368648 | tf_op jit(solution)/shard_map/ppermute | solution.py:296
  115.1 22.0 %collective-permute-start.9 = (bf16[5,48,256]{2,1,0:T(8,128)(2,1)S(1)}, bf16[5,48,256]{2,1,0:T(8,128)(2,1)S(1)}, u32[]{:S(2)}, u32[]{:S(2)}) collective-permute-start(bf16[5,48,256]{2,1,0:T(8,128)(2,1)S(1)} %get-tuple-element.24), channel_id=1, source_target_pairs={{0,120},{8,112},{16,8},{24,0},{32,24},{40,16},{48,40},{56,32},{64,... | collective-permute-start | bytes 368648 | tf_op jit(solution)/shard_map/ppermute | solution.py:296
  115.6 21.5 %collective-permute-start.8 = (bf16[5,48,256]{2,1,0:T(8,128)(2,1)S(1)}, bf16[5,48,256]{2,1,0:T(8,128)(2,1)S(1)}, u32[]{:S(2)}, u32[]{:S(2)}) collective-permute-start(bf16[5,48,256]{2,1,0:T(8,128)(2,1)S(1)} %get-tuple-element.25), channel_id=1, source_target_pairs={{0,24},{8,16},{16,40},{24,32},{32,56},{40,48},{48,72},{56,64},{64,... | collective-permute-start | bytes 368648 | tf_op jit(solution)/shard_map/ppermute | solution.py:296
  121.7 15.5 %collective-permute-start.7 = (bf16[5,48,256]{2,1,0:T(8,128)(2,1)S(1)}, bf16[5,48,256]{2,1,0:T(8,128)(2,1)S(1)}, u32[]{:S(2)}, u32[]{:S(2)}) collective-permute-start(bf16[5,48,256]{2,1,0:T(8,128)(2,1)S(1)} %get-tuple-element.26), channel_id=1, source_target_pairs={{0,112},{8,120},{16,0},{24,8},{32,16},{40,24},{48,32},{56,40},{64,... | collective-permute-start | bytes 368648 | tf_op jit(solution)/shard_map/ppermute | solution.py:296
  127.0 10.2 %collective-permute-start.6 = (bf16[5,48,256]{2,1,0:T(8,128)(2,1)S(1)}, bf16[5,48,256]{2,1,0:T(8,128)(2,1)S(1)}, u32[]{:S(2)}, u32[]{:S(2)}) collective-permute-start(bf16[5,48,256]{2,1,0:T(8,128)(2,1)S(1)} %get-tuple-element.27), channel_id=1, source_target_pairs={{0,16},{8,24},{16,32},{24,40},{32,48},{40,56},{48,64},{56,72},{64,... | collective-permute-start | bytes 368648 | tf_op jit(solution)/shard_map/ppermute | solution.py:296
  127.0 12.6 %collective-permute-start.5 = (bf16[5,48,256]{2,1,0:T(8,128)(2,1)S(1)}, bf16[5,48,256]{2,1,0:T(8,128)(2,1)S(1)}, u32[]{:S(2)}, u32[]{:S(2)}) collective-permute-start(bf16[5,48,256]{2,1,0:T(8,128)(2,1)S(1)} %get-tuple-element.28), channel_id=1, source_target_pairs={{0,104},{8,96},{16,120},{24,112},{32,8},{40,0},{48,24},{56,16},{64... | collective-permute-start | bytes 368648 | tf_op jit(solution)/shard_map/ppermute | solution.py:296
  (21 other events, 240.2 us)
